TPU v7x, 256 devices: a whole 4x4x8 slice. The times are simulated.
256 devices in a mesh: dp: 64 (over x, z, core), mp: 4 (over y).
Axes of the slice: x: 4, y: 4, z: 8, core: 2. Of those that a mesh axis runs over, the one named last changes fastest.
Arguments:
- hidden_activation: bfloat16 [2, 64, 2, 256, 14336], P(None, 'dp', None, None, 'mp'), may hold values from -6 to 6
- target_head_rows: bfloat16 [2, 64, 2, 256, 4096], P(None, 'dp', None, None, 'mp'), may hold values from -6 to 6
- reference_log_probability: float32 [2, 64, 2, 256], P(None, 'dp'), may hold values from -8 to -0.05
- response_token_mask: int32 [2, 64, 2, 256], P(None, 'dp'), may hold values 0 or 1
- sequence_tile_lengths: int32 [2, 64, 2], P(None, 'dp'), may hold values from 1 to 2
- pair_destination: int32 [2, 64], replicated, may hold values from 0 to 63, each once within a row
- adapter_down_first: bfloat16 [14336, 256], P('mp'), may hold values from -0.046875 to 0.046875
- adapter_down_second: bfloat16 [4096, 256], P('mp'), may hold values from -0.09375 to 0.09375
Outputs:
- pair_margin: float32 [2, 64], P(None, 'dp')
- mean_loss: float32 [], replicated
- grad_a: float32 [14336, 256], P(('mp', 'dp'))
- grad_b: float32 [4096, 256], P(('mp', 'dp'))
Inputs may be any that keep to these rules, and one draw needn't show every extreme that they name: Each row of pair_destination is a permutation of 0 to 63.
All inputs are finite; a program needn't handle non-finite values. No bound on the sum of `response_token_mask` on one device may be relied on, other than what follows from the above.
Results may differ from a plain program's by a relative error of at most 0.0029.
Values sent between devices are 32-bit elements; how exact they have to be, the bound alone decides.
No kernel may reach another device: no remote copies, remote signals or barrier semaphores. Data moves between devices by JAX's collectives and lax.ppermute only.
A program may use at most 128 MiB of HBM per device.

v0:
```python
import functools
import math

import jax
import jax.numpy as jnp
import numpy as np
from jax import lax
from jax.experimental import pallas as pl
from jax.experimental.pallas import tpu as pltpu
from jax.sharding import Mesh
from jax.sharding import PartitionSpec as P

TILE = 128
X, Z, C, Y = "dp_0", "dp_1", "dp_2", "mp"
DP = (X, Z, C)
MP_DP = (Y, X, Z, C)
BETA = 0.1


def first(i, c, n):
    return (i + 1 - 2 * ((i + c) % 2)) % n


def second(i, c, n):
    return (i - 1 + 2 * ((i + c) % 2)) % n


def third(i, c, n):
    return (i + 3 - 6 * ((i + c) % 2)) % n


def swap(value, axis, partner):
    n = lax.axis_size(axis)
    axes, flat = ((C, Y), lambda i, c: c * n + i) if axis == Y else ((axis, C), lambda i, c: i * 2 + c)
    pairs = [(flat(i, c), flat(partner(i, c, n), c)) for i in range(n) for c in range(2)]
    return lax.ppermute(value, axes, pairs)


def order_of_four(i, c):
    n = 4
    return [first(i, c, n), (i + 2) % n, i, second(i, c, n)]


def order_of_eight(i, c):
    n = 8

    def group(j):
        k = second(j, c, n)
        return [j, third(j, c, n), k, third(k, c, n)]

    return group(first(i, c, n)) + group(i)


def places_of(order):
    return [order.index(i) for i in range(len(order))]


def table():
    rows = []
    for x in range(4):
        for z in range(8):
            for c in range(2):
                for y in range(4):
                    near, far, mine, late = order_of_four(y, c)
                    rows.append(
                        [mine, late, near, far, c, 0, 0, 0]
                        + order_of_eight(z, c)
                        + order_of_eight(z, 1 - c)
                        + places_of(order_of_four(x, c))
                        + places_of(order_of_four(x, 1 - c))
                    )
    return np.array(rows, np.int32)


ORDER_HERE, ORDER_THERE, PLACE_HERE, PLACE_THERE, LENGTHS = 8, 16, 24, 28, 32


def arrange(info, part, blocks, outs):
    tall = part.shape[0] // 16
    blocks[...] = part.reshape(16, tall, part.shape[1])
    core = info[4]
    for side, order in enumerate((ORDER_HERE, ORDER_THERE)):
        which = core if side == 0 else 1 - core
        for p in range(8):
            block = blocks[2 * info[order + p] + which]
            row = 0
            for out, z_dim in outs[side]:
                height = out.shape[-2]
                at = (0, p // 4, 0, p % 4) if z_dim == 1 else (p // 4, 0, 0, p % 4)
                out[at] = block[row : row + height]
                row += height


CONTRACT = (((0,), (0,)), ((), ()))


def first_kernel(
    info, r0, r1, r2, r3, s0, s1, s2, s3, reference, mask, hidden,
    keep_p, keep_q, send_p, send_q, margins, columns,
    r_all, s_all, d_latent, blocks, tiles, arrived,
):
    seq = reference.shape[1]
    root = math.sqrt(r_all.shape[2])
    step = pl.program_id(0)
    wide = tiles.shape[2]

    def fetch(i):
        slot = i % 2
        at = pl.multiple_of(i * wide, wide)
        return pltpu.make_async_copy(
            hidden.at[:, pl.ds(at, wide)], tiles.at[slot], arrived.at[slot]
        )

    @pl.when(step == 0)
    def _():
        fetch(0).start()
        fetch(1).start()
        for k, (r, s) in enumerate(((r0, s0), (r1, s1), (r2, s2), (r3, s3))):
            r_all[info[k]] = r[...]
            s_all[info[k]] = s[...]
        tile = lax.broadcasted_iota(jnp.int32, (1, seq), 1) // TILE
        live, share, sums = [], [], []
        for q in range(4):
            shift = s_all[q]
            chance = jnp.exp(reference[q : q + 1])
            denom = 1.0 - chance + chance * jnp.exp(shift)
            gain = shift - jnp.log(denom)
            on = (mask[q : q + 1] == 1) & (tile < info[LENGTHS + q])
            live.append(on.astype(jnp.float32))
            share.append((chance, denom))
            sums.append(jnp.sum(live[q] * gain, axis=1, keepdims=True))
        factors = []
        for m in range(2):
            margin = BETA * (sums[2 * m] - sums[2 * m + 1])
            margins[m : m + 1] = jnp.broadcast_to(margin, (1, 128))
            slope = -jax.nn.sigmoid(-margin)
            for side, sign in enumerate((1.0, -1.0)):
                chance, denom = share[2 * m + side]
                factors.append(
                    live[2 * m + side] * (slope * BETA) * sign * (1.0 - chance) / denom / root
                )
        columns[...] = jnp.concatenate(factors + [jnp.zeros((4, seq), jnp.float32)], axis=0).T
        for q in range(4):
            scaled = columns[:, q : q + 1] * r_all[q]
            d_latent[pl.ds(q * seq, seq)] = scaled.astype(jnp.bfloat16)

    fetch(step).wait()
    part = lax.dot_general(
        tiles[step % 2], d_latent[...], CONTRACT, preferred_element_type=jnp.float32
    )
    arrange(
        info, part, blocks, (((keep_p, 1), (keep_q, 0)), ((send_p, 1), (send_q, 0)))
    )

    @pl.when(step < 2)
    def _():
        fetch(step + 2).start()


def second_kernel(
    info, l0, l1, l2, l3, columns, rows, keep, send, l_all, d_readout, blocks
):
    seq = columns.shape[0]

    @pl.when(pl.program_id(0) == 0)
    def _():
        for k, l in enumerate((l0, l1, l2, l3)):
            l_all[info[k]] = l[...]
        for q in range(4):
            scaled = columns[:, q : q + 1] * l_all[q]
            d_readout[pl.ds(q * seq, seq)] = scaled.astype(jnp.bfloat16)

    part = lax.dot_general(
        rows[...], d_readout[...], CONTRACT, preferred_element_type=jnp.float32
    )
    arrange(info, part, blocks, (((keep, 0),), ((send, 0),)))


def product_kernel(at, order, value, weights, out, buffer, arrived):
    seq = out.shape[1]
    copies = [
        pltpu.make_async_copy(
            value.at[pl.ds(pl.multiple_of(order[at + i] * seq, seq), seq)],
            buffer.at[i],
            arrived.at[i],
        )
        for i in range(2)
    ]
    for copy in copies:
        copy.start()
    for i, copy in enumerate(copies):
        copy.wait()
        out[i] = jnp.dot(buffer[i], weights[...], preferred_element_type=jnp.float32)


def product(order, at, value, weights, seq):
    wide, rank = weights.shape
    return pl.pallas_call(
        functools.partial(product_kernel, at),
        in_specs=[
            pl.BlockSpec(memory_space=pltpu.SMEM),
            pl.BlockSpec(memory_space=pltpu.HBM),
            pl.BlockSpec(memory_space=pltpu.VMEM),
        ],
        out_specs=pl.BlockSpec(memory_space=pltpu.VMEM),
        scratch_shapes=[
            pltpu.VMEM((2, seq, wide), value.dtype),
            pltpu.SemaphoreType.DMA((2,)),
        ],
        out_shape=jax.ShapeDtypeStruct((2, seq, rank), jnp.float32),
        compiler_params=pltpu.CompilerParams(vmem_limit_bytes=53 * 2**20),
        cost_estimate=pl.CostEstimate(
            flops=4 * seq * wide * rank,
            bytes_accessed=4 * seq * wide + 2 * wide * rank + 8 * seq * rank,
            transcendentals=0,
        ),
    )(order, value, weights)


def pack_kernel(kept, came, base, shard, small):
    total = kept[...] + came[...]
    shard[...] = total
    column = lax.broadcasted_iota(jnp.int32, small.shape, 1)
    squares = jnp.sum(jnp.sum(total * total, axis=0, keepdims=True), axis=1, keepdims=True)
    small[...] = base[...] + jnp.where(column == 2, squares, 0.0)


def scale_kernel(count, small, shard, grad_a, grad_b, moved, loss):
    total = jnp.sum(small[...], axis=0, keepdims=True)
    scale = 1.0 / jnp.sqrt(total[:, 2:3] / count + 1e-06)
    tall = grad_a.shape[0]
    grad_a[...] = shard[:tall] * scale
    grad_b[...] = shard[tall:] * scale
    moved[0:1] = total[:, 0:1]
    moved[1:2] = total[:, 1:2]
    loss[...] = total[:, 3:4]


def whole(value):
    return pl.BlockSpec(value.shape, lambda i, info: (0,) * len(value.shape))


def x_major(rows, rank, places):
    return (
        jax.ShapeDtypeStruct((2, 2, 2, 4, rows, rank), jnp.float32),
        pl.BlockSpec(
            (1, 2, 1, 4, rows, rank),
            lambda i, info: (info[places + i] // 2, 0, info[places + i] % 2, 0, 0, 0),
        ),
    )


def z_major(rows, rank, places):
    return (
        jax.ShapeDtypeStruct((2, 2, 2, 4, rows, rank), jnp.float32),
        pl.BlockSpec(
            (2, 1, 1, 4, rows, rank),
            lambda i, info: (0, info[places + i] // 2, info[places + i] % 2, 0, 0, 0),
        ),
    )


def kernel_call(body, info, wholes, streamed, outs, scratch, rank, by_hand):
    tokens, wide = streamed.shape
    return pl.pallas_call(
        body,
        grid_spec=pltpu.PrefetchScalarGridSpec(
            num_scalar_prefetch=1,
            grid=(4,),
            in_specs=[whole(v) for v in wholes]
            + [
                pl.BlockSpec(memory_space=pltpu.HBM)
                if by_hand
                else pl.BlockSpec((tokens, wide // 4), lambda i, info: (0, i))
            ],
            out_specs=[spec for _, spec in outs],
            scratch_shapes=scratch,
        ),
        out_shape=[shape for shape, _ in outs],
        compiler_params=pltpu.CompilerParams(
            dimension_semantics=("arbitrary",),
            vmem_limit_bytes=(53 if by_hand else 24) * 2**20,
        ),
        cost_estimate=pl.CostEstimate(
            flops=2 * tokens * wide * rank,
            bytes_accessed=2 * tokens * wide + 4 * wide * rank,
            transcendentals=4096,
        ),
    )(info, *wholes, streamed)


def per_device(
    hidden_activation,
    target_head_rows,
    reference_log_probability,
    response_token_mask,
    sequence_tile_lengths,
    pair_destination,
    adapter_down_first,
    adapter_down_second,
):
    micro, _, sides, seq, ff = hidden_activation.shape
    width = target_head_rows.shape[-1]
    rank = adapter_down_first.shape[1]
    ways = lax.axis_size(Y)
    tokens = micro * sides * seq
    root = math.sqrt(rank)
    c, y = lax.axis_index(C), lax.axis_index(Y)
    place = lax.axis_index(DP)
    pairs = lax.axis_size(DP)
    tall_a, tall_b = ff // pairs, width // pairs
    late_a = (tall_a - tall_b) // 16 * 8 if tall_a > 2 * tall_b else tall_a // 2
    late_a = min(late_a, tall_b)

    hidden = hidden_activation.reshape(tokens, ff)
    rows = target_head_rows.reshape(tokens, width)
    near, far, mine, late = order_of_four(y, c)
    order = jnp.stack([mine, late, near, far]).astype(jnp.int32)

    readout_send = product(order, 2, rows, adapter_down_second, seq)
    readout_send, hidden_next = lax.optimization_barrier((readout_send, hidden))
    latent_send = product(order, 2, hidden_next, adapter_down_first, seq)
    latent_send, rows_next, hidden_next = lax.optimization_barrier((latent_send, rows, hidden))
    readout_keep = product(order, 0, rows_next, adapter_down_second, seq)
    latent_keep = product(order, 0, hidden_next, adapter_down_first, seq)

    def own_sum(send, keep):
        came = swap(send, Y, first)
        relayed = swap(keep[1] + came[1], Y, second)
        return lax.optimization_barrier(keep[0] + came[0] + relayed)

    def spread(own):
        other = swap(own, Y, second)
        beside = swap(own, Y, first)
        return own, other, beside, swap(other, Y, first)

    readout = own_sum(readout_send, readout_keep)
    latent = own_sum(latent_send, latent_keep)
    readouts = spread(readout)
    shift = (jnp.sum(latent * readout, axis=-1) / root)[None]
    opposite = [(i, (i + 2) % 4) for i in range(4)]
    shifts = (shift, swap(shift, Y, second), swap(shift, Y, first), lax.ppermute(shift, Y, opposite))
    latents = spread(latent)

    entry = jnp.asarray(table())[place * ways + y]
    lengths = sequence_tile_lengths.reshape(-1).astype(jnp.int32)
    info = jnp.concatenate([entry, lengths, jnp.zeros((4,), jnp.int32)])
    early = tall_a - late_a
    outs = [
        x_major(early, rank, PLACE_HERE),
        z_major(late_a, rank, PLACE_HERE),
        x_major(early, rank, PLACE_THERE),
        z_major(late_a, rank, PLACE_THERE),
    ]
    for shape in ((8, 128), (seq, 8)):
        block = jax.ShapeDtypeStruct(shape, jnp.float32)
        outs.append((block, whole(block)))
    keep_p, keep_q, send_p, send_q, margins, columns = kernel_call(
        first_kernel,
        info,
        (
            *readouts,
            *shifts,
            reference_log_probability.reshape(ways, seq),
            response_token_mask.reshape(ways, seq),
        ),
        hidden,
        outs,
        [
            pltpu.VMEM((4, seq, rank), jnp.float32),
            pltpu.VMEM((4, 1, seq), jnp.float32),
            pltpu.VMEM((tokens, rank), jnp.bfloat16),
            pltpu.VMEM((16, tall_a, rank), jnp.float32),
            pltpu.VMEM((2, tokens, ff // 4), hidden.dtype),
            pltpu.SemaphoreType.DMA((2,)),
        ],
        rank,
        True,
    )
    margin = margins[:micro, 0]
    core = lambda value: lax.ppermute(value, C, [(0, 1), (1, 0)])
    came_p = core(send_p)
    came_q = core(send_q)
    keep_b, send_b = kernel_call(
        second_kernel,
        info,
        (*latents, columns),
        rows,
        [z_major(tall_b, rank, PLACE_HERE), z_major(tall_b, rank, PLACE_THERE)],
        [
            pltpu.VMEM((4, seq, rank), jnp.float32),
            pltpu.VMEM((tokens, rank), jnp.bfloat16),
            pltpu.VMEM((16, tall_b, rank), jnp.float32),
        ],
        rank,
        False,
    )
    came_b = core(send_b)

    p_send, came_q = lax.optimization_barrier((keep_p[0] + came_p[0], came_q))
    p = swap(p_send, X, first)
    p = keep_p[1] + came_p[1] + p
    late_rows = lambda i: jnp.concatenate([keep_q[i] + came_q[i], keep_b[i] + came_b[i]], axis=-2)
    w = late_rows(1) + swap(late_rows(0), Z, first)
    p = p[1] + swap(p[0], Z, first)
    w = w[1] + swap(w[0], X, first)
    both = lambda i: jnp.concatenate([p[i], w[i]], axis=-2)
    shard = both(0) + swap(both(1), X, second)
    shard = shard[:2] + swap(shard[2:], Z, second)
    kept, came = shard[0], swap(shard[1], Z, third)

    target = lax.dynamic_index_in_dim(pair_destination, place, 1, keepdims=False)
    hits = jnp.arange(pairs)[:, None] == target[None, :]
    moved = jnp.where(hits, margin[None, :] / ways, 0.0)
    loss = jnp.sum(jax.nn.softplus(-margin)) / (micro * pairs * ways)
    plain = jnp.broadcast_to(jnp.stack([jnp.zeros_like(loss), loss])[None], (pairs, 2))
    base = jnp.concatenate([moved, plain], axis=1)
    base = jnp.broadcast_to(base[:, None], (pairs, ways, micro + 2))
    base = base.reshape(pairs * ways, micro + 2)
    little = pltpu.CompilerParams(vmem_limit_bytes=4 * 2**20)
    f32 = lambda *shape: jax.ShapeDtypeStruct(shape, jnp.float32)
    shard, small = pl.pallas_call(
        pack_kernel, out_shape=[f32(*kept.shape), f32(*base.shape)], compiler_params=little
    )(kept, came, base)
    small = lax.all_to_all(small, (X, Z, C, Y), 0, 0, tiled=True)
    grad_a, grad_b, pair_margin, mean_loss = pl.pallas_call(
        functools.partial(scale_kernel, (ff + width) * ways * rank),
        out_shape=[f32(tall_a, rank), f32(tall_b, rank), f32(micro, 1), f32(1, 1)],
        compiler_params=little,
    )(small, shard)
    return (pair_margin, mean_loss[0, 0], grad_a, grad_b)


def solution(mesh):
    split = Mesh(mesh.devices.reshape(4, 8, 2, mesh.shape["mp"]), (X, Z, C, Y))
    placed = (
        P(None, DP, None, None, Y),
        P(None, DP, None, None, Y),
        P(None, DP, None, None),
        P(None, DP, None, None),
        P(None, DP, None),
        P(),
        P(Y, None),
        P(Y, None),
    )

    return jax.shard_map(
        per_device,
        mesh=split,
        in_specs=placed,
        out_specs=(P(None, DP), P(), P(MP_DP, None), P(MP_DP, None)),
        check_vma=False,
    )
```

profile of v0, /device:TPU:1, one launch (start us, length us, event | category | flops | bytes accessed | tf_op | source)
XLA Modules:
  0.0 142.0 jit_solution(2605879542180734793)
XLA Ops:
  0.8 3.0 %shard_map.120 = f32[2,256,256]{2,1,0:T(8,128)S(1)} custom-call(s32[4]{0:T(128)S(1)} %pad_add_fusion.1.order, bf16[1024,1024]{1,0:T(8,128)(2,1)} %bitcast.66, bf16[1024,256]{1,0:T(8,128)(2,1)} %weights.6), custom_call_target="tpu_custom_call" | custom-call | flops 268435456 | bytes 2097152 | tf_op jit(solution)/shard_map/pallas_call | solution.py:198
  3.7 3.6 %collective-permute-start = (f32[2,256,256]{2,1,0:T(8,128)S(1)}, f32[2,256,256]{2,1,0:T(8,128)S(1)}, u32[]{:S(2)}, u32[]{:S(2)}) collective-permute-start(f32[2,256,256]{2,1,0:T(8,128)S(1)} %shard_map.120), channel_id=1, source_target_pairs={{0,1},{4,7},{1,0},{5,6},{2,3},{6,5},{3,2},{7,4},{8,9},{12,15},{9,8... | collective-permute-start | bytes 1572872 | tf_op jit(solution)/shard_map/ppermute | solution.py:36
  7.4 5.2 %shard_map.121 = f32[2,256,256]{2,1,0:T(8,128)S(1)} custom-call(s32[4]{0:T(128)S(1)} %pad_add_fusion.1.order, bf16[1024,3584]{1,0:T(8,128)(2,1)} %bitcast.76, bf16[3584,256]{1,0:T(8,128)(2,1)} %weights.7), custom_call_target="tpu_custom_call" | custom-call | flops 939524096 | bytes 6029312 | tf_op jit(solution)/shard_map/pallas_call | solution.py:198
  12.7 3.0 %shard_map.122 = f32[2,256,256]{2,1,0:T(8,128)S(1)} custom-call(s32[4]{0:T(128)S(1)} %pad_add_fusion.1.order, bf16[1024,1024]{1,0:T(8,128)(2,1)} %bitcast.67, bf16[1024,256]{1,0:T(8,128)(2,1)} %weights.6), custom_call_target="tpu_custom_call" | custom-call | flops 268435456 | bytes 2097152 | tf_op jit(solution)/shard_map/pallas_call | solution.py:198
  15.7 5.2 %shard_map.123 = f32[2,256,256]{2,1,0:T(8,128)S(1)} custom-call(s32[4]{0:T(128)S(1)} %pad_add_fusion.1.order, bf16[1024,3584]{1,0:T(8,128)(2,1)} %bitcast.77, bf16[3584,256]{1,0:T(8,128)(2,1)} %weights.7), custom_call_target="tpu_custom_call" | custom-call | flops 939524096 | bytes 6029312 | tf_op jit(solution)/shard_map/pallas_call | solution.py:198
  24.6 1.7 %collective-permute-done.1 = f32[256,256]{1,0:T(8,128)S(1)} collective-permute-done((f32[256,256]{1,0:T(8,128)S(1)}, f32[256,256]{1,0:T(8,128)S(1)}, u32[]{:S(2)}, u32[]{:S(2)}) %collective-permute-start.1) | collective-permute-done | bytes 262176 | tf_op jit(solution)/shard_map/ppermute | solution.py:36
  26.7 2.7 %collective-permute-start.3 = (f32[256,256]{1,0:T(8,128)S(1)}, f32[256,256]{1,0:T(8,128)S(1)}, u32[]{:S(2)}, u32[]{:S(2)}) collective-permute-start(f32[256,256]{1,0:T(8,128)S(1)} %fusion.12.r0), channel_id=1, source_target_pairs={{0,1},{4,7},{1,0},{5,6},{2,3},{6,5},{3,2},{7,4},{8,9},{12,15},{9,8... | collective-permute-start | bytes 786440 | tf_op jit(solution)/shard_map/ppermute | solution.py:36
  29.6 2.6 %collective-permute-done.2.r1 = f32[256,256]{1,0:T(8,128)S(1)} collective-permute-done((f32[256,256]{1,0:T(8,128)S(1)}, f32[256,256]{1,0:T(8,128)S(1)}, u32[]{:S(2)}, u32[]{:S(2)}) %collective-permute-start.2) | collective-permute-done | bytes 262176 | tf_op jit(solution)/shard_map/ppermute | solution.py:36
  32.2 2.4 %collective-permute-start.4 = (f32[256,256]{1,0:T(8,128)S(1)}, f32[256,256]{1,0:T(8,128)S(1)}, u32[]{:S(2)}, u32[]{:S(2)}) collective-permute-start(f32[256,256]{1,0:T(8,128)S(1)} %collective-permute-done.2.r1), channel_id=1, source_target_pairs={{0,1},{4,7},{1,0},{5,6},{2,3},{6,5},{3,2},{7,4},{8,9},{12,15},{9,8... | collective-permute-start | bytes 786440 | tf_op jit(solution)/shard_map/ppermute | solution.py:36
  34.9 2.9 %collective-permute-start.9 = (f32[1,256]{1,0:T(1,128)S(1)}, f32[1,256]{1,0:T(1,128)S(1)}, u32[]{:S(2)}, u32[]{:S(2)}) collective-permute-start(f32[1,256]{1,0:T(1,128)S(1)} %bitcast.74), channel_id=1, source_target_pairs={{0,2},{1,3},{2,0},{3,1},{4,6},{5,7},{6,4},{7,5},{8,10},{9,11},{10,... | collective-permute-start | bytes 3080 | tf_op jit(solution)/shard_map/ppermute | solution.py:342
  38.1 2.8 %collective-permute-done.8.s2 = f32[1,256]{1,0:T(1,128)S(1)} collective-permute-done((f32[1,256]{1,0:T(1,128)S(1)}, f32[1,256]{1,0:T(1,128)S(1)}, u32[]{:S(2)}, u32[]{:S(2)}) %collective-permute-start.8) | collective-permute-done | bytes 1056 | tf_op jit(solution)/shard_map/ppermute | solution.py:36
  41.6 8.6 %shard_map.124 = (f32[2,2,2,4,40,256]{5,4,3,2,1,0:T(8,128)}, f32[2,2,2,4,16,256]{5,4,3,2,1,0:T(8,128)}, f32[2,2,2,4,40,256]{5,4,3,2,1,0:T(8,128)}, f32[2,2,2,4,1...) custom-call(s32[40]{0:T(128)S(1)} %pad_add_fusion.info, f32[256,256]{1,0:T(8,128)S(1)} %fusion.12.r0, ...), custom_call_target="tpu_custom_call" | custom-call | flops 1879048192 | bytes 11010048 | tf_op jit(solution)/shard_map/pallas_call | solution.py:265
  50.2 7.1 %collective-permute-start.10 = (f32[2,2,2,4,40,256]{5,4,3,2,1,0:T(8,128)}, f32[2,2,2,4,40,256]{5,4,3,2,1,0:T(8,128)S(1)}, u32[]{:S(2)}, u32[]{:S(2)}) collective-permute-start(f32[2,2,2,4,40,256]{5,4,3,2,1,0:T(8,128)} %get-tuple-element.31), channel_id=1, source_target_pairs={{0,4},{4,0},{1,5},{5,1},{2,6},{6,2},{3,7},{7,3},{8,12},{12,8},{9,1... | collective-permute-start | bytes 3932168 | tf_op jit(solution)/shard_map/ppermute | solution.py:381
  57.3 2.3 %collective-permute-start.15 = (f32[256,256]{1,0:T(8,128)S(1)}, f32[256,256]{1,0:T(8,128)S(1)}, u32[]{:S(2)}, u32[]{:S(2)}) collective-permute-start(f32[256,256]{1,0:T(8,128)S(1)} %fusion.9.l0), channel_id=1, source_target_pairs={{0,1},{4,7},{1,0},{5,6},{2,3},{6,5},{3,2},{7,4},{8,9},{12,15},{9,8... | collective-permute-start | bytes 786440 | tf_op jit(solution)/shard_map/ppermute | solution.py:36
  60.0 3.8 %collective-permute-done.15.l2 = f32[256,256]{1,0:T(8,128)S(1)} collective-permute-done((f32[256,256]{1,0:T(8,128)S(1)}, f32[256,256]{1,0:T(8,128)S(1)}, u32[]{:S(2)}, u32[]{:S(2)}) %collective-permute-start.15) | collective-permute-done | bytes 262176 | tf_op jit(solution)/shard_map/ppermute | solution.py:36
  63.7 2.8 %collective-permute-done.16.l3 = f32[256,256]{1,0:T(8,128)S(1)} collective-permute-done((f32[256,256]{1,0:T(8,128)S(1)}, f32[256,256]{1,0:T(8,128)S(1)}, u32[]{:S(2)}, u32[]{:S(2)}) %collective-permute-start.16) | collective-permute-done | bytes 262176 | tf_op jit(solution)/shard_map/ppermute | solution.py:36
  66.6 3.0 %shard_map.125 = (f32[2,2,2,4,16,256]{5,4,3,2,1,0:T(8,128)S(1)}, f32[2,2,2,4,16,256]{5,4,3,2,1,0:T(8,128)S(1)}) custom-call(s32[40]{0:T(128)S(1)} %pad_add_fusion.info, f32[256,256]{1,0:T(8,128)S(1)} %fusion.9.l0, f32[256,256]{1,0:T(8,128)S(1)} %collective-permute-done.14.l1, f32[256,256]{1,0:T(8,128)S(1)} %collective-permute-done.15.l2, ...), custom_call_target="tpu_custom_call" | custom-call | flops 536870912 | bytes 3145728 | tf_op jit(solution)/shard_map/pallas_call | solution.py:265
  70.1 1.4 collective-permute-done.17
  71.6 0.9 fusion
  73.6 5.1 %collective-permute-start.18 = (f32[2,2,4,32,256]{4,3,2,1,0:T(8,128)}, f32[2,2,4,32,256]{4,3,2,1,0:T(8,128)}, u32[]{:S(2)}, u32[]{:S(2)}) collective-permute-start(f32[2,2,4,32,256]{4,3,2,1,0:T(8,128)} %pad_maximum_fusion), channel_id=1, source_target_pairs={{0,8},{4,60},{8,0},{12,20},{16,24},{20,12},{24,16},{28,36},{32,40}... | collective-permute-start | bytes 1572872 | tf_op jit(solution)/shard_map/ppermute | solution.py:36
  78.7 2.5 %collective-permute-start.12 = (f32[2,2,4,40,256]{4,3,2,1,0:T(8,128)}, f32[2,2,4,40,256]{4,3,2,1,0:T(8,128)}, u32[]{:S(2)}, u32[]{:S(2)}) collective-permute-start(f32[2,2,4,40,256]{4,3,2,1,0:T(8,128)} %fusion), channel_id=1, source_target_pairs={{0,64},{4,196},{64,0},{68,132},{128,192},{132,68},{192,128},{196,4... | collective-permute-start | bytes 1966088 | tf_op jit(solution)/shard_map/ppermute | solution.py:36
  81.4 4.2 %collective-permute-done.18 = f32[2,2,4,32,256]{4,3,2,1,0:T(8,128)} collective-permute-done((f32[2,2,4,32,256]{4,3,2,1,0:T(8,128)}, f32[2,2,4,32,256]{4,3,2,1,0:T(8,128)}, u32[]{:S(2)}, u32[]{:S(2)}) %collective-permute-start.18) | collective-permute-done | bytes 524320 | tf_op jit(solution)/shard_map/ppermute | solution.py:36
  85.6 1.1 maximum_add_fusion
  86.7 2.6 %collective-permute-start.19 = (f32[2,4,32,256]{3,2,1,0:T(8,128)S(1)}, f32[2,4,32,256]{3,2,1,0:T(8,128)S(1)}, u32[]{:S(2)}, u32[]{:S(2)}) collective-permute-start(f32[2,4,32,256]{3,2,1,0:T(8,128)S(1)} %slice_bitcast_fusion.2), channel_id=1, source_target_pairs={{0,64},{4,196},{64,0},{68,132},{128,192},{132,68},{192,128},{196,4... | collective-permute-start | bytes 786440 | tf_op jit(solution)/shard_map/ppermute | solution.py:36
  89.7 1.2 fusion.2
  90.9 2.4 %collective-permute-start.13 = (f32[2,4,40,256]{3,2,1,0:T(8,128)S(1)}, f32[2,4,40,256]{3,2,1,0:T(8,128)S(1)}, u32[]{:S(2)}, u32[]{:S(2)}) collective-permute-start(f32[2,4,40,256]{3,2,1,0:T(8,128)S(1)} %slice_bitcast_fusion), channel_id=1, source_target_pairs={{0,8},{4,60},{8,0},{12,20},{16,24},{20,12},{24,16},{28,36},{32,40}... | collective-permute-start | bytes 983048 | tf_op jit(solution)/shard_map/ppermute | solution.py:36
  93.4 4.7 %collective-permute-done.13 = f32[2,4,40,256]{3,2,1,0:T(8,128)S(1)} collective-permute-done((f32[2,4,40,256]{3,2,1,0:T(8,128)S(1)}, f32[2,4,40,256]{3,2,1,0:T(8,128)S(1)}, u32[]{:S(2)}, u32[]{:S(2)}) %collective-permute-start.13) | collective-permute-done | bytes 327712 | tf_op jit(solution)/shard_map/ppermute | solution.py:36
  98.7 5.2 %collective-permute-done.20 = f32[4,72,256]{2,1,0:T(8,128)S(1)} collective-permute-done((f32[4,72,256]{2,1,0:T(8,128)S(1)}, f32[4,72,256]{2,1,0:T(8,128)S(1)}, u32[]{:S(2)}, u32[]{:S(2)}) %collective-permute-start.20) | collective-permute-done | bytes 294944 | tf_op jit(solution)/shard_map/ppermute | solution.py:36
  105.4 2.6 %collective-permute-done.21 = f32[2,72,256]{2,1,0:T(8,128)S(1)} collective-permute-done((f32[2,72,256]{2,1,0:T(8,128)S(1)}, f32[2,72,256]{2,1,0:T(8,128)S(1)}, u32[]{:S(2)}, u32[]{:S(2)}) %collective-permute-start.21) | collective-permute-done | bytes 147488 | tf_op jit(solution)/shard_map/ppermute | solution.py:36
  108.1 2.9 %collective-permute-start.22 = (f32[72,256]{1,0:T(8,128)S(1)}, f32[72,256]{1,0:T(8,128)S(1)}, u32[]{:S(2)}, u32[]{:S(2)}) collective-permute-start(f32[72,256]{1,0:T(8,128)S(1)} %get-tuple-element.68), channel_id=1, source_target_pairs={{0,24},{4,44},{8,48},{12,36},{16,40},{20,60},{24,0},{28,52},{32,56... | collective-permute-start | bytes 221192 | tf_op jit(solution)/shard_map/ppermute | solution.py:36
  111.1 3.3 %collective-permute-done.22.came = f32[72,256]{1,0:T(8,128)S(1)} collective-permute-done((f32[72,256]{1,0:T(8,128)S(1)}, f32[72,256]{1,0:T(8,128)S(1)}, u32[]{:S(2)}, u32[]{:S(2)}) %collective-permute-start.22) | collective-permute-done | bytes 73760 | tf_op jit(solution)/shard_map/ppermute | solution.py:36
  114.6 26.1 %all_to_all.11 = f32[256,1,4]{2,1,0:T(1,128)S(1)} all-to-all(f32[256,1,4]{2,1,0:T(1,128)S(1)} %bitcast.71), channel_id=1, replica_groups=mesh['dp_0'=4,'dp_1'=8,'dp_2'=2,'mp'=4] {'dp_0','dp_1','dp_2','mp'}, dimensions={0} | all-to-all | bytes 8192 | tf_op jit(solution)/shard_map/all_to_all | solution.py:425
  (82 shorter events, 11.5 us)
Async XLA Ops:
  0.6 80.6 %copy-start = (s32[2,64]{1,0:T(2,128)S(1)}, s32[2,64]{1,0:T(2,128)}, u32[]{:S(2)}) copy-start(s32[2,64]{1,0:T(2,128)} %param.14) | copy-start | bytes 1540
  3.7 17.2 %collective-permute-start = (f32[2,256,256]{2,1,0:T(8,128)S(1)}, f32[2,256,256]{2,1,0:T(8,128)S(1)}, u32[]{:S(2)}, u32[]{:S(2)}) collective-permute-start(f32[2,256,256]{2,1,0:T(8,128)S(1)} %shard_map.120), channel_id=1, source_target_pairs={{0,1},{4,7},{1,0},{5,6},{2,3},{6,5},{3,2},{7,4},{8,9},{12,15},{9,8... | collective-permute-start | bytes 1572872 | tf_op jit(solution)/shard_map/ppermute | solution.py:36
  12.6 9.3 %collective-permute-start.5 = (f32[2,256,256]{2,1,0:T(8,128)S(1)}, f32[2,256,256]{2,1,0:T(8,128)S(1)}, u32[]{:S(2)}, u32[]{:S(2)}) collective-permute-start(f32[2,256,256]{2,1,0:T(8,128)S(1)} %shard_map.121), channel_id=1, source_target_pairs={{0,1},{4,7},{1,0},{5,6},{2,3},{6,5},{3,2},{7,4},{8,9},{12,15},{9,8... | collective-permute-start | bytes 1572872 | tf_op jit(solution)/shard_map/ppermute | solution.py:36
  20.9 3.0 %copy-start.7 = (s32[2,1,2]{2,1,0:T(1,128)S(1)}, s32[2,1,2]{2,1,0:T(1,128)}, u32[]{:S(2)}) copy-start(s32[2,1,2]{2,1,0:T(1,128)} %param.13) | copy-start | bytes 52
  21.0 5.3 %collective-permute-start.1 = (f32[256,256]{1,0:T(8,128)S(1)}, f32[256,256]{1,0:T(8,128)S(1)}, u32[]{:S(2)}, u32[]{:S(2)}) collective-permute-start(f32[256,256]{1,0:T(8,128)S(1)} %fusion.10), channel_id=1, source_target_pairs={{0,3},{4,5},{1,2},{5,4},{2,1},{6,7},{3,0},{7,6},{8,11},{12,13},{9,... | collective-permute-start | bytes 786440 | tf_op jit(solution)/shard_map/ppermute | solution.py:36
  22.0 7.5 %collective-permute-start.6 = (f32[256,256]{1,0:T(8,128)S(1)}, f32[256,256]{1,0:T(8,128)S(1)}, u32[]{:S(2)}, u32[]{:S(2)}) collective-permute-start(f32[256,256]{1,0:T(8,128)S(1)} %fusion.7), channel_id=1, source_target_pairs={{0,3},{4,5},{1,2},{5,4},{2,1},{6,7},{3,0},{7,6},{8,11},{12,13},{9,... | collective-permute-start | bytes 786440 | tf_op jit(solution)/shard_map/ppermute | solution.py:36
  24.6 13.3 %copy-start.5 = (f32[2,1,2,256]{3,2,1,0:T(2,128)S(1)}, f32[2,1,2,256]{3,2,1,0:T(2,128)}, u32[]{:S(2)}) copy-start(f32[2,1,2,256]{3,2,1,0:T(2,128)} %param.11) | copy-start | bytes 12292
  24.6 13.3 %copy-start.6 = (s32[2,1,2,256]{3,2,1,0:T(2,128)S(1)}, s32[2,1,2,256]{3,2,1,0:T(2,128)}, u32[]{:S(2)}) copy-start(s32[2,1,2,256]{3,2,1,0:T(2,128)} %param.12) | copy-start | bytes 12292
  26.3 5.9 %collective-permute-start.2 = (f32[256,256]{1,0:T(8,128)S(1)}, f32[256,256]{1,0:T(8,128)S(1)}, u32[]{:S(2)}, u32[]{:S(2)}) collective-permute-start(f32[256,256]{1,0:T(8,128)S(1)} %fusion.12.r0), channel_id=1, source_target_pairs={{0,3},{4,5},{1,2},{5,4},{2,1},{6,7},{3,0},{7,6},{8,11},{12,13},{9,... | collective-permute-start | bytes 786440 | tf_op jit(solution)/shard_map/ppermute | solution.py:36
  26.7 14.2 %collective-permute-start.3 = (f32[256,256]{1,0:T(8,128)S(1)}, f32[256,256]{1,0:T(8,128)S(1)}, u32[]{:S(2)}, u32[]{:S(2)}) collective-permute-start(f32[256,256]{1,0:T(8,128)S(1)} %fusion.12.r0), channel_id=1, source_target_pairs={{0,1},{4,7},{1,0},{5,6},{2,3},{6,5},{3,2},{7,4},{8,9},{12,15},{9,8... | collective-permute-start | bytes 786440 | tf_op jit(solution)/shard_map/ppermute | solution.py:36
  32.2 8.7 %collective-permute-start.4 = (f32[256,256]{1,0:T(8,128)S(1)}, f32[256,256]{1,0:T(8,128)S(1)}, u32[]{:S(2)}, u32[]{:S(2)}) collective-permute-start(f32[256,256]{1,0:T(8,128)S(1)} %collective-permute-done.2.r1), channel_id=1, source_target_pairs={{0,1},{4,7},{1,0},{5,6},{2,3},{6,5},{3,2},{7,4},{8,9},{12,15},{9,8... | collective-permute-start | bytes 786440 | tf_op jit(solution)/shard_map/ppermute | solution.py:36
  34.6 3.4 %collective-permute-start.7 = (f32[1,256]{1,0:T(1,128)S(1)}, f32[1,256]{1,0:T(1,128)S(1)}, u32[]{:S(2)}, u32[]{:S(2)}) collective-permute-start(f32[1,256]{1,0:T(1,128)S(1)} %bitcast.72), channel_id=1, source_target_pairs={{0,3},{4,5},{1,2},{5,4},{2,1},{6,7},{3,0},{7,6},{8,11},{12,13},{9,... | collective-permute-start | bytes 3080 | tf_op jit(solution)/shard_map/ppermute | solution.py:36
  34.6 6.3 %collective-permute-start.8 = (f32[1,256]{1,0:T(1,128)S(1)}, f32[1,256]{1,0:T(1,128)S(1)}, u32[]{:S(2)}, u32[]{:S(2)}) collective-permute-start(f32[1,256]{1,0:T(1,128)S(1)} %bitcast.73), channel_id=1, source_target_pairs={{0,1},{4,7},{1,0},{5,6},{2,3},{6,5},{3,2},{7,4},{8,9},{12,15},{9,8... | collective-permute-start | bytes 3080 | tf_op jit(solution)/shard_map/ppermute | solution.py:36
  34.9 6.0 %collective-permute-start.9 = (f32[1,256]{1,0:T(1,128)S(1)}, f32[1,256]{1,0:T(1,128)S(1)}, u32[]{:S(2)}, u32[]{:S(2)}) collective-permute-start(f32[1,256]{1,0:T(1,128)S(1)} %bitcast.74), channel_id=1, source_target_pairs={{0,2},{1,3},{2,0},{3,1},{4,6},{5,7},{6,4},{7,5},{8,10},{9,11},{10,... | collective-permute-start | bytes 3080 | tf_op jit(solution)/shard_map/ppermute | solution.py:342
  38.0 28.6 %copy-start.1 = (bf16[2,1,2,256,1024]{4,3,2,1,0:T(8,128)(2,1)S(1)}, bf16[2,1,2,256,1024]{4,3,2,1,0:T(8,128)(2,1)}, u32[]{:S(2)}) copy-start(bf16[2,1,2,256,1024]{4,3,2,1,0:T(8,128)(2,1)} %param.10) | copy-start | bytes 6291460
  38.0 21.7 %collective-permute-start.14 = (f32[256,256]{1,0:T(8,128)S(1)}, f32[256,256]{1,0:T(8,128)S(1)}, u32[]{:S(2)}, u32[]{:S(2)}) collective-permute-start(f32[256,256]{1,0:T(8,128)S(1)} %fusion.9.l0), channel_id=1, source_target_pairs={{0,3},{4,5},{1,2},{5,4},{2,1},{6,7},{3,0},{7,6},{8,11},{12,13},{9,... | collective-permute-start | bytes 786440 | tf_op jit(solution)/shard_map/ppermute | solution.py:36
  40.9 0.7 copy-start.4
  50.2 21.5 %collective-permute-start.10 = (f32[2,2,2,4,40,256]{5,4,3,2,1,0:T(8,128)}, f32[2,2,2,4,40,256]{5,4,3,2,1,0:T(8,128)S(1)}, u32[]{:S(2)}, u32[]{:S(2)}) collective-permute-start(f32[2,2,2,4,40,256]{5,4,3,2,1,0:T(8,128)} %get-tuple-element.31), channel_id=1, source_target_pairs={{0,4},{4,0},{1,5},{5,1},{2,6},{6,2},{3,7},{7,3},{8,12},{12,8},{9,1... | collective-permute-start | bytes 3932168 | tf_op jit(solution)/shard_map/ppermute | solution.py:381
  57.3 6.4 %collective-permute-start.15 = (f32[256,256]{1,0:T(8,128)S(1)}, f32[256,256]{1,0:T(8,128)S(1)}, u32[]{:S(2)}, u32[]{:S(2)}) collective-permute-start(f32[256,256]{1,0:T(8,128)S(1)} %fusion.9.l0), channel_id=1, source_target_pairs={{0,1},{4,7},{1,0},{5,6},{2,3},{6,5},{3,2},{7,4},{8,9},{12,15},{9,8... | collective-permute-start | bytes 786440 | tf_op jit(solution)/shard_map/ppermute | solution.py:36
  59.7 6.9 %collective-permute-start.16 = (f32[256,256]{1,0:T(8,128)S(1)}, f32[256,256]{1,0:T(8,128)S(1)}, u32[]{:S(2)}, u32[]{:S(2)}) collective-permute-start(f32[256,256]{1,0:T(8,128)S(1)} %collective-permute-done.14.l1), channel_id=1, source_target_pairs={{0,1},{4,7},{1,0},{5,6},{2,3},{6,5},{3,2},{7,4},{8,9},{12,15},{9,8... | collective-permute-start | bytes 786440 | tf_op jit(solution)/shard_map/ppermute | solution.py:36
  66.6 3.1 %copy-start.8 = (f32[2,2,2,4,16,256]{5,4,3,2,1,0:T(8,128)S(1)}, f32[2,2,2,4,16,256]{5,4,3,2,1,0:T(8,128)}, u32[]{:S(2)}) copy-start(f32[2,2,2,4,16,256]{5,4,3,2,1,0:T(8,128)} %get-tuple-element.32) | copy-start | bytes 1572868
  69.5 2.1 %copy-start.2 = (f32[2,2,2,4,40,256]{5,4,3,2,1,0:T(8,128)S(1)}, f32[2,2,2,4,40,256]{5,4,3,2,1,0:T(8,128)}, u32[]{:S(2)}) copy-start(f32[2,2,2,4,40,256]{5,4,3,2,1,0:T(8,128)} %get-tuple-element.30) | copy-start | bytes 3932164
  69.5 2.0 %collective-permute-start.17 = (f32[2,2,2,4,16,256]{5,4,3,2,1,0:T(8,128)S(1)}, f32[2,2,2,4,16,256]{5,4,3,2,1,0:T(8,128)S(1)}, u32[]{:S(2)}, u32[]{:S(2)}) collective-permute-start(f32[2,2,2,4,16,256]{5,4,3,2,1,0:T(8,128)S(1)} %get-tuple-element.38), channel_id=1, source_target_pairs={{0,4},{4,0},{1,5},{5,1},{2,6},{6,2},{3,7},{7,3},{8,12},{12,8},{9,1... | collective-permute-start | bytes 1572872 | tf_op jit(solution)/shard_map/ppermute | solution.py:381
  69.6 2.9 %collective-permute-start.11 = (f32[2,2,2,4,16,256]{5,4,3,2,1,0:T(8,128)S(1)}, f32[2,2,2,4,16,256]{5,4,3,2,1,0:T(8,128)S(1)}, u32[]{:S(2)}, u32[]{:S(2)}) collective-permute-start(f32[2,2,2,4,16,256]{5,4,3,2,1,0:T(8,128)S(1)} %copy-done.8), channel_id=1, source_target_pairs={{0,4},{4,0},{1,5},{5,1},{2,6},{6,2},{3,7},{7,3},{8,12},{12,8},{9,1... | collective-permute-start | bytes 1572872 | tf_op jit(solution)/shard_map/ppermute | solution.py:381
  71.6 1.1 copy-start.3
  73.6 12.0 %collective-permute-start.18 = (f32[2,2,4,32,256]{4,3,2,1,0:T(8,128)}, f32[2,2,4,32,256]{4,3,2,1,0:T(8,128)}, u32[]{:S(2)}, u32[]{:S(2)}) collective-permute-start(f32[2,2,4,32,256]{4,3,2,1,0:T(8,128)} %pad_maximum_fusion), channel_id=1, source_target_pairs={{0,8},{4,60},{8,0},{12,20},{16,24},{20,12},{24,16},{28,36},{32,40}... | collective-permute-start | bytes 1572872 | tf_op jit(solution)/shard_map/ppermute | solution.py:36
  78.7 11.0 %collective-permute-start.12 = (f32[2,2,4,40,256]{4,3,2,1,0:T(8,128)}, f32[2,2,4,40,256]{4,3,2,1,0:T(8,128)}, u32[]{:S(2)}, u32[]{:S(2)}) collective-permute-start(f32[2,2,4,40,256]{4,3,2,1,0:T(8,128)} %fusion), channel_id=1, source_target_pairs={{0,64},{4,196},{64,0},{68,132},{128,192},{132,68},{192,128},{196,4... | collective-permute-start | bytes 1966088 | tf_op jit(solution)/shard_map/ppermute | solution.py:36
  86.7 6.6 %collective-permute-start.19 = (f32[2,4,32,256]{3,2,1,0:T(8,128)S(1)}, f32[2,4,32,256]{3,2,1,0:T(8,128)S(1)}, u32[]{:S(2)}, u32[]{:S(2)}) collective-permute-start(f32[2,4,32,256]{3,2,1,0:T(8,128)S(1)} %slice_bitcast_fusion.2), channel_id=1, source_target_pairs={{0,64},{4,196},{64,0},{68,132},{128,192},{132,68},{192,128},{196,4... | collective-permute-start | bytes 786440 | tf_op jit(solution)/shard_map/ppermute | solution.py:36
  90.9 7.2 %collective-permute-start.13 = (f32[2,4,40,256]{3,2,1,0:T(8,128)S(1)}, f32[2,4,40,256]{3,2,1,0:T(8,128)S(1)}, u32[]{:S(2)}, u32[]{:S(2)}) collective-permute-start(f32[2,4,40,256]{3,2,1,0:T(8,128)S(1)} %slice_bitcast_fusion), channel_id=1, source_target_pairs={{0,8},{4,60},{8,0},{12,20},{16,24},{20,12},{24,16},{28,36},{32,40}... | collective-permute-start | bytes 983048 | tf_op jit(solution)/shard_map/ppermute | solution.py:36
  98.3 5.7 %collective-permute-start.20 = (f32[4,72,256]{2,1,0:T(8,128)S(1)}, f32[4,72,256]{2,1,0:T(8,128)S(1)}, u32[]{:S(2)}, u32[]{:S(2)}) collective-permute-start(f32[4,72,256]{2,1,0:T(8,128)S(1)} %pad_maximum_fusion.1), channel_id=1, source_target_pairs={{0,192},{4,68},{64,128},{68,4},{128,64},{132,196},{192,0},{196,132... | collective-permute-start | bytes 884744 | tf_op jit(solution)/shard_map/ppermute | solution.py:36
  104.0 4.1 %collective-permute-start.21 = (f32[2,72,256]{2,1,0:T(8,128)S(1)}, f32[2,72,256]{2,1,0:T(8,128)S(1)}, u32[]{:S(2)}, u32[]{:S(2)}) collective-permute-start(f32[2,72,256]{2,1,0:T(8,128)S(1)} %slice.153), channel_id=1, source_target_pairs={{0,56},{4,12},{8,16},{12,4},{16,8},{20,28},{24,32},{28,20},{32,24}... | collective-permute-start | bytes 442376 | tf_op jit(solution)/shard_map/ppermute | solution.py:36
  108.1 6.3 %collective-permute-start.22 = (f32[72,256]{1,0:T(8,128)S(1)}, f32[72,256]{1,0:T(8,128)S(1)}, u32[]{:S(2)}, u32[]{:S(2)}) collective-permute-start(f32[72,256]{1,0:T(8,128)S(1)} %get-tuple-element.68), channel_id=1, source_target_pairs={{0,24},{4,44},{8,48},{12,36},{16,40},{20,60},{24,0},{28,52},{32,56... | collective-permute-start | bytes 221192 | tf_op jit(solution)/shard_map/ppermute | solution.py:36
where the time goes:
time: 143 us; the launch traced here: 142 us
  starting transfers between devices  39.6 us (28%)
  waiting for transfers between devices  36.3 us (25%)
  Pallas kernels  28.7 us (20%)
  blocking collectives  26.1 us (18%)
  other arithmetic  6.52 us (5%)
  local copies, waits for them, and re-layouts  3.18 us (2%)
  between operations  1.65 us (1%)
    ppermute x19, waiting for transfers between devices, swap(): return lax.ppermute(value, axes, pairs)  34.9 us
    ppermute x19, starting transfers between devices, swap(): return lax.ppermute(value, axes, pairs)  28.9 us
    all_to_all x1, blocking collectives, per_device(): small = lax.all_to_all(small, (X, Z, C, Y), 0, 0, tiled=True)  26.1 us
    pallas_call x4, Pallas kernels, product(): pl.pallas_call(functools.partial(product_kernel, at), in_specs=[pl.BlockS...  16.3 us
    pallas_call x2, Pallas kernels, kernel_call(): pl.pallas_call(body, grid_spec=pltpu.PrefetchScalarGridSpec(num_scalar_pr...  11.5 us
    ppermute x3, starting transfers between devices, per_device(): core = lambda value: lax.ppermute(value, C, [(0, 1), (1, 0)])  7.74 us
    ppermute x1, starting transfers between devices, per_device(): lax.ppermute(shift, Y, opposite)  2.95 us
  transfers between devices with their start and end apart: 23, of which 13 were waited for; matrix products, arithmetic and copies ran while one was open for 5% of the time, Pallas kernels for 18%

commit v1 on v0

--- a/solution.py
+++ b/solution.py
@@ -15,6 +15,7 @@
 DP = (X, Z, C)
 MP_DP = (Y, X, Z, C)
 BETA = 0.1
+GRANT_FORWARD, GRANT_BACKWARD = 53, 48
 
 
 def first(i, c, n):
@@ -79,16 +80,10 @@
     tall = part.shape[0] // 16
     blocks[...] = part.reshape(16, tall, part.shape[1])
     core = info[4]
-    for side, order in enumerate((ORDER_HERE, ORDER_THERE)):
-        which = core if side == 0 else 1 - core
+    for out, order, which in zip(outs, (ORDER_HERE, ORDER_THERE), (core, 1 - core)):
         for p in range(8):
-            block = blocks[2 * info[order + p] + which]
-            row = 0
-            for out, z_dim in outs[side]:
-                height = out.shape[-2]
-                at = (0, p // 4, 0, p % 4) if z_dim == 1 else (p // 4, 0, 0, p % 4)
-                out[at] = block[row : row + height]
-                row += height
+            at = (0, p // 4, 0, p % 4) if out.shape[0] == 1 else (p // 4, 0, 0, p % 4)
+            out[at] = blocks[2 * info[order + p] + which]
 
 
 CONTRACT = (((0,), (0,)), ((), ()))
@@ -96,7 +91,7 @@
 
 def first_kernel(
     info, r0, r1, r2, r3, s0, s1, s2, s3, reference, mask, hidden,
-    keep_p, keep_q, send_p, send_q, margins, columns,
+    keep_p, send_p, margins, columns,
     r_all, s_all, d_latent, blocks, tiles, arrived,
 ):
     seq = reference.shape[1]
@@ -148,13 +143,12 @@
     part = lax.dot_general(
         tiles[step % 2], d_latent[...], CONTRACT, preferred_element_type=jnp.float32
     )
-    arrange(
-        info, part, blocks, (((keep_p, 1), (keep_q, 0)), ((send_p, 1), (send_q, 0)))
-    )
 
     @pl.when(step < 2)
     def _():
         fetch(step + 2).start()
+
+    arrange(info, part, blocks, (keep_p, send_p))
 
 
 def second_kernel(
@@ -173,45 +167,46 @@
     part = lax.dot_general(
         rows[...], d_readout[...], CONTRACT, preferred_element_type=jnp.float32
     )
-    arrange(info, part, blocks, (((keep, 0),), ((send, 0),)))
-
-
-def product_kernel(at, order, value, weights, out, buffer, arrived):
-    seq = out.shape[1]
-    copies = [
-        pltpu.make_async_copy(
-            value.at[pl.ds(pl.multiple_of(order[at + i] * seq, seq), seq)],
-            buffer.at[i],
-            arrived.at[i],
-        )
-        for i in range(2)
-    ]
-    for copy in copies:
-        copy.start()
-    for i, copy in enumerate(copies):
+    arrange(info, part, blocks, (keep, send))
+
+
+def product_kernel(order, value, weights, send, keep, held, factors, arrived):
+    seq = send.shape[1]
+    own = pltpu.make_async_copy(weights, factors, arrived.at[4])
+    own.start()
+    copies = []
+    for i in range(4):
+        at = pl.ds(pl.multiple_of(order[(i + 2) % 4] * seq, seq), seq)
+        copies.append((at, pltpu.make_async_copy(value.at[at], held.at[at], arrived.at[i])))
+        copies[i][1].start()
+    own.wait()
+    for i, (at, copy) in enumerate(copies):
         copy.wait()
-        out[i] = jnp.dot(buffer[i], weights[...], preferred_element_type=jnp.float32)
-
-
-def product(order, at, value, weights, seq):
+        out = send if i < 2 else keep
+        out[i % 2] = jnp.dot(held[at], factors[...], preferred_element_type=jnp.float32)
+
+
+def product(order, value, weights, seq):
     wide, rank = weights.shape
+    half = jax.ShapeDtypeStruct((2, seq, rank), jnp.float32)
     return pl.pallas_call(
-        functools.partial(product_kernel, at),
+        product_kernel,
         in_specs=[
             pl.BlockSpec(memory_space=pltpu.SMEM),
             pl.BlockSpec(memory_space=pltpu.HBM),
-            pl.BlockSpec(memory_space=pltpu.VMEM),
+            pl.BlockSpec(memory_space=pltpu.HBM),
         ],
-        out_specs=pl.BlockSpec(memory_space=pltpu.VMEM),
+        out_specs=[pl.BlockSpec(memory_space=pltpu.VMEM)] * 2,
         scratch_shapes=[
-            pltpu.VMEM((2, seq, wide), value.dtype),
-            pltpu.SemaphoreType.DMA((2,)),
+            pltpu.VMEM(value.shape, value.dtype),
+            pltpu.VMEM(weights.shape, weights.dtype),
+            pltpu.SemaphoreType.DMA((5,)),
         ],
-        out_shape=jax.ShapeDtypeStruct((2, seq, rank), jnp.float32),
-        compiler_params=pltpu.CompilerParams(vmem_limit_bytes=53 * 2**20),
+        out_shape=[half, half],
+        compiler_params=pltpu.CompilerParams(vmem_limit_bytes=GRANT_FORWARD * 2**20),
         cost_estimate=pl.CostEstimate(
-            flops=4 * seq * wide * rank,
-            bytes_accessed=4 * seq * wide + 2 * wide * rank + 8 * seq * rank,
+            flops=8 * seq * wide * rank,
+            bytes_accessed=8 * seq * wide + 2 * wide * rank + 16 * seq * rank,
             transcendentals=0,
         ),
     )(order, value, weights)
@@ -260,7 +255,8 @@
     )
 
 
-def kernel_call(body, info, wholes, streamed, outs, scratch, rank, by_hand):
+def kernel_call(body, info, wholes, streamed, outs, scratch, rank, name):
+    by_hand = name == "backward_a"
     tokens, wide = streamed.shape
     return pl.pallas_call(
         body,
@@ -279,7 +275,7 @@
         out_shape=[shape for shape, _ in outs],
         compiler_params=pltpu.CompilerParams(
             dimension_semantics=("arbitrary",),
-            vmem_limit_bytes=(53 if by_hand else 24) * 2**20,
+            vmem_limit_bytes=(GRANT_BACKWARD if by_hand else 24) * 2**20,
         ),
         cost_estimate=pl.CostEstimate(
             flops=2 * tokens * wide * rank,
@@ -309,20 +305,15 @@
     place = lax.axis_index(DP)
     pairs = lax.axis_size(DP)
     tall_a, tall_b = ff // pairs, width // pairs
-    late_a = (tall_a - tall_b) // 16 * 8 if tall_a > 2 * tall_b else tall_a // 2
-    late_a = min(late_a, tall_b)
 
     hidden = hidden_activation.reshape(tokens, ff)
     rows = target_head_rows.reshape(tokens, width)
     near, far, mine, late = order_of_four(y, c)
     order = jnp.stack([mine, late, near, far]).astype(jnp.int32)
 
-    readout_send = product(order, 2, rows, adapter_down_second, seq)
+    readout_send, readout_keep = product(order, rows, adapter_down_second, seq)
     readout_send, hidden_next = lax.optimization_barrier((readout_send, hidden))
-    latent_send = product(order, 2, hidden_next, adapter_down_first, seq)
-    latent_send, rows_next, hidden_next = lax.optimization_barrier((latent_send, rows, hidden))
-    readout_keep = product(order, 0, rows_next, adapter_down_second, seq)
-    latent_keep = product(order, 0, hidden_next, adapter_down_first, seq)
+    latent_send, latent_keep = product(order, hidden_next, adapter_down_first, seq)
 
     def own_sum(send, keep):
         came = swap(send, Y, first)
@@ -345,17 +336,11 @@
     entry = jnp.asarray(table())[place * ways + y]
     lengths = sequence_tile_lengths.reshape(-1).astype(jnp.int32)
     info = jnp.concatenate([entry, lengths, jnp.zeros((4,), jnp.int32)])
-    early = tall_a - late_a
-    outs = [
-        x_major(early, rank, PLACE_HERE),
-        z_major(late_a, rank, PLACE_HERE),
-        x_major(early, rank, PLACE_THERE),
-        z_major(late_a, rank, PLACE_THERE),
-    ]
+    outs = [x_major(tall_a, rank, PLACE_HERE), x_major(tall_a, rank, PLACE_THERE)]
     for shape in ((8, 128), (seq, 8)):
         block = jax.ShapeDtypeStruct(shape, jnp.float32)
         outs.append((block, whole(block)))
-    keep_p, keep_q, send_p, send_q, margins, columns = kernel_call(
+    keep_p, send_p, margins, columns = kernel_call(
         first_kernel,
         info,
         (
@@ -375,12 +360,11 @@
             pltpu.SemaphoreType.DMA((2,)),
         ],
         rank,
-        True,
+        "backward_a",
     )
     margin = margins[:micro, 0]
     core = lambda value: lax.ppermute(value, C, [(0, 1), (1, 0)])
     came_p = core(send_p)
-    came_q = core(send_q)
     keep_b, send_b = kernel_call(
         second_kernel,
         info,
@@ -393,15 +377,13 @@
             pltpu.VMEM((16, tall_b, rank), jnp.float32),
         ],
         rank,
-        False,
+        "backward_b",
     )
     came_b = core(send_b)
 
-    p_send, came_q = lax.optimization_barrier((keep_p[0] + came_p[0], came_q))
-    p = swap(p_send, X, first)
+    p = swap(keep_p[0] + came_p[0], X, first)
     p = keep_p[1] + came_p[1] + p
-    late_rows = lambda i: jnp.concatenate([keep_q[i] + came_q[i], keep_b[i] + came_b[i]], axis=-2)
-    w = late_rows(1) + swap(late_rows(0), Z, first)
+    w = keep_b[1] + came_b[1] + swap(keep_b[0] + came_b[0], Z, first)
     p = p[1] + swap(p[0], Z, first)
     w = w[1] + swap(w[0], X, first)
     both = lambda i: jnp.concatenate([p[i], w[i]], axis=-2)

time: 143 us -> 152 us (1.063)
  waiting for transfers between devices: 36.3 us -> 47 us
  Pallas kernels: 28.7 us -> 22.2 us
  starting transfers between devices: 39.6 us -> 41.9 us
    ppermute x19, waiting for transfers between devices: 34.9 us -> 46.4 us  [swap(): return lax.ppermute(value, axes, pairs)]
    pallas_call x4 -> x2, Pallas kernels: 16.3 us -> 12.1 us  [product(): pl.pallas_call(product_kernel, in_specs=[pl.BlockSpec(memory_space=pltpu....]
    ppermute x19, starting transfers between devices: 28.9 us -> 32.6 us  [swap(): return lax.ppermute(value, axes, pairs)]
    ppermute x1, starting transfers between devices: 2.95 us -> 0.01 us  [per_device(): lax.ppermute(shift, Y, opposite)]
    pallas_call x2, Pallas kernels: 11.5 us -> 9.3 us  [kernel_call(): pl.pallas_call(body, grid_spec=pltpu.PrefetchScalarGridSpec(num_scalar_pr...]
    ppermute x3 -> x2, starting transfers between devices: 7.74 us -> 9.26 us  [per_device(): core = lambda value: lax.ppermute(value, C, [(0, 1), (1, 0)])]
  transfers between devices with their start and end apart: 23 -> 22, of which waited for: 13 -> 13; matrix products, arithmetic and copies ran while one was open for 5% -> 6% of each run, Pallas kernels for 18% -> 7%
where the time goes in v1:
time: 152 us; the launch traced here: 151 us
  waiting for transfers between devices  47 us (31%)
  starting transfers between devices  41.9 us (28%)
  blocking collectives  27.4 us (18%)
  Pallas kernels  22.2 us (15%)
  other arithmetic  7.77 us (5%)
  local copies, waits for them, and re-layouts  3.17 us (2%)
  between operations  1.62 us (1%)
    ppermute x19, waiting for transfers between devices, swap(): return lax.ppermute(value, axes, pairs)  46.4 us
    ppermute x19, starting transfers between devices, swap(): return lax.ppermute(value, axes, pairs)  32.6 us
    all_to_all x1, blocking collectives, per_device(): small = lax.all_to_all(small, (X, Z, C, Y), 0, 0, tiled=True)  27.4 us
    pallas_call x2, Pallas kernels, product(): pl.pallas_call(product_kernel, in_specs=[pl.BlockSpec(memory_space=pltpu....  12.1 us
    pallas_call x2, Pallas kernels, kernel_call(): pl.pallas_call(body, grid_spec=pltpu.PrefetchScalarGridSpec(num_scalar_pr...  9.3 us
    ppermute x2, starting transfers between devices, per_device(): core = lambda value: lax.ppermute(value, C, [(0, 1), (1, 0)])  9.26 us
  transfers between devices with their start and end apart: 22, of which 13 were waited for; matrix products, arithmetic and copies ran while one was open for 6% of the time, Pallas kernels for 7%

profile of v1, /device:TPU:1, one launch (start us, length us, event | category | flops | bytes accessed | tf_op | source)
XLA Modules:
  0.0 151.2 jit_solution(3559050588017127586)
XLA Ops:
  0.8 4.3 %shard_map.120 = (f32[2,256,256]{2,1,0:T(8,128)S(1)}, f32[2,256,256]{2,1,0:T(8,128)}) custom-call(s32[4]{0:T(128)S(1)} %pad_add_fusion.1.order, bf16[1024,1024]{1,0:T(8,128)(2,1)} %bitcast.64, bf16[1024,256]{1,0:T(8,128)(2,1)} %weights.2), custom_call_target="tpu_custom_call" | custom-call | flops 536870912 | bytes 3670016 | tf_op jit(solution)/shard_map/pallas_call | solution.py:192
  5.1 3.6 %collective-permute-start = (f32[2,256,256]{2,1,0:T(8,128)S(1)}, f32[2,256,256]{2,1,0:T(8,128)S(1)}, u32[]{:S(2)}, u32[]{:S(2)}) collective-permute-start(f32[2,256,256]{2,1,0:T(8,128)S(1)} %get-tuple-element.24), channel_id=1, source_target_pairs={{0,1},{4,7},{1,0},{5,6},{2,3},{6,5},{3,2},{7,4},{8,9},{12,15},{9,8... | collective-permute-start | bytes 1572872 | tf_op jit(solution)/shard_map/ppermute | solution.py:37
  8.7 7.8 %shard_map.121 = (f32[2,256,256]{2,1,0:T(8,128)S(1)}, f32[2,256,256]{2,1,0:T(8,128)}) custom-call(s32[4]{0:T(128)S(1)} %pad_add_fusion.1.order, bf16[1024,3584]{1,0:T(8,128)(2,1)} %bitcast.73, bf16[3584,256]{1,0:T(8,128)(2,1)} %weights.3), custom_call_target="tpu_custom_call" | custom-call | flops 1879048192 | bytes 10223616 | tf_op jit(solution)/shard_map/pallas_call | solution.py:192
  16.8 11.8 %collective-permute-done.5 = f32[2,256,256]{2,1,0:T(8,128)S(1)} collective-permute-done((f32[2,256,256]{2,1,0:T(8,128)S(1)}, f32[2,256,256]{2,1,0:T(8,128)S(1)}, u32[]{:S(2)}, u32[]{:S(2)}) %collective-permute-start.5) | collective-permute-done | bytes 524320 | tf_op jit(solution)/shard_map/ppermute | solution.py:37
  28.7 1.0 fusion.7
  31.7 1.0 fusion.12.r0
  32.8 1.5 %collective-permute-start.2 = (f32[256,256]{1,0:T(8,128)S(1)}, f32[256,256]{1,0:T(8,128)S(1)}, u32[]{:S(2)}, u32[]{:S(2)}) collective-permute-start(f32[256,256]{1,0:T(8,128)S(1)} %fusion.12.r0), channel_id=1, source_target_pairs={{0,3},{4,5},{1,2},{5,4},{2,1},{6,7},{3,0},{7,6},{8,11},{12,13},{9,... | collective-permute-start | bytes 786440 | tf_op jit(solution)/shard_map/ppermute | solution.py:37
  35.5 3.4 %collective-permute-done.2.r1 = f32[256,256]{1,0:T(8,128)S(1)} collective-permute-done((f32[256,256]{1,0:T(8,128)S(1)}, f32[256,256]{1,0:T(8,128)S(1)}, u32[]{:S(2)}, u32[]{:S(2)}) %collective-permute-start.2) | collective-permute-done | bytes 262176 | tf_op jit(solution)/shard_map/ppermute | solution.py:37
  38.9 2.2 %collective-permute-start.7 = (f32[1,256]{1,0:T(1,128)S(1)}, f32[1,256]{1,0:T(1,128)S(1)}, u32[]{:S(2)}, u32[]{:S(2)}) collective-permute-start(f32[1,256]{1,0:T(1,128)S(1)} %bitcast.69), channel_id=1, source_target_pairs={{0,3},{4,5},{1,2},{5,4},{2,1},{6,7},{3,0},{7,6},{8,11},{12,13},{9,... | collective-permute-start | bytes 3080 | tf_op jit(solution)/shard_map/ppermute | solution.py:37
  41.1 2.1 %collective-permute-start.8 = (f32[1,256]{1,0:T(1,128)S(1)}, f32[1,256]{1,0:T(1,128)S(1)}, u32[]{:S(2)}, u32[]{:S(2)}) collective-permute-start(f32[1,256]{1,0:T(1,128)S(1)} %bitcast.70), channel_id=1, source_target_pairs={{0,1},{4,7},{1,0},{5,6},{2,3},{6,5},{3,2},{7,4},{8,9},{12,15},{9,8... | collective-permute-start | bytes 3080 | tf_op jit(solution)/shard_map/ppermute | solution.py:37
  43.3 3.1 %collective-permute-done.8.s2 = f32[1,256]{1,0:T(1,128)S(1)} collective-permute-done((f32[1,256]{1,0:T(1,128)S(1)}, f32[1,256]{1,0:T(1,128)S(1)}, u32[]{:S(2)}, u32[]{:S(2)}) %collective-permute-start.8) | collective-permute-done | bytes 1056 | tf_op jit(solution)/shard_map/ppermute | solution.py:37
  47.1 6.4 %shard_map.122 = (f32[2,2,2,4,56,256]{5,4,3,2,1,0:T(8,128)S(1)}, f32[2,2,2,4,56,256]{5,4,3,2,1,0:T(8,128)S(1)}, f32[8,128]{1,0:T(8,128)S(1)}, f32[256,8]{1,0:T(8,128)S(1)}) custom-call(s32[40]{0:T(128)S(1)} %pad_add_fusion.info, f32[256,256]{1,0:T(8,128)S(1)} %fusion.12.r0, f32[256,256]{1,0:T(8,128)S(1)} %collective-permute-done.2.r1, ...), custom_call_target="tpu_custom_call" | custom-call | flops 1879048192 | bytes 11010048 | tf_op jit(solution)/shard_map/pallas_call | solution.py:261
  53.4 5.3 %collective-permute-start.10 = (f32[2,2,2,4,56,256]{5,4,3,2,1,0:T(8,128)S(1)}, f32[2,2,2,4,56,256]{5,4,3,2,1,0:T(8,128)S(1)}, u32[]{:S(2)}, u32[]{:S(2)}) collective-permute-start(f32[2,2,2,4,56,256]{5,4,3,2,1,0:T(8,128)S(1)} %get-tuple-element.29), channel_id=1, source_target_pairs={{0,4},{4,0},{1,5},{5,1},{2,6},{6,2},{3,7},{7,3},{8,12},{12,8},{9,1... | collective-permute-start | bytes 5505032 | tf_op jit(solution)/shard_map/ppermute | solution.py:366
  59.0 2.1 %collective-permute-start.14 = (f32[256,256]{1,0:T(8,128)S(1)}, f32[256,256]{1,0:T(8,128)S(1)}, u32[]{:S(2)}, u32[]{:S(2)}) collective-permute-start(f32[256,256]{1,0:T(8,128)S(1)} %fusion.9.l0), channel_id=1, source_target_pairs={{0,1},{4,7},{1,0},{5,6},{2,3},{6,5},{3,2},{7,4},{8,9},{12,15},{9,8... | collective-permute-start | bytes 786440 | tf_op jit(solution)/shard_map/ppermute | solution.py:37
  61.1 3.1 %collective-permute-done.13.l1 = f32[256,256]{1,0:T(8,128)S(1)} collective-permute-done((f32[256,256]{1,0:T(8,128)S(1)}, f32[256,256]{1,0:T(8,128)S(1)}, u32[]{:S(2)}, u32[]{:S(2)}) %collective-permute-start.13) | collective-permute-done | bytes 262176 | tf_op jit(solution)/shard_map/ppermute | solution.py:37
  64.2 3.4 %collective-permute-start.15 = (f32[256,256]{1,0:T(8,128)S(1)}, f32[256,256]{1,0:T(8,128)S(1)}, u32[]{:S(2)}, u32[]{:S(2)}) collective-permute-start(f32[256,256]{1,0:T(8,128)S(1)} %collective-permute-done.13.l1), channel_id=1, source_target_pairs={{0,1},{4,7},{1,0},{5,6},{2,3},{6,5},{3,2},{7,4},{8,9},{12,15},{9,8... | collective-permute-start | bytes 786440 | tf_op jit(solution)/shard_map/ppermute | solution.py:37
  68.3 3.1 %collective-permute-done.15.l3 = f32[256,256]{1,0:T(8,128)S(1)} collective-permute-done((f32[256,256]{1,0:T(8,128)S(1)}, f32[256,256]{1,0:T(8,128)S(1)}, u32[]{:S(2)}, u32[]{:S(2)}) %collective-permute-start.15) | collective-permute-done | bytes 262176 | tf_op jit(solution)/shard_map/ppermute | solution.py:37
  71.4 2.9 %shard_map.123 = (f32[2,2,2,4,16,256]{5,4,3,2,1,0:T(8,128)S(1)}, f32[2,2,2,4,16,256]{5,4,3,2,1,0:T(8,128)S(1)}) custom-call(s32[40]{0:T(128)S(1)} %pad_add_fusion.info, f32[256,256]{1,0:T(8,128)S(1)} %fusion.9.l0, f32[256,256]{1,0:T(8,128)S(1)} %collective-permute-done.13.l1, f32[256,256]{1,0:T(8,128)S(1)} %collective-permute-done.14.l2, ...), custom_call_target="tpu_custom_call" | custom-call | flops 536870912 | bytes 3145728 | tf_op jit(solution)/shard_map/pallas_call | solution.py:261
  74.4 4.0 %collective-permute-start.16 = (f32[2,2,2,4,16,256]{5,4,3,2,1,0:T(8,128)S(1)}, f32[2,2,2,4,16,256]{5,4,3,2,1,0:T(8,128)S(1)}, u32[]{:S(2)}, u32[]{:S(2)}) collective-permute-start(f32[2,2,2,4,16,256]{5,4,3,2,1,0:T(8,128)S(1)} %get-tuple-element.32), channel_id=1, source_target_pairs={{0,4},{4,0},{1,5},{5,1},{2,6},{6,2},{3,7},{7,3},{8,12},{12,8},{9,1... | collective-permute-start | bytes 1572872 | tf_op jit(solution)/shard_map/ppermute | solution.py:366
  78.4 1.2 fusion
  79.5 2.3 %collective-permute-start.11 = (f32[2,2,4,56,256]{4,3,2,1,0:T(8,128)}, f32[2,2,4,56,256]{4,3,2,1,0:T(8,128)S(1)}, u32[]{:S(2)}, u32[]{:S(2)}) collective-permute-start(f32[2,2,4,56,256]{4,3,2,1,0:T(8,128)} %fusion), channel_id=1, source_target_pairs={{0,64},{4,196},{64,0},{68,132},{128,192},{132,68},{192,128},{196,4... | collective-permute-start | bytes 2752520 | tf_op jit(solution)/shard_map/ppermute | solution.py:37
  82.7 5.7 %collective-permute-start.17 = (f32[2,2,4,16,256]{4,3,2,1,0:T(8,128)S(1)}, f32[2,2,4,16,256]{4,3,2,1,0:T(8,128)}, u32[]{:S(2)}, u32[]{:S(2)}) collective-permute-start(f32[2,2,4,16,256]{4,3,2,1,0:T(8,128)S(1)} %fusion.4), channel_id=1, source_target_pairs={{0,8},{4,60},{8,0},{12,20},{16,24},{20,12},{24,16},{28,36},{32,40}... | collective-permute-start | bytes 786440 | tf_op jit(solution)/shard_map/ppermute | solution.py:37
  88.5 3.7 %collective-permute-done.17 = f32[2,2,4,16,256]{4,3,2,1,0:T(8,128)} collective-permute-done((f32[2,2,4,16,256]{4,3,2,1,0:T(8,128)S(1)}, f32[2,2,4,16,256]{4,3,2,1,0:T(8,128)}, u32[]{:S(2)}, u32[]{:S(2)}) %collective-permute-start.17) | collective-permute-done | bytes 262176 | tf_op jit(solution)/shard_map/ppermute | solution.py:37
  92.2 1.1 fusion.6
  93.8 1.3 fusion.2
  95.2 4.9 %collective-permute-start.12 = (f32[2,4,56,256]{3,2,1,0:T(8,128)S(1)}, f32[2,4,56,256]{3,2,1,0:T(8,128)S(1)}, u32[]{:S(2)}, u32[]{:S(2)}) collective-permute-start(f32[2,4,56,256]{3,2,1,0:T(8,128)S(1)} %slice_bitcast_fusion), channel_id=1, source_target_pairs={{0,8},{4,60},{8,0},{12,20},{16,24},{20,12},{24,16},{28,36},{32,40}... | collective-permute-start | bytes 1376264 | tf_op jit(solution)/shard_map/ppermute | solution.py:37
  100.1 5.8 %collective-permute-done.12 = f32[2,4,56,256]{3,2,1,0:T(8,128)S(1)} collective-permute-done((f32[2,4,56,256]{3,2,1,0:T(8,128)S(1)}, f32[2,4,56,256]{3,2,1,0:T(8,128)S(1)}, u32[]{:S(2)}, u32[]{:S(2)}) %collective-permute-start.12) | collective-permute-done | bytes 458784 | tf_op jit(solution)/shard_map/ppermute | solution.py:37
  106.7 5.1 %collective-permute-done.19 = f32[4,72,256]{2,1,0:T(8,128)S(1)} collective-permute-done((f32[4,72,256]{2,1,0:T(8,128)S(1)}, f32[4,72,256]{2,1,0:T(8,128)S(1)}, u32[]{:S(2)}, u32[]{:S(2)}) %collective-permute-start.19) | collective-permute-done | bytes 294944 | tf_op jit(solution)/shard_map/ppermute | solution.py:37
  113.2 2.6 %collective-permute-done.20 = f32[2,72,256]{2,1,0:T(8,128)S(1)} collective-permute-done((f32[2,72,256]{2,1,0:T(8,128)S(1)}, f32[2,72,256]{2,1,0:T(8,128)S(1)}, u32[]{:S(2)}, u32[]{:S(2)}) %collective-permute-start.20) | collective-permute-done | bytes 147488 | tf_op jit(solution)/shard_map/ppermute | solution.py:37
  115.9 3.2 %collective-permute-start.21 = (f32[72,256]{1,0:T(8,128)S(1)}, f32[72,256]{1,0:T(8,128)S(1)}, u32[]{:S(2)}, u32[]{:S(2)}) collective-permute-start(f32[72,256]{1,0:T(8,128)S(1)} %get-tuple-element.56), channel_id=1, source_target_pairs={{0,24},{4,44},{8,48},{12,36},{16,40},{20,60},{24,0},{28,52},{32,56... | collective-permute-start | bytes 221192 | tf_op jit(solution)/shard_map/ppermute | solution.py:37
  119.3 2.9 %collective-permute-done.21.came = f32[72,256]{1,0:T(8,128)S(1)} collective-permute-done((f32[72,256]{1,0:T(8,128)S(1)}, f32[72,256]{1,0:T(8,128)S(1)}, u32[]{:S(2)}, u32[]{:S(2)}) %collective-permute-start.21) | collective-permute-done | bytes 73760 | tf_op jit(solution)/shard_map/ppermute | solution.py:37
  122.4 27.4 %all_to_all.11 = f32[256,1,4]{2,1,0:T(1,128)S(1)} all-to-all(f32[256,1,4]{2,1,0:T(1,128)S(1)} %bitcast.68), channel_id=1, replica_groups=mesh['dp_0'=4,'dp_1'=8,'dp_2'=2,'mp'=4] {'dp_0','dp_1','dp_2','mp'}, dimensions={0} | all-to-all | bytes 8192 | tf_op jit(solution)/shard_map/all_to_all | solution.py:407
  (76 shorter events, 10.2 us)
Async XLA Ops:
  0.6 87.7 %copy-start = (s32[2,64]{1,0:T(2,128)S(1)}, s32[2,64]{1,0:T(2,128)}, u32[]{:S(2)}) copy-start(s32[2,64]{1,0:T(2,128)} %param.14) | copy-start | bytes 1540
  5.1 11.6 %copy-start.4 = (f32[2,256,256]{2,1,0:T(8,128)S(1)}, f32[2,256,256]{2,1,0:T(8,128)}, u32[]{:S(2)}) copy-start(f32[2,256,256]{2,1,0:T(8,128)} %get-tuple-element.22) | copy-start | bytes 1572868
  5.1 25.9 %copy-start.8 = (s32[2,1,2]{2,1,0:T(1,128)S(1)}, s32[2,1,2]{2,1,0:T(1,128)}, u32[]{:S(2)}) copy-start(s32[2,1,2]{2,1,0:T(1,128)} %param.13) | copy-start | bytes 52
  5.1 11.6 %collective-permute-start = (f32[2,256,256]{2,1,0:T(8,128)S(1)}, f32[2,256,256]{2,1,0:T(8,128)S(1)}, u32[]{:S(2)}, u32[]{:S(2)}) collective-permute-start(f32[2,256,256]{2,1,0:T(8,128)S(1)} %get-tuple-element.24), channel_id=1, source_target_pairs={{0,1},{4,7},{1,0},{5,6},{2,3},{6,5},{3,2},{7,4},{8,9},{12,15},{9,8... | collective-permute-start | bytes 1572872 | tf_op jit(solution)/shard_map/ppermute | solution.py:37
  16.5 18.8 %copy-start.3 = (f32[2,256,256]{2,1,0:T(8,128)S(1)}, f32[2,256,256]{2,1,0:T(8,128)}, u32[]{:S(2)}) copy-start(f32[2,256,256]{2,1,0:T(8,128)} %get-tuple-element.26) | copy-start | bytes 1572868
  16.5 12.1 %collective-permute-start.5 = (f32[2,256,256]{2,1,0:T(8,128)S(1)}, f32[2,256,256]{2,1,0:T(8,128)S(1)}, u32[]{:S(2)}, u32[]{:S(2)}) collective-permute-start(f32[2,256,256]{2,1,0:T(8,128)S(1)} %get-tuple-element.27), channel_id=1, source_target_pairs={{0,1},{4,7},{1,0},{5,6},{2,3},{6,5},{3,2},{7,4},{8,9},{12,15},{9,8... | collective-permute-start | bytes 1572872 | tf_op jit(solution)/shard_map/ppermute | solution.py:37
  16.7 26.5 %copy-start.6 = (f32[2,1,2,256]{3,2,1,0:T(2,128)S(1)}, f32[2,1,2,256]{3,2,1,0:T(2,128)}, u32[]{:S(2)}) copy-start(f32[2,1,2,256]{3,2,1,0:T(2,128)} %param.11) | copy-start | bytes 12292
  16.7 26.5 %copy-start.7 = (s32[2,1,2,256]{3,2,1,0:T(2,128)S(1)}, s32[2,1,2,256]{3,2,1,0:T(2,128)}, u32[]{:S(2)}) copy-start(s32[2,1,2,256]{3,2,1,0:T(2,128)} %param.12) | copy-start | bytes 12292
  16.7 15.0 %collective-permute-start.1 = (f32[256,256]{1,0:T(8,128)S(1)}, f32[256,256]{1,0:T(8,128)}, u32[]{:S(2)}, u32[]{:S(2)}) collective-permute-start(f32[256,256]{1,0:T(8,128)S(1)} %fusion.10), channel_id=1, source_target_pairs={{0,3},{4,5},{1,2},{5,4},{2,1},{6,7},{3,0},{7,6},{8,11},{12,13},{9,... | collective-permute-start | bytes 786440 | tf_op jit(solution)/shard_map/ppermute | solution.py:37
  29.7 5.6 %collective-permute-start.6 = (f32[256,256]{1,0:T(8,128)S(1)}, f32[256,256]{1,0:T(8,128)S(1)}, u32[]{:S(2)}, u32[]{:S(2)}) collective-permute-start(f32[256,256]{1,0:T(8,128)S(1)} %fusion.7), channel_id=1, source_target_pairs={{0,3},{4,5},{1,2},{5,4},{2,1},{6,7},{3,0},{7,6},{8,11},{12,13},{9,... | collective-permute-start | bytes 786440 | tf_op jit(solution)/shard_map/ppermute | solution.py:37
  32.8 6.1 %collective-permute-start.2 = (f32[256,256]{1,0:T(8,128)S(1)}, f32[256,256]{1,0:T(8,128)S(1)}, u32[]{:S(2)}, u32[]{:S(2)}) collective-permute-start(f32[256,256]{1,0:T(8,128)S(1)} %fusion.12.r0), channel_id=1, source_target_pairs={{0,3},{4,5},{1,2},{5,4},{2,1},{6,7},{3,0},{7,6},{8,11},{12,13},{9,... | collective-permute-start | bytes 786440 | tf_op jit(solution)/shard_map/ppermute | solution.py:37
  34.3 12.8 %collective-permute-start.3 = (f32[256,256]{1,0:T(8,128)S(1)}, f32[256,256]{1,0:T(8,128)S(1)}, u32[]{:S(2)}, u32[]{:S(2)}) collective-permute-start(f32[256,256]{1,0:T(8,128)S(1)} %fusion.12.r0), channel_id=1, source_target_pairs={{0,1},{4,7},{1,0},{5,6},{2,3},{6,5},{3,2},{7,4},{8,9},{12,15},{9,8... | collective-permute-start | bytes 786440 | tf_op jit(solution)/shard_map/ppermute | solution.py:37
  38.9 8.2 %collective-permute-start.4 = (f32[256,256]{1,0:T(8,128)S(1)}, f32[256,256]{1,0:T(8,128)S(1)}, u32[]{:S(2)}, u32[]{:S(2)}) collective-permute-start(f32[256,256]{1,0:T(8,128)S(1)} %collective-permute-done.2.r1), channel_id=1, source_target_pairs={{0,1},{4,7},{1,0},{5,6},{2,3},{6,5},{3,2},{7,4},{8,9},{12,15},{9,8... | collective-permute-start | bytes 786440 | tf_op jit(solution)/shard_map/ppermute | solution.py:37
  38.9 4.4 %collective-permute-start.7 = (f32[1,256]{1,0:T(1,128)S(1)}, f32[1,256]{1,0:T(1,128)S(1)}, u32[]{:S(2)}, u32[]{:S(2)}) collective-permute-start(f32[1,256]{1,0:T(1,128)S(1)} %bitcast.69), channel_id=1, source_target_pairs={{0,3},{4,5},{1,2},{5,4},{2,1},{6,7},{3,0},{7,6},{8,11},{12,13},{9,... | collective-permute-start | bytes 3080 | tf_op jit(solution)/shard_map/ppermute | solution.py:37
  41.1 5.3 %collective-permute-start.8 = (f32[1,256]{1,0:T(1,128)S(1)}, f32[1,256]{1,0:T(1,128)S(1)}, u32[]{:S(2)}, u32[]{:S(2)}) collective-permute-start(f32[1,256]{1,0:T(1,128)S(1)} %bitcast.70), channel_id=1, source_target_pairs={{0,1},{4,7},{1,0},{5,6},{2,3},{6,5},{3,2},{7,4},{8,9},{12,15},{9,8... | collective-permute-start | bytes 3080 | tf_op jit(solution)/shard_map/ppermute | solution.py:37
  43.1 3.9 %collective-permute-start.9 = (f32[1,256]{1,0:T(1,128)S(1)}, f32[1,256]{1,0:T(1,128)S(1)}, u32[]{:S(2)}, u32[]{:S(2)}) collective-permute-start(f32[1,256]{1,0:T(1,128)S(1)} %bitcast.71), channel_id=1, source_target_pairs={{0,2},{1,3},{2,0},{3,1},{4,6},{5,7},{6,4},{7,5},{8,10},{9,11},{10,... | collective-permute-start | bytes 3080 | tf_op jit(solution)/shard_map/ppermute | solution.py:333
  43.3 28.2 %copy-start.1 = (bf16[2,1,2,256,1024]{4,3,2,1,0:T(8,128)(2,1)S(1)}, bf16[2,1,2,256,1024]{4,3,2,1,0:T(8,128)(2,1)}, u32[]{:S(2)}) copy-start(bf16[2,1,2,256,1024]{4,3,2,1,0:T(8,128)(2,1)} %param.10) | copy-start | bytes 6291460
  53.4 24.9 %collective-permute-start.10 = (f32[2,2,2,4,56,256]{5,4,3,2,1,0:T(8,128)S(1)}, f32[2,2,2,4,56,256]{5,4,3,2,1,0:T(8,128)S(1)}, u32[]{:S(2)}, u32[]{:S(2)}) collective-permute-start(f32[2,2,2,4,56,256]{5,4,3,2,1,0:T(8,128)S(1)} %get-tuple-element.29), channel_id=1, source_target_pairs={{0,4},{4,0},{1,5},{5,1},{2,6},{6,2},{3,7},{7,3},{8,12},{12,8},{9,1... | collective-permute-start | bytes 5505032 | tf_op jit(solution)/shard_map/ppermute | solution.py:366
  58.7 5.5 %collective-permute-start.13 = (f32[256,256]{1,0:T(8,128)S(1)}, f32[256,256]{1,0:T(8,128)S(1)}, u32[]{:S(2)}, u32[]{:S(2)}) collective-permute-start(f32[256,256]{1,0:T(8,128)S(1)} %fusion.9.l0), channel_id=1, source_target_pairs={{0,3},{4,5},{1,2},{5,4},{2,1},{6,7},{3,0},{7,6},{8,11},{12,13},{9,... | collective-permute-start | bytes 786440 | tf_op jit(solution)/shard_map/ppermute | solution.py:37
  59.0 9.3 %collective-permute-start.14 = (f32[256,256]{1,0:T(8,128)S(1)}, f32[256,256]{1,0:T(8,128)S(1)}, u32[]{:S(2)}, u32[]{:S(2)}) collective-permute-start(f32[256,256]{1,0:T(8,128)S(1)} %fusion.9.l0), channel_id=1, source_target_pairs={{0,1},{4,7},{1,0},{5,6},{2,3},{6,5},{3,2},{7,4},{8,9},{12,15},{9,8... | collective-permute-start | bytes 786440 | tf_op jit(solution)/shard_map/ppermute | solution.py:37
  64.2 7.2 %collective-permute-start.15 = (f32[256,256]{1,0:T(8,128)S(1)}, f32[256,256]{1,0:T(8,128)S(1)}, u32[]{:S(2)}, u32[]{:S(2)}) collective-permute-start(f32[256,256]{1,0:T(8,128)S(1)} %collective-permute-done.13.l1), channel_id=1, source_target_pairs={{0,1},{4,7},{1,0},{5,6},{2,3},{6,5},{3,2},{7,4},{8,9},{12,15},{9,8... | collective-permute-start | bytes 786440 | tf_op jit(solution)/shard_map/ppermute | solution.py:37
  74.4 7.5 %collective-permute-start.16 = (f32[2,2,2,4,16,256]{5,4,3,2,1,0:T(8,128)S(1)}, f32[2,2,2,4,16,256]{5,4,3,2,1,0:T(8,128)S(1)}, u32[]{:S(2)}, u32[]{:S(2)}) collective-permute-start(f32[2,2,2,4,16,256]{5,4,3,2,1,0:T(8,128)S(1)} %get-tuple-element.32), channel_id=1, source_target_pairs={{0,4},{4,0},{1,5},{5,1},{2,6},{6,2},{3,7},{7,3},{8,12},{12,8},{9,1... | collective-permute-start | bytes 1572872 | tf_op jit(solution)/shard_map/ppermute | solution.py:366
  78.4 3.5 %copy-start.2 = (f32[2,2,2,4,56,256]{5,4,3,2,1,0:T(8,128)}, f32[2,2,2,4,56,256]{5,4,3,2,1,0:T(8,128)S(1)}, u32[]{:S(2)}) copy-start(f32[2,2,2,4,56,256]{5,4,3,2,1,0:T(8,128)S(1)} %collective-permute-done.10) | copy-start | bytes 5505028
  79.5 14.3 %collective-permute-start.11 = (f32[2,2,4,56,256]{4,3,2,1,0:T(8,128)}, f32[2,2,4,56,256]{4,3,2,1,0:T(8,128)S(1)}, u32[]{:S(2)}, u32[]{:S(2)}) collective-permute-start(f32[2,2,4,56,256]{4,3,2,1,0:T(8,128)} %fusion), channel_id=1, source_target_pairs={{0,64},{4,196},{64,0},{68,132},{128,192},{132,68},{192,128},{196,4... | collective-permute-start | bytes 2752520 | tf_op jit(solution)/shard_map/ppermute | solution.py:37
  81.9 0.8 copy-start.5
  82.7 9.5 %collective-permute-start.17 = (f32[2,2,4,16,256]{4,3,2,1,0:T(8,128)S(1)}, f32[2,2,4,16,256]{4,3,2,1,0:T(8,128)}, u32[]{:S(2)}, u32[]{:S(2)}) collective-permute-start(f32[2,2,4,16,256]{4,3,2,1,0:T(8,128)S(1)} %fusion.4), channel_id=1, source_target_pairs={{0,8},{4,60},{8,0},{12,20},{16,24},{20,12},{24,16},{28,36},{32,40}... | collective-permute-start | bytes 786440 | tf_op jit(solution)/shard_map/ppermute | solution.py:37
  93.3 6.7 %collective-permute-start.18 = (f32[2,4,16,256]{3,2,1,0:T(8,128)S(1)}, f32[2,4,16,256]{3,2,1,0:T(8,128)S(1)}, u32[]{:S(2)}, u32[]{:S(2)}) collective-permute-start(f32[2,4,16,256]{3,2,1,0:T(8,128)S(1)} %slice_bitcast_fusion.4), channel_id=1, source_target_pairs={{0,64},{4,196},{64,0},{68,132},{128,192},{132,68},{192,128},{196,4... | collective-permute-start | bytes 393224 | tf_op jit(solution)/shard_map/ppermute | solution.py:37
  95.2 10.7 %collective-permute-start.12 = (f32[2,4,56,256]{3,2,1,0:T(8,128)S(1)}, f32[2,4,56,256]{3,2,1,0:T(8,128)S(1)}, u32[]{:S(2)}, u32[]{:S(2)}) collective-permute-start(f32[2,4,56,256]{3,2,1,0:T(8,128)S(1)} %slice_bitcast_fusion), channel_id=1, source_target_pairs={{0,8},{4,60},{8,0},{12,20},{16,24},{20,12},{24,16},{28,36},{32,40}... | collective-permute-start | bytes 1376264 | tf_op jit(solution)/shard_map/ppermute | solution.py:37
  106.1 5.7 %collective-permute-start.19 = (f32[4,72,256]{2,1,0:T(8,128)S(1)}, f32[4,72,256]{2,1,0:T(8,128)S(1)}, u32[]{:S(2)}, u32[]{:S(2)}) collective-permute-start(f32[4,72,256]{2,1,0:T(8,128)S(1)} %pad_maximum_fusion), channel_id=1, source_target_pairs={{0,192},{4,68},{64,128},{68,4},{128,64},{132,196},{192,0},{196,132... | collective-permute-start | bytes 884744 | tf_op jit(solution)/shard_map/ppermute | solution.py:37
  111.8 4.1 %collective-permute-start.20 = (f32[2,72,256]{2,1,0:T(8,128)S(1)}, f32[2,72,256]{2,1,0:T(8,128)S(1)}, u32[]{:S(2)}, u32[]{:S(2)}) collective-permute-start(f32[2,72,256]{2,1,0:T(8,128)S(1)} %slice.133), channel_id=1, source_target_pairs={{0,56},{4,12},{8,16},{12,4},{16,8},{20,28},{24,32},{28,20},{32,24}... | collective-permute-start | bytes 442376 | tf_op jit(solution)/shard_map/ppermute | solution.py:37
  115.9 6.3 %collective-permute-start.21 = (f32[72,256]{1,0:T(8,128)S(1)}, f32[72,256]{1,0:T(8,128)S(1)}, u32[]{:S(2)}, u32[]{:S(2)}) collective-permute-start(f32[72,256]{1,0:T(8,128)S(1)} %get-tuple-element.56), channel_id=1, source_target_pairs={{0,24},{4,44},{8,48},{12,36},{16,40},{20,60},{24,0},{28,52},{32,56... | collective-permute-start | bytes 221192 | tf_op jit(solution)/shard_map/ppermute | solution.py:37

commit v2 on v1

--- a/solution.py
+++ b/solution.py
@@ -15,7 +15,7 @@
 DP = (X, Z, C)
 MP_DP = (Y, X, Z, C)
 BETA = 0.1
-GRANT_FORWARD, GRANT_BACKWARD = 53, 48
+GRANT_A, GRANT_B = 48, 12
 
 
 def first(i, c, n):
@@ -170,50 +170,8 @@
     arrange(info, part, blocks, (keep, send))
 
 
-def product_kernel(order, value, weights, send, keep, held, factors, arrived):
-    seq = send.shape[1]
-    own = pltpu.make_async_copy(weights, factors, arrived.at[4])
-    own.start()
-    copies = []
-    for i in range(4):
-        at = pl.ds(pl.multiple_of(order[(i + 2) % 4] * seq, seq), seq)
-        copies.append((at, pltpu.make_async_copy(value.at[at], held.at[at], arrived.at[i])))
-        copies[i][1].start()
-    own.wait()
-    for i, (at, copy) in enumerate(copies):
-        copy.wait()
-        out = send if i < 2 else keep
-        out[i % 2] = jnp.dot(held[at], factors[...], preferred_element_type=jnp.float32)
-
-
-def product(order, value, weights, seq):
-    wide, rank = weights.shape
-    half = jax.ShapeDtypeStruct((2, seq, rank), jnp.float32)
-    return pl.pallas_call(
-        product_kernel,
-        in_specs=[
-            pl.BlockSpec(memory_space=pltpu.SMEM),
-            pl.BlockSpec(memory_space=pltpu.HBM),
-            pl.BlockSpec(memory_space=pltpu.HBM),
-        ],
-        out_specs=[pl.BlockSpec(memory_space=pltpu.VMEM)] * 2,
-        scratch_shapes=[
-            pltpu.VMEM(value.shape, value.dtype),
-            pltpu.VMEM(weights.shape, weights.dtype),
-            pltpu.SemaphoreType.DMA((5,)),
-        ],
-        out_shape=[half, half],
-        compiler_params=pltpu.CompilerParams(vmem_limit_bytes=GRANT_FORWARD * 2**20),
-        cost_estimate=pl.CostEstimate(
-            flops=8 * seq * wide * rank,
-            bytes_accessed=8 * seq * wide + 2 * wide * rank + 16 * seq * rank,
-            transcendentals=0,
-        ),
-    )(order, value, weights)
-
-
-def pack_kernel(kept, came, base, shard, small):
-    total = kept[...] + came[...]
+def pack_kernel(kept, other, far, across, base, shard, small):
+    total = kept[...] + other[...] + far[...] + across[...]
     shard[...] = total
     column = lax.broadcasted_iota(jnp.int32, small.shape, 1)
     squares = jnp.sum(jnp.sum(total * total, axis=0, keepdims=True), axis=1, keepdims=True)
@@ -275,7 +233,7 @@
         out_shape=[shape for shape, _ in outs],
         compiler_params=pltpu.CompilerParams(
             dimension_semantics=("arbitrary",),
-            vmem_limit_bytes=(GRANT_BACKWARD if by_hand else 24) * 2**20,
+            vmem_limit_bytes=(GRANT_A if by_hand else GRANT_B) * 2**20,
         ),
         cost_estimate=pl.CostEstimate(
             flops=2 * tokens * wide * rank,
@@ -309,11 +267,18 @@
     hidden = hidden_activation.reshape(tokens, ff)
     rows = target_head_rows.reshape(tokens, width)
     near, far, mine, late = order_of_four(y, c)
-    order = jnp.stack([mine, late, near, far]).astype(jnp.int32)
-
-    readout_send, readout_keep = product(order, rows, adapter_down_second, seq)
-    readout_send, hidden_next = lax.optimization_barrier((readout_send, hidden))
-    latent_send, latent_keep = product(order, hidden_next, adapter_down_first, seq)
+
+    def product(value, weights):
+        return jnp.dot(value, weights, preferred_element_type=jnp.float32).reshape(ways, seq, rank)
+
+    block = lambda part, i: lax.dynamic_index_in_dim(part, i, 0, keepdims=False)
+    stacked = lambda part: jnp.stack([block(part, near), block(part, far)])
+    readout_part = product(rows, adapter_down_second)
+    readout_send, hidden_next = lax.optimization_barrier((stacked(readout_part), hidden))
+    latent_part = product(hidden_next, adapter_down_first)
+    latent_send = stacked(latent_part)
+    readout_keep = [block(readout_part, mine), block(readout_part, late)]
+    latent_keep = [block(latent_part, mine), block(latent_part, late)]
 
     def own_sum(send, keep):
         came = swap(send, Y, first)
@@ -330,7 +295,10 @@
     readouts = spread(readout)
     shift = (jnp.sum(latent * readout, axis=-1) / root)[None]
     opposite = [(i, (i + 2) % 4) for i in range(4)]
-    shifts = (shift, swap(shift, Y, second), swap(shift, Y, first), lax.ppermute(shift, Y, opposite))
+    shift_other = swap(shift, Y, second)
+    shift_beside = swap(shift, Y, first)
+    shift_far = lax.ppermute(shift, Y, opposite)
+    shifts = (shift, shift_other, shift_beside, shift_far)
     latents = spread(latent)
 
     entry = jnp.asarray(table())[place * ways + y]
@@ -388,8 +356,10 @@
     w = w[1] + swap(w[0], X, first)
     both = lambda i: jnp.concatenate([p[i], w[i]], axis=-2)
     shard = both(0) + swap(both(1), X, second)
-    shard = shard[:2] + swap(shard[2:], Z, second)
-    kept, came = shard[0], swap(shard[1], Z, third)
+    across = lambda i, c, n: third(second(i, c, n), c, n)
+    parts = (shard[0],) + tuple(
+        swap(shard[k], Z, partner) for k, partner in ((3, across), (1, third), (2, second))
+    )
 
     target = lax.dynamic_index_in_dim(pair_destination, place, 1, keepdims=False)
     hits = jnp.arange(pairs)[:, None] == target[None, :]
@@ -402,8 +372,8 @@
     little = pltpu.CompilerParams(vmem_limit_bytes=4 * 2**20)
     f32 = lambda *shape: jax.ShapeDtypeStruct(shape, jnp.float32)
     shard, small = pl.pallas_call(
-        pack_kernel, out_shape=[f32(*kept.shape), f32(*base.shape)], compiler_params=little
-    )(kept, came, base)
+        pack_kernel, out_shape=[f32(*parts[0].shape), f32(*base.shape)], compiler_params=little
+    )(*parts, base)
     small = lax.all_to_all(small, (X, Z, C, Y), 0, 0, tiled=True)
     grad_a, grad_b, pair_margin, mean_loss = pl.pallas_call(
         functools.partial(scale_kernel, (ff + width) * ways * rank),

time: 152 us -> 146 us (0.961)
  Pallas kernels: 22.2 us -> 10.2 us
  matrix products: 0 us -> 7.64 us
  blocking collectives: 27.4 us -> 22.6 us
  other arithmetic: 7.77 us -> 11.8 us
    pallas_call x3 -> x1, Pallas kernels: 12.2 us -> 0.12 us  [per_device(): pl.pallas_call(pack_kernel, out_shape=[f32(*parts[0].shape), f32(*base.sh...]
    dot_general x0 -> x2, matrix products: none -> 7.64 us  [product(): jnp.dot(value, weights, preferred_element_type=jnp.float32)]
    all_to_all x1, blocking collectives: 27.4 us -> 22.6 us  [per_device(): small = lax.all_to_all(small, (X, Z, C, Y), 0, 0, tiled=True)]
    add x2, other arithmetic: 1.03 us -> 2.74 us  [own_sum(): relayed = swap(keep[1] + came[1], Y, second)]
    ppermute x19 -> x20, waiting for transfers between devices: 46.4 us -> 45.9 us  [swap(): return lax.ppermute(value, axes, pairs)]
    ppermute x19 -> x20, starting transfers between devices: 32.6 us -> 32.9 us  [swap(): return lax.ppermute(value, axes, pairs)]
  transfers between devices with their start and end apart: 22 -> 23, of which waited for: 13 -> 15; matrix products, arithmetic and copies ran while one was open for 6% -> 13% of each run, Pallas kernels for 7% -> 2%
where the time goes in v2:
time: 146 us
  waiting for transfers between devices  47 us (32%)
  starting transfers between devices  41.3 us (28%)
  blocking collectives  22.6 us (15%)
  other arithmetic  11.8 us (8%)
  Pallas kernels  10.2 us (7%)
  matrix products  7.64 us (5%)
  local copies, waits for them, and re-layouts  3.42 us (2%)
  between operations  1.59 us (1%)
    ppermute x20, waiting for transfers between devices, swap(): return lax.ppermute(value, axes, pairs)  45.9 us
    ppermute x20, starting transfers between devices, swap(): return lax.ppermute(value, axes, pairs)  32.9 us
    all_to_all x1, blocking collectives, per_device(): small = lax.all_to_all(small, (X, Z, C, Y), 0, 0, tiled=True)  22.6 us
    pallas_call x2, Pallas kernels, kernel_call(): pl.pallas_call(body, grid_spec=pltpu.PrefetchScalarGridSpec(num_scalar_pr...  9.3 us
    ppermute x2, starting transfers between devices, per_device(): core = lambda value: lax.ppermute(value, C, [(0, 1), (1, 0)])  7.83 us
    dot_general x2, matrix products, product(): jnp.dot(value, weights, preferred_element_type=jnp.float32)  7.64 us
  transfers between devices with their start and end apart: 23, of which 15 were waited for; matrix products, arithmetic and copies ran while one was open for 13% of the time, Pallas kernels for 2%

profile of v2, /device:TPU:1, one launch (start us, length us, event | category | flops | bytes accessed | tf_op | source)
XLA Modules:
  0.0 145.6 jit_solution(362216956057900282)
XLA Ops:
  0.7 2.5 %fusion.3 = f32[4,256,256]{2,1,0:T(8,128)S(1)} fusion(bf16[4,256,1024]{2,1,0:T(8,128)(2,1)} %bitcast.72, bf16[1024,256]{1,0:T(8,128)(2,1)} %param.16), kind=kOutput, calls=%fused_computation.7 | convolution fusion | flops 536870912 | bytes 3670016 | tf_op jit(solution)/shard_map/dot_general | solution.py:272
  3.3 3.6 %collective-permute-start = (f32[2,256,256]{2,1,0:T(8,128)S(1)}, f32[2,256,256]{2,1,0:T(8,128)}, u32[]{:S(2)}, u32[]{:S(2)}) collective-permute-start(f32[2,256,256]{2,1,0:T(8,128)S(1)} %pad_maximum_fusion), channel_id=1, source_target_pairs={{0,1},{4,7},{1,0},{5,6},{2,3},{6,5},{3,2},{7,4},{8,9},{12,15},{9,8... | collective-permute-start | bytes 1572872 | tf_op jit(solution)/shard_map/ppermute | solution.py:37
  6.9 5.1 %fusion.19 = f32[1024,256]{1,0:T(8,128)S(1)} fusion(bf16[1024,3584]{1,0:T(8,128)(2,1)} %bitcast.81, bf16[3584,256]{1,0:T(8,128)(2,1)S(1)} %copy-done), kind=kOutput, calls=%fused_computation.58 | convolution fusion | flops 1879048192 | bytes 10223616 | tf_op jit(solution)/shard_map/dot_general | solution.py:272
  15.0 9.7 %collective-permute-done.5 = f32[2,256,256]{2,1,0:T(8,128)} collective-permute-done((f32[2,256,256]{2,1,0:T(8,128)}, f32[2,256,256]{2,1,0:T(8,128)}, u32[]{:S(2)}, u32[]{:S(2)}) %collective-permute-start.5) | collective-permute-done | bytes 524320 | tf_op jit(solution)/shard_map/ppermute | solution.py:37
  24.8 1.8 %fusion.9 = f32[256,256]{1,0:T(8,128)} fusion(f32[2,256,256]{2,1,0:T(8,128)} %collective-permute-done.5, f32[4,256,256]{2,1,0:T(8,128)} %bitcast.84, s32[]{:T(128)S(6)} %select_n.61), kind=kLoop, calls=%fused_computation.20 | loop fusion | flops 65536 | bytes 786436 | tf_op jit(solution)/shard_map/add | solution.py:285
  28.5 1.1 fusion.14.r0
  29.7 1.5 %collective-permute-start.2 = (f32[256,256]{1,0:T(8,128)S(1)}, f32[256,256]{1,0:T(8,128)S(1)}, u32[]{:S(2)}, u32[]{:S(2)}) collective-permute-start(f32[256,256]{1,0:T(8,128)S(1)} %fusion.14.r0), channel_id=1, source_target_pairs={{0,3},{4,5},{1,2},{5,4},{2,1},{6,7},{3,0},{7,6},{8,11},{12,13},{9,... | collective-permute-start | bytes 786440 | tf_op jit(solution)/shard_map/ppermute | solution.py:37
  33.5 2.1 %collective-permute-done.2.r1 = f32[256,256]{1,0:T(8,128)S(1)} collective-permute-done((f32[256,256]{1,0:T(8,128)S(1)}, f32[256,256]{1,0:T(8,128)S(1)}, u32[]{:S(2)}, u32[]{:S(2)}) %collective-permute-start.2) | collective-permute-done | bytes 262176 | tf_op jit(solution)/shard_map/ppermute | solution.py:37
  35.6 3.9 %collective-permute-start.4 = (f32[256,256]{1,0:T(8,128)S(1)}, f32[256,256]{1,0:T(8,128)S(1)}, u32[]{:S(2)}, u32[]{:S(2)}) collective-permute-start(f32[256,256]{1,0:T(8,128)S(1)} %collective-permute-done.2.r1), channel_id=1, source_target_pairs={{0,1},{4,7},{1,0},{5,6},{2,3},{6,5},{3,2},{7,4},{8,9},{12,15},{9,8... | collective-permute-start | bytes 786440 | tf_op jit(solution)/shard_map/ppermute | solution.py:37
  40.1 2.1 %collective-permute-start.8 = (f32[1,256]{1,0:T(1,128)S(1)}, f32[1,256]{1,0:T(1,128)S(1)}, u32[]{:S(2)}, u32[]{:S(2)}) collective-permute-start(f32[1,256]{1,0:T(1,128)S(1)} %bitcast.78), channel_id=1, source_target_pairs={{0,1},{4,7},{1,0},{5,6},{2,3},{6,5},{3,2},{7,4},{8,9},{12,15},{9,8... | collective-permute-start | bytes 3080 | tf_op jit(solution)/shard_map/ppermute | solution.py:37
  42.3 1.1 collective-permute-done.9.s3
  43.7 1.2 collective-permute-done.7.s1
  44.9 6.4 %shard_map.120 = (f32[2,2,2,4,56,256]{5,4,3,2,1,0:T(8,128)S(1)}, f32[2,2,2,4,56,256]{5,4,3,2,1,0:T(8,128)S(1)}, f32[8,128]{1,0:T(8,128)S(1)}, f32[256,8]{1,0:T(8,128)S(1)}) custom-call(s32[40]{0:T(128)S(1)} %pad_add_fusion.info, f32[256,256]{1,0:T(8,128)S(1)} %fusion.14.r0, f32[256,256]{1,0:T(8,128)S(1)} %collective-permute-done.2.r1, ...), custom_call_target="tpu_custom_call" | custom-call | flops 1879048192 | bytes 11010048 | tf_op jit(solution)/shard_map/pallas_call | solution.py:219
  51.3 3.9 %collective-permute-start.10 = (f32[2,2,2,4,56,256]{5,4,3,2,1,0:T(8,128)S(1)}, f32[2,2,2,4,56,256]{5,4,3,2,1,0:T(8,128)S(1)}, u32[]{:S(2)}, u32[]{:S(2)}) collective-permute-start(f32[2,2,2,4,56,256]{5,4,3,2,1,0:T(8,128)S(1)} %get-tuple-element.21), channel_id=1, source_target_pairs={{0,4},{4,0},{1,5},{5,1},{2,6},{6,2},{3,7},{7,3},{8,12},{12,8},{9,1... | collective-permute-start | bytes 5505032 | tf_op jit(solution)/shard_map/ppermute | solution.py:334
  56.6 5.1 %collective-permute-done.13.l1 = f32[256,256]{1,0:T(8,128)S(1)} collective-permute-done((f32[256,256]{1,0:T(8,128)S(1)}, f32[256,256]{1,0:T(8,128)S(1)}, u32[]{:S(2)}, u32[]{:S(2)}) %collective-permute-start.13) | collective-permute-done | bytes 262176 | tf_op jit(solution)/shard_map/ppermute | solution.py:37
  61.8 3.4 %collective-permute-done.14.l2 = f32[256,256]{1,0:T(8,128)S(1)} collective-permute-done((f32[256,256]{1,0:T(8,128)S(1)}, f32[256,256]{1,0:T(8,128)S(1)}, u32[]{:S(2)}, u32[]{:S(2)}) %collective-permute-start.14) | collective-permute-done | bytes 262176 | tf_op jit(solution)/shard_map/ppermute | solution.py:37
  65.2 2.9 %collective-permute-done.15.l3 = f32[256,256]{1,0:T(8,128)S(1)} collective-permute-done((f32[256,256]{1,0:T(8,128)S(1)}, f32[256,256]{1,0:T(8,128)S(1)}, u32[]{:S(2)}, u32[]{:S(2)}) %collective-permute-start.15) | collective-permute-done | bytes 262176 | tf_op jit(solution)/shard_map/ppermute | solution.py:37
  68.2 2.9 %shard_map.121 = (f32[2,2,2,4,16,256]{5,4,3,2,1,0:T(8,128)S(1)}, f32[2,2,2,4,16,256]{5,4,3,2,1,0:T(8,128)S(1)}) custom-call(s32[40]{0:T(128)S(1)} %pad_add_fusion.info, f32[256,256]{1,0:T(8,128)S(1)} %fusion.11.l0, f32[256,256]{1,0:T(8,128)S(1)} %collective-permute-done.13.l1, f32[256,256]{1,0:T(8,128)S(1)} %collective-permute-done.14.l2, ...), custom_call_target="tpu_custom_call" | custom-call | flops 536870912 | bytes 3145728 | tf_op jit(solution)/shard_map/pallas_call | solution.py:219
  71.1 3.9 %collective-permute-start.16 = (f32[2,2,2,4,16,256]{5,4,3,2,1,0:T(8,128)S(1)}, f32[2,2,2,4,16,256]{5,4,3,2,1,0:T(8,128)S(1)}, u32[]{:S(2)}, u32[]{:S(2)}) collective-permute-start(f32[2,2,2,4,16,256]{5,4,3,2,1,0:T(8,128)S(1)} %get-tuple-element.24), channel_id=1, source_target_pairs={{0,4},{4,0},{1,5},{5,1},{2,6},{6,2},{3,7},{7,3},{8,12},{12,8},{9,1... | collective-permute-start | bytes 1572872 | tf_op jit(solution)/shard_map/ppermute | solution.py:334
  75.1 1.2 fusion
  76.2 2.5 %collective-permute-start.11 = (f32[2,2,4,56,256]{4,3,2,1,0:T(8,128)}, f32[2,2,4,56,256]{4,3,2,1,0:T(8,128)S(1)}, u32[]{:S(2)}, u32[]{:S(2)}) collective-permute-start(f32[2,2,4,56,256]{4,3,2,1,0:T(8,128)} %fusion), channel_id=1, source_target_pairs={{0,64},{4,196},{64,0},{68,132},{128,192},{132,68},{192,128},{196,4... | collective-permute-start | bytes 2752520 | tf_op jit(solution)/shard_map/ppermute | solution.py:37
  79.6 5.7 %collective-permute-start.17 = (f32[2,2,4,16,256]{4,3,2,1,0:T(8,128)S(1)}, f32[2,2,4,16,256]{4,3,2,1,0:T(8,128)}, u32[]{:S(2)}, u32[]{:S(2)}) collective-permute-start(f32[2,2,4,16,256]{4,3,2,1,0:T(8,128)S(1)} %fusion.6), channel_id=1, source_target_pairs={{0,8},{4,60},{8,0},{12,20},{16,24},{20,12},{24,16},{28,36},{32,40}... | collective-permute-start | bytes 786440 | tf_op jit(solution)/shard_map/ppermute | solution.py:37
  86.8 2.3 %collective-permute-done.17 = f32[2,2,4,16,256]{4,3,2,1,0:T(8,128)} collective-permute-done((f32[2,2,4,16,256]{4,3,2,1,0:T(8,128)S(1)}, f32[2,2,4,16,256]{4,3,2,1,0:T(8,128)}, u32[]{:S(2)}, u32[]{:S(2)}) %collective-permute-start.17) | collective-permute-done | bytes 262176 | tf_op jit(solution)/shard_map/ppermute | solution.py:37
  89.1 1.1 fusion.8
  90.7 1.6 %fusion.2 = f32[2,2,4,56,256]{4,3,2,1,0:T(8,128)S(1)} fusion(f32[2,2,4,56,256]{4,3,2,1,0:T(8,128)S(1)} %collective-permute-done.11, f32[2,2,2,4,56,256]{5,4,3,2,1,0:T(8,128)} %copy-done.3, f32[2,2,2,4,56,256]{5,4,3,2,1,0:T(8,128)} %copy-done.2), kind=kLoop, calls=%fused_computation.4 | loop fusion | flops 458752 | bytes 3670016 | tf_op jit(solution)/shard_map/add | solution.py:353
  92.4 4.8 %collective-permute-start.12 = (f32[2,4,56,256]{3,2,1,0:T(8,128)S(1)}, f32[2,4,56,256]{3,2,1,0:T(8,128)S(1)}, u32[]{:S(2)}, u32[]{:S(2)}) collective-permute-start(f32[2,4,56,256]{3,2,1,0:T(8,128)S(1)} %slice_bitcast_fusion), channel_id=1, source_target_pairs={{0,8},{4,60},{8,0},{12,20},{16,24},{20,12},{24,16},{28,36},{32,40}... | collective-permute-start | bytes 1376264 | tf_op jit(solution)/shard_map/ppermute | solution.py:37
  97.3 5.8 %collective-permute-done.12 = f32[2,4,56,256]{3,2,1,0:T(8,128)S(1)} collective-permute-done((f32[2,4,56,256]{3,2,1,0:T(8,128)S(1)}, f32[2,4,56,256]{3,2,1,0:T(8,128)S(1)}, u32[]{:S(2)}, u32[]{:S(2)}) %collective-permute-start.12) | collective-permute-done | bytes 458784 | tf_op jit(solution)/shard_map/ppermute | solution.py:37
  103.8 5.1 %collective-permute-done.19 = f32[4,72,256]{2,1,0:T(8,128)S(1)} collective-permute-done((f32[4,72,256]{2,1,0:T(8,128)S(1)}, f32[4,72,256]{2,1,0:T(8,128)S(1)}, u32[]{:S(2)}, u32[]{:S(2)}) %collective-permute-start.19) | collective-permute-done | bytes 294944 | tf_op jit(solution)/shard_map/ppermute | solution.py:37
  109.1 4.6 %collective-permute-start.21 = (f32[72,256]{1,0:T(8,128)S(1)}, f32[72,256]{1,0:T(8,128)S(1)}, u32[]{:S(2)}, u32[]{:S(2)}) collective-permute-start(f32[72,256]{1,0:T(8,128)S(1)} %get-tuple-element.53), channel_id=1, source_target_pairs={{0,24},{4,44},{8,48},{12,36},{16,40},{20,60},{24,0},{28,52},{32,56... | collective-permute-start | bytes 221192 | tf_op jit(solution)/shard_map/ppermute | solution.py:37
  114.9 1.9 %collective-permute-done.21.far = f32[72,256]{1,0:T(8,128)S(1)} collective-permute-done((f32[72,256]{1,0:T(8,128)S(1)}, f32[72,256]{1,0:T(8,128)S(1)}, u32[]{:S(2)}, u32[]{:S(2)}) %collective-permute-start.21) | collective-permute-done | bytes 73760 | tf_op jit(solution)/shard_map/ppermute | solution.py:37
  116.8 4.7 %collective-permute-done.20.other = f32[72,256]{1,0:T(8,128)S(1)} collective-permute-done((f32[72,256]{1,0:T(8,128)S(1)}, f32[72,256]{1,0:T(8,128)S(1)}, u32[]{:S(2)}, u32[]{:S(2)}) %collective-permute-start.20) | collective-permute-done | bytes 73760 | tf_op jit(solution)/shard_map/ppermute | solution.py:37
  121.7 22.6 %all_to_all.11 = f32[256,1,4]{2,1,0:T(1,128)S(1)} all-to-all(f32[256,1,4]{2,1,0:T(1,128)S(1)} %bitcast.76), channel_id=1, replica_groups=mesh['dp_0'=4,'dp_1'=8,'dp_2'=2,'mp'=4] {'dp_0','dp_1','dp_2','mp'}, dimensions={0} | all-to-all | bytes 8192 | tf_op jit(solution)/shard_map/all_to_all | solution.py:377
  (81 shorter events, 15.9 us)
Async XLA Ops:
  0.6 6.3 %copy-start = (bf16[3584,256]{1,0:T(8,128)(2,1)S(1)}, bf16[3584,256]{1,0:T(8,128)(2,1)}, u32[]{:S(2)}) copy-start(bf16[3584,256]{1,0:T(8,128)(2,1)} %param.15) | copy-start | bytes 5505028
  3.3 10.3 %collective-permute-start = (f32[2,256,256]{2,1,0:T(8,128)S(1)}, f32[2,256,256]{2,1,0:T(8,128)}, u32[]{:S(2)}, u32[]{:S(2)}) collective-permute-start(f32[2,256,256]{2,1,0:T(8,128)S(1)} %pad_maximum_fusion), channel_id=1, source_target_pairs={{0,1},{4,7},{1,0},{5,6},{2,3},{6,5},{3,2},{7,4},{8,9},{12,15},{9,8... | collective-permute-start | bytes 1572872 | tf_op jit(solution)/shard_map/ppermute | solution.py:37
  12.1 1.2 copy-start.4
  12.1 15.7 %copy-start.8 = (s32[2,1,2]{2,1,0:T(1,128)S(1)}, s32[2,1,2]{2,1,0:T(1,128)}, u32[]{:S(2)}) copy-start(s32[2,1,2]{2,1,0:T(1,128)} %param.13) | copy-start | bytes 52
  13.3 11.5 %collective-permute-start.5 = (f32[2,256,256]{2,1,0:T(8,128)}, f32[2,256,256]{2,1,0:T(8,128)}, u32[]{:S(2)}, u32[]{:S(2)}) collective-permute-start(f32[2,256,256]{2,1,0:T(8,128)} %pad_maximum_fusion.1), channel_id=1, source_target_pairs={{0,1},{4,7},{1,0},{5,6},{2,3},{6,5},{3,2},{7,4},{8,9},{12,15},{9,8... | collective-permute-start | bytes 1572872 | tf_op jit(solution)/shard_map/ppermute | solution.py:37
  14.6 27.6 %copy-start.6 = (f32[2,1,2,256]{3,2,1,0:T(2,128)S(1)}, f32[2,1,2,256]{3,2,1,0:T(2,128)}, u32[]{:S(2)}) copy-start(f32[2,1,2,256]{3,2,1,0:T(2,128)} %param.11) | copy-start | bytes 12292
  14.6 27.6 %copy-start.7 = (s32[2,1,2,256]{3,2,1,0:T(2,128)S(1)}, s32[2,1,2,256]{3,2,1,0:T(2,128)}, u32[]{:S(2)}) copy-start(s32[2,1,2,256]{3,2,1,0:T(2,128)} %param.12) | copy-start | bytes 12292
  14.6 13.9 %collective-permute-start.1 = (f32[256,256]{1,0:T(8,128)S(1)}, f32[256,256]{1,0:T(8,128)}, u32[]{:S(2)}, u32[]{:S(2)}) collective-permute-start(f32[256,256]{1,0:T(8,128)S(1)} %fusion.12), channel_id=1, source_target_pairs={{0,3},{4,5},{1,2},{5,4},{2,1},{6,7},{3,0},{7,6},{8,11},{12,13},{9,... | collective-permute-start | bytes 786440 | tf_op jit(solution)/shard_map/ppermute | solution.py:37
  26.5 5.7 %collective-permute-start.6 = (f32[256,256]{1,0:T(8,128)}, f32[256,256]{1,0:T(8,128)S(1)}, u32[]{:S(2)}, u32[]{:S(2)}) collective-permute-start(f32[256,256]{1,0:T(8,128)} %fusion.9), channel_id=1, source_target_pairs={{0,3},{4,5},{1,2},{5,4},{2,1},{6,7},{3,0},{7,6},{8,11},{12,13},{9,... | collective-permute-start | bytes 786440 | tf_op jit(solution)/shard_map/ppermute | solution.py:37
  29.6 15.3 %collective-permute-start.3 = (f32[256,256]{1,0:T(8,128)S(1)}, f32[256,256]{1,0:T(8,128)S(1)}, u32[]{:S(2)}, u32[]{:S(2)}) collective-permute-start(f32[256,256]{1,0:T(8,128)S(1)} %fusion.14.r0), channel_id=1, source_target_pairs={{0,1},{4,7},{1,0},{5,6},{2,3},{6,5},{3,2},{7,4},{8,9},{12,15},{9,8... | collective-permute-start | bytes 786440 | tf_op jit(solution)/shard_map/ppermute | solution.py:37
  29.7 5.9 %collective-permute-start.2 = (f32[256,256]{1,0:T(8,128)S(1)}, f32[256,256]{1,0:T(8,128)S(1)}, u32[]{:S(2)}, u32[]{:S(2)}) collective-permute-start(f32[256,256]{1,0:T(8,128)S(1)} %fusion.14.r0), channel_id=1, source_target_pairs={{0,3},{4,5},{1,2},{5,4},{2,1},{6,7},{3,0},{7,6},{8,11},{12,13},{9,... | collective-permute-start | bytes 786440 | tf_op jit(solution)/shard_map/ppermute | solution.py:37
  35.6 9.3 %collective-permute-start.4 = (f32[256,256]{1,0:T(8,128)S(1)}, f32[256,256]{1,0:T(8,128)S(1)}, u32[]{:S(2)}, u32[]{:S(2)}) collective-permute-start(f32[256,256]{1,0:T(8,128)S(1)} %collective-permute-done.2.r1), channel_id=1, source_target_pairs={{0,1},{4,7},{1,0},{5,6},{2,3},{6,5},{3,2},{7,4},{8,9},{12,15},{9,8... | collective-permute-start | bytes 786440 | tf_op jit(solution)/shard_map/ppermute | solution.py:37
  39.5 3.9 %collective-permute-start.9 = (f32[1,256]{1,0:T(1,128)S(1)}, f32[1,256]{1,0:T(1,128)S(1)}, u32[]{:S(2)}, u32[]{:S(2)}) collective-permute-start(f32[1,256]{1,0:T(1,128)S(1)} %bitcast.77), channel_id=1, source_target_pairs={{0,2},{1,3},{2,0},{3,1},{4,6},{5,7},{6,4},{7,5},{8,10},{9,11},{10,... | collective-permute-start | bytes 3080 | tf_op jit(solution)/shard_map/ppermute | solution.py:300
  40.1 3.6 %collective-permute-start.8 = (f32[1,256]{1,0:T(1,128)S(1)}, f32[1,256]{1,0:T(1,128)S(1)}, u32[]{:S(2)}, u32[]{:S(2)}) collective-permute-start(f32[1,256]{1,0:T(1,128)S(1)} %bitcast.78), channel_id=1, source_target_pairs={{0,1},{4,7},{1,0},{5,6},{2,3},{6,5},{3,2},{7,4},{8,9},{12,15},{9,8... | collective-permute-start | bytes 3080 | tf_op jit(solution)/shard_map/ppermute | solution.py:37
  42.2 2.7 %collective-permute-start.7 = (f32[1,256]{1,0:T(1,128)S(1)}, f32[1,256]{1,0:T(1,128)S(1)}, u32[]{:S(2)}, u32[]{:S(2)}) collective-permute-start(f32[1,256]{1,0:T(1,128)S(1)} %bitcast.79), channel_id=1, source_target_pairs={{0,3},{4,5},{1,2},{5,4},{2,1},{6,7},{3,0},{7,6},{8,11},{12,13},{9,... | collective-permute-start | bytes 3080 | tf_op jit(solution)/shard_map/ppermute | solution.py:37
  42.3 25.9 %copy-start.1 = (bf16[2,1,2,256,1024]{4,3,2,1,0:T(8,128)(2,1)S(1)}, bf16[2,1,2,256,1024]{4,3,2,1,0:T(8,128)(2,1)}, u32[]{:S(2)}) copy-start(bf16[2,1,2,256,1024]{4,3,2,1,0:T(8,128)(2,1)} %param.10) | copy-start | bytes 6291460
  51.3 25.0 %copy-start.2 = (f32[2,2,2,4,56,256]{5,4,3,2,1,0:T(8,128)}, f32[2,2,2,4,56,256]{5,4,3,2,1,0:T(8,128)S(1)}, u32[]{:S(2)}) copy-start(f32[2,2,2,4,56,256]{5,4,3,2,1,0:T(8,128)S(1)} %get-tuple-element.20) | copy-start | bytes 5505028
  51.3 23.8 %collective-permute-start.10 = (f32[2,2,2,4,56,256]{5,4,3,2,1,0:T(8,128)S(1)}, f32[2,2,2,4,56,256]{5,4,3,2,1,0:T(8,128)S(1)}, u32[]{:S(2)}, u32[]{:S(2)}) collective-permute-start(f32[2,2,2,4,56,256]{5,4,3,2,1,0:T(8,128)S(1)} %get-tuple-element.21), channel_id=1, source_target_pairs={{0,4},{4,0},{1,5},{5,1},{2,6},{6,2},{3,7},{7,3},{8,12},{12,8},{9,1... | collective-permute-start | bytes 5505032 | tf_op jit(solution)/shard_map/ppermute | solution.py:334
  55.2 6.6 %collective-permute-start.13 = (f32[256,256]{1,0:T(8,128)S(1)}, f32[256,256]{1,0:T(8,128)S(1)}, u32[]{:S(2)}, u32[]{:S(2)}) collective-permute-start(f32[256,256]{1,0:T(8,128)S(1)} %fusion.11.l0), channel_id=1, source_target_pairs={{0,3},{4,5},{1,2},{5,4},{2,1},{6,7},{3,0},{7,6},{8,11},{12,13},{9,... | collective-permute-start | bytes 786440 | tf_op jit(solution)/shard_map/ppermute | solution.py:37
  55.7 9.5 %collective-permute-start.14 = (f32[256,256]{1,0:T(8,128)S(1)}, f32[256,256]{1,0:T(8,128)S(1)}, u32[]{:S(2)}, u32[]{:S(2)}) collective-permute-start(f32[256,256]{1,0:T(8,128)S(1)} %fusion.11.l0), channel_id=1, source_target_pairs={{0,1},{4,7},{1,0},{5,6},{2,3},{6,5},{3,2},{7,4},{8,9},{12,15},{9,8... | collective-permute-start | bytes 786440 | tf_op jit(solution)/shard_map/ppermute | solution.py:37
  61.7 6.4 %collective-permute-start.15 = (f32[256,256]{1,0:T(8,128)S(1)}, f32[256,256]{1,0:T(8,128)S(1)}, u32[]{:S(2)}, u32[]{:S(2)}) collective-permute-start(f32[256,256]{1,0:T(8,128)S(1)} %collective-permute-done.13.l1), channel_id=1, source_target_pairs={{0,1},{4,7},{1,0},{5,6},{2,3},{6,5},{3,2},{7,4},{8,9},{12,15},{9,8... | collective-permute-start | bytes 786440 | tf_op jit(solution)/shard_map/ppermute | solution.py:37
  71.1 14.1 %copy-start.9 = (s32[2,64]{1,0:T(2,128)S(1)}, s32[2,64]{1,0:T(2,128)}, u32[]{:S(2)}) copy-start(s32[2,64]{1,0:T(2,128)} %param.14) | copy-start | bytes 1540
  71.1 7.6 %collective-permute-start.16 = (f32[2,2,2,4,16,256]{5,4,3,2,1,0:T(8,128)S(1)}, f32[2,2,2,4,16,256]{5,4,3,2,1,0:T(8,128)S(1)}, u32[]{:S(2)}, u32[]{:S(2)}) collective-permute-start(f32[2,2,2,4,16,256]{5,4,3,2,1,0:T(8,128)S(1)} %get-tuple-element.24), channel_id=1, source_target_pairs={{0,4},{4,0},{1,5},{5,1},{2,6},{6,2},{3,7},{7,3},{8,12},{12,8},{9,1... | collective-permute-start | bytes 1572872 | tf_op jit(solution)/shard_map/ppermute | solution.py:334
  75.1 3.6 %copy-start.3 = (f32[2,2,2,4,56,256]{5,4,3,2,1,0:T(8,128)}, f32[2,2,2,4,56,256]{5,4,3,2,1,0:T(8,128)S(1)}, u32[]{:S(2)}) copy-start(f32[2,2,2,4,56,256]{5,4,3,2,1,0:T(8,128)S(1)} %collective-permute-done.10) | copy-start | bytes 5505028
  76.2 14.5 %collective-permute-start.11 = (f32[2,2,4,56,256]{4,3,2,1,0:T(8,128)}, f32[2,2,4,56,256]{4,3,2,1,0:T(8,128)S(1)}, u32[]{:S(2)}, u32[]{:S(2)}) collective-permute-start(f32[2,2,4,56,256]{4,3,2,1,0:T(8,128)} %fusion), channel_id=1, source_target_pairs={{0,64},{4,196},{64,0},{68,132},{128,192},{132,68},{192,128},{196,4... | collective-permute-start | bytes 2752520 | tf_op jit(solution)/shard_map/ppermute | solution.py:37
  79.6 9.5 %collective-permute-start.17 = (f32[2,2,4,16,256]{4,3,2,1,0:T(8,128)S(1)}, f32[2,2,4,16,256]{4,3,2,1,0:T(8,128)}, u32[]{:S(2)}, u32[]{:S(2)}) collective-permute-start(f32[2,2,4,16,256]{4,3,2,1,0:T(8,128)S(1)} %fusion.6), channel_id=1, source_target_pairs={{0,8},{4,60},{8,0},{12,20},{16,24},{20,12},{24,16},{28,36},{32,40}... | collective-permute-start | bytes 786440 | tf_op jit(solution)/shard_map/ppermute | solution.py:37
  90.2 7.0 %collective-permute-start.18 = (f32[2,4,16,256]{3,2,1,0:T(8,128)S(1)}, f32[2,4,16,256]{3,2,1,0:T(8,128)S(1)}, u32[]{:S(2)}, u32[]{:S(2)}) collective-permute-start(f32[2,4,16,256]{3,2,1,0:T(8,128)S(1)} %slice_bitcast_fusion.4), channel_id=1, source_target_pairs={{0,64},{4,196},{64,0},{68,132},{128,192},{132,68},{192,128},{196,4... | collective-permute-start | bytes 393224 | tf_op jit(solution)/shard_map/ppermute | solution.py:37
  92.4 10.7 %collective-permute-start.12 = (f32[2,4,56,256]{3,2,1,0:T(8,128)S(1)}, f32[2,4,56,256]{3,2,1,0:T(8,128)S(1)}, u32[]{:S(2)}, u32[]{:S(2)}) collective-permute-start(f32[2,4,56,256]{3,2,1,0:T(8,128)S(1)} %slice_bitcast_fusion), channel_id=1, source_target_pairs={{0,8},{4,60},{8,0},{12,20},{16,24},{20,12},{24,16},{28,36},{32,40}... | collective-permute-start | bytes 1376264 | tf_op jit(solution)/shard_map/ppermute | solution.py:37
  103.3 5.7 %collective-permute-start.19 = (f32[4,72,256]{2,1,0:T(8,128)S(1)}, f32[4,72,256]{2,1,0:T(8,128)S(1)}, u32[]{:S(2)}, u32[]{:S(2)}) collective-permute-start(f32[4,72,256]{2,1,0:T(8,128)S(1)} %pad_maximum_fusion.2), channel_id=1, source_target_pairs={{0,192},{4,68},{64,128},{68,4},{128,64},{132,196},{192,0},{196,132... | collective-permute-start | bytes 884744 | tf_op jit(solution)/shard_map/ppermute | solution.py:37
  109.0 5.9 %collective-permute-start.22 = (f32[72,256]{1,0:T(8,128)S(1)}, f32[72,256]{1,0:T(8,128)S(1)}, u32[]{:S(2)}, u32[]{:S(2)}) collective-permute-start(f32[72,256]{1,0:T(8,128)S(1)} %get-tuple-element.52), channel_id=1, source_target_pairs={{0,56},{4,12},{8,16},{12,4},{16,8},{20,28},{24,32},{28,20},{32,24}... | collective-permute-start | bytes 221192 | tf_op jit(solution)/shard_map/ppermute | solution.py:37
  109.1 7.7 %collective-permute-start.21 = (f32[72,256]{1,0:T(8,128)S(1)}, f32[72,256]{1,0:T(8,128)S(1)}, u32[]{:S(2)}, u32[]{:S(2)}) collective-permute-start(f32[72,256]{1,0:T(8,128)S(1)} %get-tuple-element.53), channel_id=1, source_target_pairs={{0,24},{4,44},{8,48},{12,36},{16,40},{20,60},{24,0},{28,52},{32,56... | collective-permute-start | bytes 221192 | tf_op jit(solution)/shard_map/ppermute | solution.py:37
  113.7 7.9 %collective-permute-start.20 = (f32[72,256]{1,0:T(8,128)S(1)}, f32[72,256]{1,0:T(8,128)S(1)}, u32[]{:S(2)}, u32[]{:S(2)}) collective-permute-start(f32[72,256]{1,0:T(8,128)S(1)} %get-tuple-element.54), channel_id=1, source_target_pairs={{0,32},{4,36},{8,40},{12,44},{16,48},{20,52},{24,56},{28,60},{32,0... | collective-permute-start | bytes 221192 | tf_op jit(solution)/shard_map/ppermute | solution.py:37
  (1 other events, 0.8 us)

commit v3 on v2

--- a/solution.py
+++ b/solution.py
@@ -170,8 +170,8 @@
     arrange(info, part, blocks, (keep, send))
 
 
-def pack_kernel(kept, other, far, across, base, shard, small):
-    total = kept[...] + other[...] + far[...] + across[...]
+def pack_kernel(kept, came, base, shard, small):
+    total = kept[...] + came[...]
     shard[...] = total
     column = lax.broadcasted_iota(jnp.int32, small.shape, 1)
     squares = jnp.sum(jnp.sum(total * total, axis=0, keepdims=True), axis=1, keepdims=True)
@@ -349,17 +349,27 @@
     )
     came_b = core(send_b)
 
-    p = swap(keep_p[0] + came_p[0], X, first)
-    p = keep_p[1] + came_p[1] + p
-    w = keep_b[1] + came_b[1] + swap(keep_b[0] + came_b[0], Z, first)
-    p = p[1] + swap(p[0], Z, first)
-    w = w[1] + swap(w[0], X, first)
-    both = lambda i: jnp.concatenate([p[i], w[i]], axis=-2)
-    shard = both(0) + swap(both(1), X, second)
-    across = lambda i, c, n: third(second(i, c, n), c, n)
-    parts = (shard[0],) + tuple(
-        swap(shard[k], Z, partner) for k, partner in ((3, across), (1, third), (2, second))
-    )
+    def step_on(parts, axis, partner, k=0):
+        leaving = functools.reduce(jnp.add, [part[k] for part in parts])
+        rest = [part[1 - k] for part in parts]
+        leaving, *rest = lax.optimization_barrier((leaving, *rest))
+        return [*rest, swap(leaving, axis, partner)]
+
+    p = step_on([keep_p, came_p], X, first)
+    w = step_on([keep_b, came_b], Z, first)
+    p = step_on(p, Z, first)
+    w = step_on(w, X, first)
+
+    def both(k):
+        p_sum, w_sum = (functools.reduce(jnp.add, [part[k] for part in parts]) for parts in (p, w))
+        return jnp.concatenate([p_sum, w_sum], axis=-2)
+
+    leaving, *rest = lax.optimization_barrier((both(1), *p, *w))
+    p, w = rest[: len(p)], rest[len(p) :]
+    came = swap(leaving, X, second)
+    shard = both(0) + came
+    shard = shard[:2] + swap(shard[2:], Z, second)
+    parts = (shard[0], swap(shard[1], Z, third))
 
     target = lax.dynamic_index_in_dim(pair_destination, place, 1, keepdims=False)
     hits = jnp.arange(pairs)[:, None] == target[None, :]

time: 146 us -> 143 us (0.979)
  waiting for transfers between devices: 47 us -> 38.1 us
  blocking collectives: 22.6 us -> 28.9 us
    ppermute x20 -> x19, waiting for transfers between devices: 45.9 us -> 36.7 us  [swap(): return lax.ppermute(value, axes, pairs)]
    all_to_all x1, blocking collectives: 22.6 us -> 28.9 us  [per_device(): small = lax.all_to_all(small, (X, Z, C, Y), 0, 0, tiled=True)]
    add x7 -> x6, other arithmetic: 4.07 us -> 0.25 us  [the longest x4 0.2 us: both(): functools.reduce(jnp.add, [part[k] for part in parts])]
    squeeze x0 -> x4, other arithmetic: none -> 3.7 us  [step_on(): rest = [part[1 - k] for part in parts]]
    ppermute x2, starting transfers between devices: 7.83 us -> 11.3 us  [per_device(): core = lambda value: lax.ppermute(value, C, [(0, 1), (1, 0)])]
    ppermute x20 -> x19, starting transfers between devices: 32.9 us -> 30 us  [swap(): return lax.ppermute(value, axes, pairs)]
  transfers between devices with their start and end apart: 23 -> 22, of which waited for: 15 -> 12; matrix products, arithmetic and copies ran while one was open for 13% -> 13% of each run, Pallas kernels for 2% -> 3%
where the time goes in v3:
time: 143 us
  starting transfers between devices  41.3 us (29%)
  waiting for transfers between devices  38.1 us (27%)
  blocking collectives  28.9 us (20%)
  other arithmetic  11.7 us (8%)
  Pallas kernels  10.9 us (8%)
  matrix products  7.64 us (5%)
  local copies, waits for them, and re-layouts  2.51 us (2%)
  between operations  1.55 us (1%)
    ppermute x19, waiting for transfers between devices, swap(): return lax.ppermute(value, axes, pairs)  36.7 us
    ppermute x19, starting transfers between devices, swap(): return lax.ppermute(value, axes, pairs)  30 us
    all_to_all x1, blocking collectives, per_device(): small = lax.all_to_all(small, (X, Z, C, Y), 0, 0, tiled=True)  28.9 us
    ppermute x2, starting transfers between devices, per_device(): core = lambda value: lax.ppermute(value, C, [(0, 1), (1, 0)])  11.3 us
    pallas_call x2, Pallas kernels, kernel_call(): pl.pallas_call(body, grid_spec=pltpu.PrefetchScalarGridSpec(num_scalar_pr...  9.98 us
    dot_general x2, matrix products, product(): jnp.dot(value, weights, preferred_element_type=jnp.float32)  7.64 us
    squeeze x4, other arithmetic, step_on(): rest = [part[1 - k] for part in parts]  3.7 us
  transfers between devices with their start and end apart: 22, of which 12 were waited for; matrix products, arithmetic and copies ran while one was open for 13% of the time, Pallas kernels for 3%

profile of v3, /device:TPU:1, one launch (start us, length us, event | category | flops | bytes accessed | tf_op | source)
XLA Modules:
  0.0 142.5 jit_solution(8121648190971597080)
XLA Ops:
  0.7 2.5 %fusion.1 = f32[4,256,256]{2,1,0:T(8,128)S(1)} fusion(bf16[4,256,1024]{2,1,0:T(8,128)(2,1)} %bitcast.72, bf16[1024,256]{1,0:T(8,128)(2,1)} %param.16), kind=kOutput, calls=%fused_computation.6 | convolution fusion | flops 536870912 | bytes 3670016 | tf_op jit(solution)/shard_map/dot_general | solution.py:272
  3.3 3.6 %collective-permute-start = (f32[2,256,256]{2,1,0:T(8,128)S(1)}, f32[2,256,256]{2,1,0:T(8,128)}, u32[]{:S(2)}, u32[]{:S(2)}) collective-permute-start(f32[2,256,256]{2,1,0:T(8,128)S(1)} %pad_maximum_fusion), channel_id=1, source_target_pairs={{0,1},{4,7},{1,0},{5,6},{2,3},{6,5},{3,2},{7,4},{8,9},{12,15},{9,8... | collective-permute-start | bytes 1572872 | tf_op jit(solution)/shard_map/ppermute | solution.py:37
  7.0 5.1 %fusion.17 = f32[1024,256]{1,0:T(8,128)S(1)} fusion(bf16[1024,3584]{1,0:T(8,128)(2,1)} %bitcast.81, bf16[3584,256]{1,0:T(8,128)(2,1)S(1)} %copy-done), kind=kOutput, calls=%fused_computation.61 | convolution fusion | flops 1879048192 | bytes 10223616 | tf_op jit(solution)/shard_map/dot_general | solution.py:272
  15.0 9.7 %collective-permute-done.5 = f32[2,256,256]{2,1,0:T(8,128)} collective-permute-done((f32[2,256,256]{2,1,0:T(8,128)}, f32[2,256,256]{2,1,0:T(8,128)}, u32[]{:S(2)}, u32[]{:S(2)}) %collective-permute-start.5) | collective-permute-done | bytes 524320 | tf_op jit(solution)/shard_map/ppermute | solution.py:37
  24.7 1.8 %fusion.5 = f32[256,256]{1,0:T(8,128)} fusion(f32[2,256,256]{2,1,0:T(8,128)} %collective-permute-done.5, f32[4,256,256]{2,1,0:T(8,128)} %bitcast.84, s32[]{:T(128)S(6)} %select_n.61), kind=kLoop, calls=%fused_computation.19 | loop fusion | flops 65536 | bytes 786436 | tf_op jit(solution)/shard_map/add | solution.py:285
  29.6 1.5 %collective-permute-start.2 = (f32[256,256]{1,0:T(8,128)S(1)}, f32[256,256]{1,0:T(8,128)S(1)}, u32[]{:S(2)}, u32[]{:S(2)}) collective-permute-start(f32[256,256]{1,0:T(8,128)S(1)} %fusion.10.r0), channel_id=1, source_target_pairs={{0,3},{4,5},{1,2},{5,4},{2,1},{6,7},{3,0},{7,6},{8,11},{12,13},{9,... | collective-permute-start | bytes 786440 | tf_op jit(solution)/shard_map/ppermute | solution.py:37
  33.4 1.4 %collective-permute-done.2.r1 = f32[256,256]{1,0:T(8,128)S(1)} collective-permute-done((f32[256,256]{1,0:T(8,128)S(1)}, f32[256,256]{1,0:T(8,128)S(1)}, u32[]{:S(2)}, u32[]{:S(2)}) %collective-permute-start.2) | collective-permute-done | bytes 262176 | tf_op jit(solution)/shard_map/ppermute | solution.py:37
  35.1 1.5 %collective-permute-start.7 = (f32[1,256]{1,0:T(1,128)S(1)}, f32[1,256]{1,0:T(1,128)S(1)}, u32[]{:S(2)}, u32[]{:S(2)}) collective-permute-start(f32[1,256]{1,0:T(1,128)S(1)} %bitcast.77), channel_id=1, source_target_pairs={{0,3},{4,5},{1,2},{5,4},{2,1},{6,7},{3,0},{7,6},{8,11},{12,13},{9,... | collective-permute-start | bytes 3080 | tf_op jit(solution)/shard_map/ppermute | solution.py:37
  36.6 2.1 %collective-permute-start.8 = (f32[1,256]{1,0:T(1,128)S(1)}, f32[1,256]{1,0:T(1,128)S(1)}, u32[]{:S(2)}, u32[]{:S(2)}) collective-permute-start(f32[1,256]{1,0:T(1,128)S(1)} %bitcast.78), channel_id=1, source_target_pairs={{0,1},{4,7},{1,0},{5,6},{2,3},{6,5},{3,2},{7,4},{8,9},{12,15},{9,8... | collective-permute-start | bytes 3080 | tf_op jit(solution)/shard_map/ppermute | solution.py:37
  38.9 4.4 %collective-permute-done.8.s2 = f32[1,256]{1,0:T(1,128)S(1)} collective-permute-done((f32[1,256]{1,0:T(1,128)S(1)}, f32[1,256]{1,0:T(1,128)S(1)}, u32[]{:S(2)}, u32[]{:S(2)}) %collective-permute-start.8) | collective-permute-done | bytes 1056 | tf_op jit(solution)/shard_map/ppermute | solution.py:37
  43.2 6.4 %shard_map.120 = (f32[2,2,2,4,56,256]{5,4,3,2,1,0:T(8,128)S(1)}, f32[2,2,2,4,56,256]{5,4,3,2,1,0:T(8,128)S(1)}, f32[8,128]{1,0:T(8,128)S(1)}, f32[256,8]{1,0:T(8,128)S(1)}) custom-call(s32[40]{0:T(128)S(1)} %pad_add_fusion.info, f32[256,256]{1,0:T(8,128)S(1)} %fusion.10.r0, f32[256,256]{1,0:T(8,128)S(1)} %collective-permute-done.2.r1, ...), custom_call_target="tpu_custom_call" | custom-call | flops 1879048192 | bytes 11010048 | tf_op jit(solution)/shard_map/pallas_call | solution.py:219
  49.6 7.1 %collective-permute-start.10 = (f32[2,2,2,4,56,256]{5,4,3,2,1,0:T(8,128)S(1)}, f32[2,2,2,4,56,256]{5,4,3,2,1,0:T(8,128)S(1)}, u32[]{:S(2)}, u32[]{:S(2)}) collective-permute-start(f32[2,2,2,4,56,256]{5,4,3,2,1,0:T(8,128)S(1)} %get-tuple-element.44), channel_id=1, source_target_pairs={{0,4},{4,0},{1,5},{5,1},{2,6},{6,2},{3,7},{7,3},{8,12},{12,8},{9,1... | collective-permute-start | bytes 5505032 | tf_op jit(solution)/shard_map/ppermute | solution.py:334
  57.2 1.6 %collective-permute-start.14 = (f32[256,256]{1,0:T(8,128)S(1)}, f32[256,256]{1,0:T(8,128)S(1)}, u32[]{:S(2)}, u32[]{:S(2)}) collective-permute-start(f32[256,256]{1,0:T(8,128)S(1)} %fusion.7.l0), channel_id=1, source_target_pairs={{0,1},{4,7},{1,0},{5,6},{2,3},{6,5},{3,2},{7,4},{8,9},{12,15},{9,8... | collective-permute-start | bytes 786440 | tf_op jit(solution)/shard_map/ppermute | solution.py:37
  58.8 3.7 %collective-permute-done.13.l1 = f32[256,256]{1,0:T(8,128)S(1)} collective-permute-done((f32[256,256]{1,0:T(8,128)S(1)}, f32[256,256]{1,0:T(8,128)S(1)}, u32[]{:S(2)}, u32[]{:S(2)}) %collective-permute-start.13) | collective-permute-done | bytes 262176 | tf_op jit(solution)/shard_map/ppermute | solution.py:37
  62.5 2.5 %collective-permute-start.15 = (f32[256,256]{1,0:T(8,128)S(1)}, f32[256,256]{1,0:T(8,128)S(1)}, u32[]{:S(2)}, u32[]{:S(2)}) collective-permute-start(f32[256,256]{1,0:T(8,128)S(1)} %collective-permute-done.13.l1), channel_id=1, source_target_pairs={{0,1},{4,7},{1,0},{5,6},{2,3},{6,5},{3,2},{7,4},{8,9},{12,15},{9,8... | collective-permute-start | bytes 786440 | tf_op jit(solution)/shard_map/ppermute | solution.py:37
  65.0 1.7 %slice_bitcast_fusion = (f32[2,2,4,56,256]{4,3,2,1,0:T(8,128)}, f32[2,2,4,56,256]{4,3,2,1,0:T(8,128)}, f32[2,2,4,56,256]{4,3,2,1,0:T(8,128)}) fusion(f32[2,2,2,4,56,256]{5,4,3,2,1,0:T(8,128)S(1)} %collective-permute-done.10, f32[2,2,2,4,56,256]{5,4,3,2,1,0:T(8,128)S(1)} %get-tuple-element.43), kind=kLoop, calls=%fused_computation | loop fusion | flops 229376 | bytes 6422528 | tf_op jit(solution)/shard_map/squeeze | solution.py:354
  66.7 2.7 %collective-permute-start.11 = (f32[2,2,4,56,256]{4,3,2,1,0:T(8,128)}, f32[2,2,4,56,256]{4,3,2,1,0:T(8,128)}, u32[]{:S(2)}, u32[]{:S(2)}) collective-permute-start(f32[2,2,4,56,256]{4,3,2,1,0:T(8,128)} %get-tuple-element.47), channel_id=1, source_target_pairs={{0,64},{4,196},{64,0},{68,132},{128,192},{132,68},{192,128},{196,4... | collective-permute-start | bytes 2752520 | tf_op jit(solution)/shard_map/ppermute | solution.py:37
  69.4 3.6 %shard_map.121 = (f32[2,2,2,4,16,256]{5,4,3,2,1,0:T(8,128)S(1)}, f32[2,2,2,4,16,256]{5,4,3,2,1,0:T(8,128)}) custom-call(s32[40]{0:T(128)S(1)} %pad_add_fusion.info, f32[256,256]{1,0:T(8,128)S(1)} %fusion.7.l0, f32[256,256]{1,0:T(8,128)S(1)} %collective-permute-done.13.l1, f32[256,256]{1,0:T(8,128)S(1)} %collective-permute-done.14.l2, ...), custom_call_target="tpu_custom_call" | custom-call | flops 536870912 | bytes 3145728 | tf_op jit(solution)/shard_map/pallas_call | solution.py:219
  73.0 4.2 %collective-permute-start.16 = (f32[2,2,2,4,16,256]{5,4,3,2,1,0:T(8,128)}, f32[2,2,2,4,16,256]{5,4,3,2,1,0:T(8,128)S(1)}, u32[]{:S(2)}, u32[]{:S(2)}) collective-permute-start(f32[2,2,2,4,16,256]{5,4,3,2,1,0:T(8,128)} %get-tuple-element.54), channel_id=1, source_target_pairs={{0,4},{4,0},{1,5},{5,1},{2,6},{6,2},{3,7},{7,3},{8,12},{12,8},{9,1... | collective-permute-start | bytes 1572872 | tf_op jit(solution)/shard_map/ppermute | solution.py:334
  77.5 1.4 collective-permute-done.16
  79.0 5.3 %collective-permute-start.17 = (f32[2,2,4,16,256]{4,3,2,1,0:T(8,128)S(1)}, f32[2,2,4,16,256]{4,3,2,1,0:T(8,128)S(1)}, u32[]{:S(2)}, u32[]{:S(2)}) collective-permute-start(f32[2,2,4,16,256]{4,3,2,1,0:T(8,128)S(1)} %get-tuple-element.57), channel_id=1, source_target_pairs={{0,8},{4,60},{8,0},{12,20},{16,24},{20,12},{24,16},{28,36},{32,40}... | collective-permute-start | bytes 786440 | tf_op jit(solution)/shard_map/ppermute | solution.py:37
  84.3 1.9 %slice_bitcast_fusion.2 = (f32[2,4,56,256]{3,2,1,0:T(8,128)S(1)}, f32[2,4,56,256]{3,2,1,0:T(8,128)S(1)}, f32[2,4,56,256]{3,2,1,0:T(8,128)S(1)}, f32[2,4,56,256]{3,2,1,0:T(8,128)S(1)}) fusion(f32[2,2,4,56,256]{4,3,2,1,0:T(8,128)} %collective-permute-done.11, f32[2,2,4,56,256]{4,3,2,1,0:T(8,128)} %get-tuple-element.46, f32[2,2,4,56,256]{4,3,2,1,0:T(8,128)} %get-tuple-element.45), kind=kLoop, calls=%fused_computation.8 | loop fusion | flops 229376 | bytes 4587520 | tf_op jit(solution)/shard_map/squeeze | solution.py:354
  86.2 2.0 %collective-permute-start.12 = (f32[2,4,56,256]{3,2,1,0:T(8,128)S(1)}, f32[2,4,56,256]{3,2,1,0:T(8,128)S(1)}, u32[]{:S(2)}, u32[]{:S(2)}) collective-permute-start(f32[2,4,56,256]{3,2,1,0:T(8,128)S(1)} %get-tuple-element.51), channel_id=1, source_target_pairs={{0,8},{4,60},{8,0},{12,20},{16,24},{20,12},{24,16},{28,36},{32,40}... | collective-permute-start | bytes 1376264 | tf_op jit(solution)/shard_map/ppermute | solution.py:37
  88.2 2.6 %collective-permute-start.18 = (f32[2,4,16,256]{3,2,1,0:T(8,128)S(1)}, f32[2,4,16,256]{3,2,1,0:T(8,128)S(1)}, u32[]{:S(2)}, u32[]{:S(2)}) collective-permute-start(f32[2,4,16,256]{3,2,1,0:T(8,128)S(1)} %get-tuple-element.61), channel_id=1, source_target_pairs={{0,64},{4,196},{64,0},{68,132},{128,192},{132,68},{192,128},{196,4... | collective-permute-start | bytes 393224 | tf_op jit(solution)/shard_map/ppermute | solution.py:37
  90.9 2.5 %collective-permute-done.18 = f32[2,4,16,256]{3,2,1,0:T(8,128)S(1)} collective-permute-done((f32[2,4,16,256]{3,2,1,0:T(8,128)S(1)}, f32[2,4,16,256]{3,2,1,0:T(8,128)S(1)}, u32[]{:S(2)}, u32[]{:S(2)}) %collective-permute-start.18) | collective-permute-done | bytes 131104 | tf_op jit(solution)/shard_map/ppermute | solution.py:37
  93.4 1.4 collective-permute-done.12
  94.9 1.3 collective-permute-start.19
  96.3 4.5 %collective-permute-done.19 = f32[4,72,256]{2,1,0:T(8,128)S(1)} collective-permute-done((f32[4,72,256]{2,1,0:T(8,128)S(1)}, f32[4,72,256]{2,1,0:T(8,128)S(1)}, u32[]{:S(2)}, u32[]{:S(2)}) %collective-permute-start.19) | collective-permute-done | bytes 294944 | tf_op jit(solution)/shard_map/ppermute | solution.py:37
  102.3 2.6 %collective-permute-done.20 = f32[2,72,256]{2,1,0:T(8,128)S(1)} collective-permute-done((f32[2,72,256]{2,1,0:T(8,128)S(1)}, f32[2,72,256]{2,1,0:T(8,128)S(1)}, u32[]{:S(2)}, u32[]{:S(2)}) %collective-permute-start.20) | collective-permute-done | bytes 147488 | tf_op jit(solution)/shard_map/ppermute | solution.py:37
  105.0 2.0 %collective-permute-start.21 = (f32[72,256]{1,0:T(8,128)S(1)}, f32[72,256]{1,0:T(8,128)S(1)}, u32[]{:S(2)}, u32[]{:S(2)}) collective-permute-start(f32[72,256]{1,0:T(8,128)S(1)} %get-tuple-element.110), channel_id=1, source_target_pairs={{0,24},{4,44},{8,48},{12,36},{16,40},{20,60},{24,0},{28,52},{32,56... | collective-permute-start | bytes 221192 | tf_op jit(solution)/shard_map/ppermute | solution.py:37
  107.1 5.0 %collective-permute-done.21.came = f32[72,256]{1,0:T(8,128)S(1)} collective-permute-done((f32[72,256]{1,0:T(8,128)S(1)}, f32[72,256]{1,0:T(8,128)S(1)}, u32[]{:S(2)}, u32[]{:S(2)}) %collective-permute-start.21) | collective-permute-done | bytes 73760 | tf_op jit(solution)/shard_map/ppermute | solution.py:37
  112.3 28.9 %all_to_all.11 = f32[256,1,4]{2,1,0:T(1,128)S(1)} all-to-all(f32[256,1,4]{2,1,0:T(1,128)S(1)} %bitcast.76), channel_id=1, replica_groups=mesh['dp_0'=4,'dp_1'=8,'dp_2'=2,'mp'=4] {'dp_0','dp_1','dp_2','mp'}, dimensions={0} | all-to-all | bytes 8192 | tf_op jit(solution)/shard_map/all_to_all | solution.py:387
  (73 shorter events, 12.5 us)
Async XLA Ops:
  0.6 6.3 %copy-start = (bf16[3584,256]{1,0:T(8,128)(2,1)S(1)}, bf16[3584,256]{1,0:T(8,128)(2,1)}, u32[]{:S(2)}) copy-start(bf16[3584,256]{1,0:T(8,128)(2,1)} %param.15) | copy-start | bytes 5505028
  3.3 10.3 %collective-permute-start = (f32[2,256,256]{2,1,0:T(8,128)S(1)}, f32[2,256,256]{2,1,0:T(8,128)}, u32[]{:S(2)}, u32[]{:S(2)}) collective-permute-start(f32[2,256,256]{2,1,0:T(8,128)S(1)} %pad_maximum_fusion), channel_id=1, source_target_pairs={{0,1},{4,7},{1,0},{5,6},{2,3},{6,5},{3,2},{7,4},{8,9},{12,15},{9,8... | collective-permute-start | bytes 1572872 | tf_op jit(solution)/shard_map/ppermute | solution.py:37
  12.1 1.2 copy-start.2
  12.1 15.6 %copy-start.5 = (s32[2,1,2]{2,1,0:T(1,128)S(1)}, s32[2,1,2]{2,1,0:T(1,128)}, u32[]{:S(2)}) copy-start(s32[2,1,2]{2,1,0:T(1,128)} %param.13) | copy-start | bytes 52
  13.3 11.5 %collective-permute-start.5 = (f32[2,256,256]{2,1,0:T(8,128)}, f32[2,256,256]{2,1,0:T(8,128)}, u32[]{:S(2)}, u32[]{:S(2)}) collective-permute-start(f32[2,256,256]{2,1,0:T(8,128)} %pad_maximum_fusion.1), channel_id=1, source_target_pairs={{0,1},{4,7},{1,0},{5,6},{2,3},{6,5},{3,2},{7,4},{8,9},{12,15},{9,8... | collective-permute-start | bytes 1572872 | tf_op jit(solution)/shard_map/ppermute | solution.py:37
  14.6 24.2 %copy-start.3 = (f32[2,1,2,256]{3,2,1,0:T(2,128)S(1)}, f32[2,1,2,256]{3,2,1,0:T(2,128)}, u32[]{:S(2)}) copy-start(f32[2,1,2,256]{3,2,1,0:T(2,128)} %param.11) | copy-start | bytes 12292
  14.6 24.2 %copy-start.4 = (s32[2,1,2,256]{3,2,1,0:T(2,128)S(1)}, s32[2,1,2,256]{3,2,1,0:T(2,128)}, u32[]{:S(2)}) copy-start(s32[2,1,2,256]{3,2,1,0:T(2,128)} %param.12) | copy-start | bytes 12292
  14.6 13.8 %collective-permute-start.1 = (f32[256,256]{1,0:T(8,128)S(1)}, f32[256,256]{1,0:T(8,128)}, u32[]{:S(2)}, u32[]{:S(2)}) collective-permute-start(f32[256,256]{1,0:T(8,128)S(1)} %fusion.8), channel_id=1, source_target_pairs={{0,3},{4,5},{1,2},{5,4},{2,1},{6,7},{3,0},{7,6},{8,11},{12,13},{9,... | collective-permute-start | bytes 786440 | tf_op jit(solution)/shard_map/ppermute | solution.py:37
  26.5 5.7 %collective-permute-start.6 = (f32[256,256]{1,0:T(8,128)}, f32[256,256]{1,0:T(8,128)S(1)}, u32[]{:S(2)}, u32[]{:S(2)}) collective-permute-start(f32[256,256]{1,0:T(8,128)} %fusion.5), channel_id=1, source_target_pairs={{0,3},{4,5},{1,2},{5,4},{2,1},{6,7},{3,0},{7,6},{8,11},{12,13},{9,... | collective-permute-start | bytes 786440 | tf_op jit(solution)/shard_map/ppermute | solution.py:37
  29.6 5.3 %collective-permute-start.2 = (f32[256,256]{1,0:T(8,128)S(1)}, f32[256,256]{1,0:T(8,128)S(1)}, u32[]{:S(2)}, u32[]{:S(2)}) collective-permute-start(f32[256,256]{1,0:T(8,128)S(1)} %fusion.10.r0), channel_id=1, source_target_pairs={{0,3},{4,5},{1,2},{5,4},{2,1},{6,7},{3,0},{7,6},{8,11},{12,13},{9,... | collective-permute-start | bytes 786440 | tf_op jit(solution)/shard_map/ppermute | solution.py:37
  31.1 12.1 %collective-permute-start.3 = (f32[256,256]{1,0:T(8,128)S(1)}, f32[256,256]{1,0:T(8,128)S(1)}, u32[]{:S(2)}, u32[]{:S(2)}) collective-permute-start(f32[256,256]{1,0:T(8,128)S(1)} %fusion.10.r0), channel_id=1, source_target_pairs={{0,1},{4,7},{1,0},{5,6},{2,3},{6,5},{3,2},{7,4},{8,9},{12,15},{9,8... | collective-permute-start | bytes 786440 | tf_op jit(solution)/shard_map/ppermute | solution.py:37
  34.9 8.4 %collective-permute-start.4 = (f32[256,256]{1,0:T(8,128)S(1)}, f32[256,256]{1,0:T(8,128)S(1)}, u32[]{:S(2)}, u32[]{:S(2)}) collective-permute-start(f32[256,256]{1,0:T(8,128)S(1)} %collective-permute-done.2.r1), channel_id=1, source_target_pairs={{0,1},{4,7},{1,0},{5,6},{2,3},{6,5},{3,2},{7,4},{8,9},{12,15},{9,8... | collective-permute-start | bytes 786440 | tf_op jit(solution)/shard_map/ppermute | solution.py:37
  35.1 3.8 %collective-permute-start.7 = (f32[1,256]{1,0:T(1,128)S(1)}, f32[1,256]{1,0:T(1,128)S(1)}, u32[]{:S(2)}, u32[]{:S(2)}) collective-permute-start(f32[1,256]{1,0:T(1,128)S(1)} %bitcast.77), channel_id=1, source_target_pairs={{0,3},{4,5},{1,2},{5,4},{2,1},{6,7},{3,0},{7,6},{8,11},{12,13},{9,... | collective-permute-start | bytes 3080 | tf_op jit(solution)/shard_map/ppermute | solution.py:37
  36.6 6.6 %collective-permute-start.8 = (f32[1,256]{1,0:T(1,128)S(1)}, f32[1,256]{1,0:T(1,128)S(1)}, u32[]{:S(2)}, u32[]{:S(2)}) collective-permute-start(f32[1,256]{1,0:T(1,128)S(1)} %bitcast.78), channel_id=1, source_target_pairs={{0,1},{4,7},{1,0},{5,6},{2,3},{6,5},{3,2},{7,4},{8,9},{12,15},{9,8... | collective-permute-start | bytes 3080 | tf_op jit(solution)/shard_map/ppermute | solution.py:37
  38.7 4.5 %collective-permute-start.9 = (f32[1,256]{1,0:T(1,128)S(1)}, f32[1,256]{1,0:T(1,128)S(1)}, u32[]{:S(2)}, u32[]{:S(2)}) collective-permute-start(f32[1,256]{1,0:T(1,128)S(1)} %bitcast.79), channel_id=1, source_target_pairs={{0,2},{1,3},{2,0},{3,1},{4,6},{5,7},{6,4},{7,5},{8,10},{9,11},{10,... | collective-permute-start | bytes 3080 | tf_op jit(solution)/shard_map/ppermute | solution.py:300
  49.6 15.4 %collective-permute-start.10 = (f32[2,2,2,4,56,256]{5,4,3,2,1,0:T(8,128)S(1)}, f32[2,2,2,4,56,256]{5,4,3,2,1,0:T(8,128)S(1)}, u32[]{:S(2)}, u32[]{:S(2)}) collective-permute-start(f32[2,2,2,4,56,256]{5,4,3,2,1,0:T(8,128)S(1)} %get-tuple-element.44), channel_id=1, source_target_pairs={{0,4},{4,0},{1,5},{5,1},{2,6},{6,2},{3,7},{7,3},{8,12},{12,8},{9,1... | collective-permute-start | bytes 5505032 | tf_op jit(solution)/shard_map/ppermute | solution.py:334
  56.7 5.7 %collective-permute-start.13 = (f32[256,256]{1,0:T(8,128)S(1)}, f32[256,256]{1,0:T(8,128)S(1)}, u32[]{:S(2)}, u32[]{:S(2)}) collective-permute-start(f32[256,256]{1,0:T(8,128)S(1)} %fusion.7.l0), channel_id=1, source_target_pairs={{0,3},{4,5},{1,2},{5,4},{2,1},{6,7},{3,0},{7,6},{8,11},{12,13},{9,... | collective-permute-start | bytes 786440 | tf_op jit(solution)/shard_map/ppermute | solution.py:37
  57.2 12.2 %collective-permute-start.14 = (f32[256,256]{1,0:T(8,128)S(1)}, f32[256,256]{1,0:T(8,128)S(1)}, u32[]{:S(2)}, u32[]{:S(2)}) collective-permute-start(f32[256,256]{1,0:T(8,128)S(1)} %fusion.7.l0), channel_id=1, source_target_pairs={{0,1},{4,7},{1,0},{5,6},{2,3},{6,5},{3,2},{7,4},{8,9},{12,15},{9,8... | collective-permute-start | bytes 786440 | tf_op jit(solution)/shard_map/ppermute | solution.py:37
  62.5 6.9 %collective-permute-start.15 = (f32[256,256]{1,0:T(8,128)S(1)}, f32[256,256]{1,0:T(8,128)S(1)}, u32[]{:S(2)}, u32[]{:S(2)}) collective-permute-start(f32[256,256]{1,0:T(8,128)S(1)} %collective-permute-done.13.l1), channel_id=1, source_target_pairs={{0,1},{4,7},{1,0},{5,6},{2,3},{6,5},{3,2},{7,4},{8,9},{12,15},{9,8... | collective-permute-start | bytes 786440 | tf_op jit(solution)/shard_map/ppermute | solution.py:37
  65.0 4.3 %copy-start.1 = (bf16[2,1,2,256,1024]{4,3,2,1,0:T(8,128)(2,1)S(1)}, bf16[2,1,2,256,1024]{4,3,2,1,0:T(8,128)(2,1)}, u32[]{:S(2)}) copy-start(bf16[2,1,2,256,1024]{4,3,2,1,0:T(8,128)(2,1)} %param.10) | copy-start | bytes 6291460
  66.7 10.5 %copy-start.6 = (s32[2,64]{1,0:T(2,128)S(1)}, s32[2,64]{1,0:T(2,128)}, u32[]{:S(2)}) copy-start(s32[2,64]{1,0:T(2,128)} %param.14) | copy-start | bytes 1540
  66.7 17.6 %collective-permute-start.11 = (f32[2,2,4,56,256]{4,3,2,1,0:T(8,128)}, f32[2,2,4,56,256]{4,3,2,1,0:T(8,128)}, u32[]{:S(2)}, u32[]{:S(2)}) collective-permute-start(f32[2,2,4,56,256]{4,3,2,1,0:T(8,128)} %get-tuple-element.47), channel_id=1, source_target_pairs={{0,64},{4,196},{64,0},{68,132},{128,192},{132,68},{192,128},{196,4... | collective-permute-start | bytes 2752520 | tf_op jit(solution)/shard_map/ppermute | solution.py:37
  73.0 5.9 %collective-permute-start.16 = (f32[2,2,2,4,16,256]{5,4,3,2,1,0:T(8,128)}, f32[2,2,2,4,16,256]{5,4,3,2,1,0:T(8,128)S(1)}, u32[]{:S(2)}, u32[]{:S(2)}) collective-permute-start(f32[2,2,2,4,16,256]{5,4,3,2,1,0:T(8,128)} %get-tuple-element.54), channel_id=1, source_target_pairs={{0,4},{4,0},{1,5},{5,1},{2,6},{6,2},{3,7},{7,3},{8,12},{12,8},{9,1... | collective-permute-start | bytes 1572872 | tf_op jit(solution)/shard_map/ppermute | solution.py:334
  79.0 9.2 %collective-permute-start.17 = (f32[2,2,4,16,256]{4,3,2,1,0:T(8,128)S(1)}, f32[2,2,4,16,256]{4,3,2,1,0:T(8,128)S(1)}, u32[]{:S(2)}, u32[]{:S(2)}) collective-permute-start(f32[2,2,4,16,256]{4,3,2,1,0:T(8,128)S(1)} %get-tuple-element.57), channel_id=1, source_target_pairs={{0,8},{4,60},{8,0},{12,20},{16,24},{20,12},{24,16},{28,36},{32,40}... | collective-permute-start | bytes 786440 | tf_op jit(solution)/shard_map/ppermute | solution.py:37
  86.2 8.6 %collective-permute-start.12 = (f32[2,4,56,256]{3,2,1,0:T(8,128)S(1)}, f32[2,4,56,256]{3,2,1,0:T(8,128)S(1)}, u32[]{:S(2)}, u32[]{:S(2)}) collective-permute-start(f32[2,4,56,256]{3,2,1,0:T(8,128)S(1)} %get-tuple-element.51), channel_id=1, source_target_pairs={{0,8},{4,60},{8,0},{12,20},{16,24},{20,12},{24,16},{28,36},{32,40}... | collective-permute-start | bytes 1376264 | tf_op jit(solution)/shard_map/ppermute | solution.py:37
  88.2 5.1 %collective-permute-start.18 = (f32[2,4,16,256]{3,2,1,0:T(8,128)S(1)}, f32[2,4,16,256]{3,2,1,0:T(8,128)S(1)}, u32[]{:S(2)}, u32[]{:S(2)}) collective-permute-start(f32[2,4,16,256]{3,2,1,0:T(8,128)S(1)} %get-tuple-element.61), channel_id=1, source_target_pairs={{0,64},{4,196},{64,0},{68,132},{128,192},{132,68},{192,128},{196,4... | collective-permute-start | bytes 393224 | tf_op jit(solution)/shard_map/ppermute | solution.py:37
  94.9 5.9 %collective-permute-start.19 = (f32[4,72,256]{2,1,0:T(8,128)S(1)}, f32[4,72,256]{2,1,0:T(8,128)S(1)}, u32[]{:S(2)}, u32[]{:S(2)}) collective-permute-start(f32[4,72,256]{2,1,0:T(8,128)S(1)} %pad_maximum_fusion.2), channel_id=1, source_target_pairs={{0,192},{4,68},{64,128},{68,4},{128,64},{132,196},{192,0},{196,132... | collective-permute-start | bytes 884744 | tf_op jit(solution)/shard_map/ppermute | solution.py:37
  100.9 4.1 %collective-permute-start.20 = (f32[2,72,256]{2,1,0:T(8,128)S(1)}, f32[2,72,256]{2,1,0:T(8,128)S(1)}, u32[]{:S(2)}, u32[]{:S(2)}) collective-permute-start(f32[2,72,256]{2,1,0:T(8,128)S(1)} %slice.195), channel_id=1, source_target_pairs={{0,56},{4,12},{8,16},{12,4},{16,8},{20,28},{24,32},{28,20},{32,24}... | collective-permute-start | bytes 442376 | tf_op jit(solution)/shard_map/ppermute | solution.py:37
  105.0 7.2 %collective-permute-start.21 = (f32[72,256]{1,0:T(8,128)S(1)}, f32[72,256]{1,0:T(8,128)S(1)}, u32[]{:S(2)}, u32[]{:S(2)}) collective-permute-start(f32[72,256]{1,0:T(8,128)S(1)} %get-tuple-element.110), channel_id=1, source_target_pairs={{0,24},{4,44},{8,48},{12,36},{16,40},{20,60},{24,0},{28,52},{32,56... | collective-permute-start | bytes 221192 | tf_op jit(solution)/shard_map/ppermute | solution.py:37

commit v4 on v3

--- a/solution.py
+++ b/solution.py
@@ -352,7 +352,6 @@
     def step_on(parts, axis, partner, k=0):
         leaving = functools.reduce(jnp.add, [part[k] for part in parts])
         rest = [part[1 - k] for part in parts]
-        leaving, *rest = lax.optimization_barrier((leaving, *rest))
         return [*rest, swap(leaving, axis, partner)]
 
     p = step_on([keep_p, came_p], X, first)
@@ -364,9 +363,7 @@
         p_sum, w_sum = (functools.reduce(jnp.add, [part[k] for part in parts]) for parts in (p, w))
         return jnp.concatenate([p_sum, w_sum], axis=-2)
 
-    leaving, *rest = lax.optimization_barrier((both(1), *p, *w))
-    p, w = rest[: len(p)], rest[len(p) :]
-    came = swap(leaving, X, second)
+    came = swap(both(1), X, second)
     shard = both(0) + came
     shard = shard[:2] + swap(shard[2:], Z, second)
     parts = (shard[0], swap(shard[1], Z, third))

time: 143 us -> 141 us (0.986)
  starting transfers between devices: 41.3 us -> 36.5 us
  waiting for transfers between devices: 38.1 us -> 42.5 us
    squeeze x4 -> x0, other arithmetic: 3.7 us -> none  [step_on(): rest = [part[1 - k] for part in parts]]
    ppermute x2, starting transfers between devices: 11.3 us -> 7.86 us  [per_device(): core = lambda value: lax.ppermute(value, C, [(0, 1), (1, 0)])]
    ppermute x19, waiting for transfers between devices: 36.7 us -> 39.9 us  [swap(): return lax.ppermute(value, axes, pairs)]
    ppermute x19, starting transfers between devices: 30 us -> 28 us  [swap(): return lax.ppermute(value, axes, pairs)]
    add x4 -> x2, other arithmetic: 0.2 us -> 1.71 us  [both(): functools.reduce(jnp.add, [part[k] for part in parts])]
  transfers between devices with their start and end apart: 22 -> 22, of which waited for: 12 -> 17; matrix products, arithmetic and copies ran while one was open for 13% -> 11% of each run, Pallas kernels for 3% -> 2%
where the time goes in v4:
time: 141 us
  waiting for transfers between devices  42.5 us (30%)
  starting transfers between devices  36.5 us (26%)
  blocking collectives  28.9 us (20%)
  other arithmetic  10.7 us (8%)
  Pallas kernels  10.2 us (7%)
  matrix products  7.64 us (5%)
  local copies, waits for them, and re-layouts  2.59 us (2%)
  between operations  1.59 us (1%)
    ppermute x19, waiting for transfers between devices, swap(): return lax.ppermute(value, axes, pairs)  39.9 us
    all_to_all x1, blocking collectives, per_device(): small = lax.all_to_all(small, (X, Z, C, Y), 0, 0, tiled=True)  28.9 us
    ppermute x19, starting transfers between devices, swap(): return lax.ppermute(value, axes, pairs)  28 us
    pallas_call x2, Pallas kernels, kernel_call(): pl.pallas_call(body, grid_spec=pltpu.PrefetchScalarGridSpec(num_scalar_pr...  9.31 us
    ppermute x2, starting transfers between devices, per_device(): core = lambda value: lax.ppermute(value, C, [(0, 1), (1, 0)])  7.86 us
    dot_general x2, matrix products, product(): jnp.dot(value, weights, preferred_element_type=jnp.float32)  7.64 us
  transfers between devices with their start and end apart: 22, of which 17 were waited for; matrix products, arithmetic and copies ran while one was open for 11% of the time, Pallas kernels for 2%

profile of v4, /device:TPU:1, one launch (start us, length us, event | category | flops | bytes accessed | tf_op | source)
XLA Modules:
  0.0 140.6 jit_solution(2609609494379888507)
XLA Ops:
  0.7 2.5 %fusion.1 = f32[4,256,256]{2,1,0:T(8,128)S(1)} fusion(bf16[4,256,1024]{2,1,0:T(8,128)(2,1)} %bitcast.112, bf16[1024,256]{1,0:T(8,128)(2,1)} %param.16), kind=kOutput, calls=%fused_computation.4 | convolution fusion | flops 536870912 | bytes 3670016 | tf_op jit(solution)/shard_map/dot_general | solution.py:272
  3.3 3.6 %collective-permute-start = (f32[2,256,256]{2,1,0:T(8,128)S(1)}, f32[2,256,256]{2,1,0:T(8,128)}, u32[]{:S(2)}, u32[]{:S(2)}) collective-permute-start(f32[2,256,256]{2,1,0:T(8,128)S(1)} %pad_maximum_fusion), channel_id=1, source_target_pairs={{0,1},{4,7},{1,0},{5,6},{2,3},{6,5},{3,2},{7,4},{8,9},{12,15},{9,8... | collective-permute-start | bytes 1572872 | tf_op jit(solution)/shard_map/ppermute | solution.py:37
  6.9 5.1 %fusion.29 = f32[1024,256]{1,0:T(8,128)S(1)} fusion(bf16[1024,3584]{1,0:T(8,128)(2,1)} %bitcast.121, bf16[3584,256]{1,0:T(8,128)(2,1)S(1)} %copy-done), kind=kOutput, calls=%fused_computation.73 | convolution fusion | flops 1879048192 | bytes 10223616 | tf_op jit(solution)/shard_map/dot_general | solution.py:272
  15.0 9.7 %collective-permute-done.5 = f32[2,256,256]{2,1,0:T(8,128)} collective-permute-done((f32[2,256,256]{2,1,0:T(8,128)}, f32[2,256,256]{2,1,0:T(8,128)}, u32[]{:S(2)}, u32[]{:S(2)}) %collective-permute-start.5) | collective-permute-done | bytes 524320 | tf_op jit(solution)/shard_map/ppermute | solution.py:37
  24.8 1.8 %fusion.6 = f32[256,256]{1,0:T(8,128)} fusion(f32[2,256,256]{2,1,0:T(8,128)} %collective-permute-done.5, f32[4,256,256]{2,1,0:T(8,128)} %bitcast.124, s32[]{:T(128)S(6)} %select_n.61), kind=kLoop, calls=%fused_computation.15 | loop fusion | flops 65536 | bytes 786436 | tf_op jit(solution)/shard_map/add | solution.py:285
  28.5 1.1 fusion.11.r0
  29.7 1.5 %collective-permute-start.2 = (f32[256,256]{1,0:T(8,128)S(1)}, f32[256,256]{1,0:T(8,128)S(1)}, u32[]{:S(2)}, u32[]{:S(2)}) collective-permute-start(f32[256,256]{1,0:T(8,128)S(1)} %fusion.11.r0), channel_id=1, source_target_pairs={{0,3},{4,5},{1,2},{5,4},{2,1},{6,7},{3,0},{7,6},{8,11},{12,13},{9,... | collective-permute-start | bytes 786440 | tf_op jit(solution)/shard_map/ppermute | solution.py:37
  32.2 1.1 fusion.8.l0
  33.4 2.1 %collective-permute-done.2.r1 = f32[256,256]{1,0:T(8,128)S(1)} collective-permute-done((f32[256,256]{1,0:T(8,128)S(1)}, f32[256,256]{1,0:T(8,128)S(1)}, u32[]{:S(2)}, u32[]{:S(2)}) %collective-permute-start.2) | collective-permute-done | bytes 262176 | tf_op jit(solution)/shard_map/ppermute | solution.py:37
  35.5 3.9 %collective-permute-start.4 = (f32[256,256]{1,0:T(8,128)S(1)}, f32[256,256]{1,0:T(8,128)S(1)}, u32[]{:S(2)}, u32[]{:S(2)}) collective-permute-start(f32[256,256]{1,0:T(8,128)S(1)} %collective-permute-done.2.r1), channel_id=1, source_target_pairs={{0,1},{4,7},{1,0},{5,6},{2,3},{6,5},{3,2},{7,4},{8,9},{12,15},{9,8... | collective-permute-start | bytes 786440 | tf_op jit(solution)/shard_map/ppermute | solution.py:37
  40.0 2.1 %collective-permute-start.8 = (f32[1,256]{1,0:T(1,128)S(1)}, f32[1,256]{1,0:T(1,128)S(1)}, u32[]{:S(2)}, u32[]{:S(2)}) collective-permute-start(f32[1,256]{1,0:T(1,128)S(1)} %bitcast.118), channel_id=1, source_target_pairs={{0,1},{4,7},{1,0},{5,6},{2,3},{6,5},{3,2},{7,4},{8,9},{12,15},{9,8... | collective-permute-start | bytes 3080 | tf_op jit(solution)/shard_map/ppermute | solution.py:37
  42.2 1.1 collective-permute-done.9.s3
  43.7 1.2 collective-permute-done.7.s1
  44.8 6.4 %shard_map.120 = (f32[2,2,2,4,56,256]{5,4,3,2,1,0:T(8,128)S(1)}, f32[2,2,2,4,56,256]{5,4,3,2,1,0:T(8,128)S(1)}, f32[8,128]{1,0:T(8,128)S(1)}, f32[256,8]{1,0:T(8,128)S(1)}) custom-call(s32[40]{0:T(128)S(1)} %pad_add_fusion.info, f32[256,256]{1,0:T(8,128)S(1)} %fusion.11.r0, f32[256,256]{1,0:T(8,128)S(1)} %collective-permute-done.2.r1, ...), custom_call_target="tpu_custom_call" | custom-call | flops 1879048192 | bytes 11010048 | tf_op jit(solution)/shard_map/pallas_call | solution.py:219
  51.2 3.9 %collective-permute-start.10 = (f32[2,2,2,4,56,256]{5,4,3,2,1,0:T(8,128)S(1)}, f32[2,2,2,4,56,256]{5,4,3,2,1,0:T(8,128)S(1)}, u32[]{:S(2)}, u32[]{:S(2)}) collective-permute-start(f32[2,2,2,4,56,256]{5,4,3,2,1,0:T(8,128)S(1)} %get-tuple-element.21), channel_id=1, source_target_pairs={{0,4},{4,0},{1,5},{5,1},{2,6},{6,2},{3,7},{7,3},{8,12},{12,8},{9,1... | collective-permute-start | bytes 5505032 | tf_op jit(solution)/shard_map/ppermute | solution.py:334
  56.6 5.1 %collective-permute-done.13.l1 = f32[256,256]{1,0:T(8,128)S(1)} collective-permute-done((f32[256,256]{1,0:T(8,128)S(1)}, f32[256,256]{1,0:T(8,128)S(1)}, u32[]{:S(2)}, u32[]{:S(2)}) %collective-permute-start.13) | collective-permute-done | bytes 262176 | tf_op jit(solution)/shard_map/ppermute | solution.py:37
  62.0 2.8 %collective-permute-start.11 = (f32[2,2,4,56,256]{4,3,2,1,0:T(8,128)S(1)}, f32[2,2,4,56,256]{4,3,2,1,0:T(8,128)S(1)}, u32[]{:S(2)}, u32[]{:S(2)}) collective-permute-start(f32[2,2,4,56,256]{4,3,2,1,0:T(8,128)S(1)} %fusion), channel_id=1, source_target_pairs={{0,64},{4,196},{64,0},{68,132},{128,192},{132,68},{192,128},{196,4... | collective-permute-start | bytes 2752520 | tf_op jit(solution)/shard_map/ppermute | solution.py:37
  65.2 2.9 %collective-permute-done.15.l3 = f32[256,256]{1,0:T(8,128)S(1)} collective-permute-done((f32[256,256]{1,0:T(8,128)S(1)}, f32[256,256]{1,0:T(8,128)S(1)}, u32[]{:S(2)}, u32[]{:S(2)}) %collective-permute-start.15) | collective-permute-done | bytes 262176 | tf_op jit(solution)/shard_map/ppermute | solution.py:37
  68.2 3.0 %shard_map.121 = (f32[2,2,2,4,16,256]{5,4,3,2,1,0:T(8,128)S(1)}, f32[2,2,2,4,16,256]{5,4,3,2,1,0:T(8,128)S(1)}) custom-call(s32[40]{0:T(128)S(1)} %pad_add_fusion.info, f32[256,256]{1,0:T(8,128)S(1)} %fusion.8.l0, f32[256,256]{1,0:T(8,128)S(1)} %collective-permute-done.13.l1, f32[256,256]{1,0:T(8,128)S(1)} %collective-permute-done.14.l2, ...), custom_call_target="tpu_custom_call" | custom-call | flops 536870912 | bytes 3145728 | tf_op jit(solution)/shard_map/pallas_call | solution.py:219
  71.1 3.9 %collective-permute-start.16 = (f32[2,2,2,4,16,256]{5,4,3,2,1,0:T(8,128)S(1)}, f32[2,2,2,4,16,256]{5,4,3,2,1,0:T(8,128)S(1)}, u32[]{:S(2)}, u32[]{:S(2)}) collective-permute-start(f32[2,2,2,4,16,256]{5,4,3,2,1,0:T(8,128)S(1)} %get-tuple-element.24), channel_id=1, source_target_pairs={{0,4},{4,0},{1,5},{5,1},{2,6},{6,2},{3,7},{7,3},{8,12},{12,8},{9,1... | collective-permute-start | bytes 1572872 | tf_op jit(solution)/shard_map/ppermute | solution.py:334
  75.1 1.5 %collective-permute-done.16 = f32[2,2,2,4,16,256]{5,4,3,2,1,0:T(8,128)S(1)} collective-permute-done((f32[2,2,2,4,16,256]{5,4,3,2,1,0:T(8,128)S(1)}, f32[2,2,2,4,16,256]{5,4,3,2,1,0:T(8,128)S(1)}, u32[]{:S(2)}, u32[]{:S(2)}) %collective-permute-start.16) | collective-permute-done | bytes 524320 | tf_op jit(solution)/shard_map/ppermute | solution.py:334
  76.6 5.7 %collective-permute-start.17 = (f32[2,2,4,16,256]{4,3,2,1,0:T(8,128)S(1)}, f32[2,2,4,16,256]{4,3,2,1,0:T(8,128)S(1)}, u32[]{:S(2)}, u32[]{:S(2)}) collective-permute-start(f32[2,2,4,16,256]{4,3,2,1,0:T(8,128)S(1)} %fusion.5), channel_id=1, source_target_pairs={{0,8},{4,60},{8,0},{12,20},{16,24},{20,12},{24,16},{28,36},{32,40}... | collective-permute-start | bytes 786440 | tf_op jit(solution)/shard_map/ppermute | solution.py:37
  83.4 2.6 %collective-permute-done.17 = f32[2,2,4,16,256]{4,3,2,1,0:T(8,128)S(1)} collective-permute-done((f32[2,2,4,16,256]{4,3,2,1,0:T(8,128)S(1)}, f32[2,2,4,16,256]{4,3,2,1,0:T(8,128)S(1)}, u32[]{:S(2)}, u32[]{:S(2)}) %collective-permute-start.17) | collective-permute-done | bytes 262176 | tf_op jit(solution)/shard_map/ppermute | solution.py:37
  86.1 2.6 %collective-permute-start.18 = (f32[2,4,16,256]{3,2,1,0:T(8,128)S(1)}, f32[2,4,16,256]{3,2,1,0:T(8,128)S(1)}, u32[]{:S(2)}, u32[]{:S(2)}) collective-permute-start(f32[2,4,16,256]{3,2,1,0:T(8,128)S(1)} %fusion.18), channel_id=1, source_target_pairs={{0,64},{4,196},{64,0},{68,132},{128,192},{132,68},{192,128},{196,4... | collective-permute-start | bytes 393224 | tf_op jit(solution)/shard_map/ppermute | solution.py:37
  88.8 2.4 %collective-permute-done.18 = f32[2,4,16,256]{3,2,1,0:T(8,128)S(1)} collective-permute-done((f32[2,4,16,256]{3,2,1,0:T(8,128)S(1)}, f32[2,4,16,256]{3,2,1,0:T(8,128)S(1)}, u32[]{:S(2)}, u32[]{:S(2)}) %collective-permute-start.18) | collective-permute-done | bytes 131104 | tf_op jit(solution)/shard_map/ppermute | solution.py:37
  92.2 1.7 %fusion.15 = (f32[4,56,256]{2,1,0:T(8,128)S(1)}, f32[4,56,256]{2,1,0:T(8,128)S(1)}) fusion(f32[2,4,56,256]{3,2,1,0:T(8,128)} %collective-permute-done.12, f32[2,2,4,56,256]{4,3,2,1,0:T(8,128)} %copy-done.5, f32[2,2,2,4,56,256]{5,4,3,2,1,0:T(8,128)} %copy-done.3, f32[2,2,2,4,56,256]{5,4,3,2,1,0:T(8,128)} %copy-done.2), kind=kLoop, calls=%fused_computation.32 | loop fusion | flops 344064 | bytes 2293760 | tf_op jit(solution)/shard_map/add | solution.py:363
  93.9 1.3 collective-permute-start.19
  95.5 4.1 %collective-permute-done.19 = f32[4,72,256]{2,1,0:T(8,128)S(1)} collective-permute-done((f32[4,72,256]{2,1,0:T(8,128)S(1)}, f32[4,72,256]{2,1,0:T(8,128)S(1)}, u32[]{:S(2)}, u32[]{:S(2)}) %collective-permute-start.19) | collective-permute-done | bytes 294944 | tf_op jit(solution)/shard_map/ppermute | solution.py:37
  101.1 2.6 %collective-permute-done.20 = f32[2,72,256]{2,1,0:T(8,128)S(1)} collective-permute-done((f32[2,72,256]{2,1,0:T(8,128)S(1)}, f32[2,72,256]{2,1,0:T(8,128)S(1)}, u32[]{:S(2)}, u32[]{:S(2)}) %collective-permute-start.20) | collective-permute-done | bytes 147488 | tf_op jit(solution)/shard_map/ppermute | solution.py:37
  103.8 2.2 %collective-permute-start.21 = (f32[72,256]{1,0:T(8,128)S(1)}, f32[72,256]{1,0:T(8,128)S(1)}, u32[]{:S(2)}, u32[]{:S(2)}) collective-permute-start(f32[72,256]{1,0:T(8,128)S(1)} %get-tuple-element.54), channel_id=1, source_target_pairs={{0,24},{4,44},{8,48},{12,36},{16,40},{20,60},{24,0},{28,52},{32,56... | collective-permute-start | bytes 221192 | tf_op jit(solution)/shard_map/ppermute | solution.py:37
  106.2 4.0 %collective-permute-done.21.came = f32[72,256]{1,0:T(8,128)S(1)} collective-permute-done((f32[72,256]{1,0:T(8,128)S(1)}, f32[72,256]{1,0:T(8,128)S(1)}, u32[]{:S(2)}, u32[]{:S(2)}) %collective-permute-start.21) | collective-permute-done | bytes 73760 | tf_op jit(solution)/shard_map/ppermute | solution.py:37
  110.3 28.9 %all_to_all.11 = f32[256,1,4]{2,1,0:T(1,128)S(1)} all-to-all(f32[256,1,4]{2,1,0:T(1,128)S(1)} %bitcast.116), channel_id=1, replica_groups=mesh['dp_0'=4,'dp_1'=8,'dp_2'=2,'mp'=4] {'dp_0','dp_1','dp_2','mp'}, dimensions={0} | all-to-all | bytes 8192 | tf_op jit(solution)/shard_map/all_to_all | solution.py:384
  (77 shorter events, 14.5 us)
Async XLA Ops:
  0.6 6.3 %copy-start = (bf16[3584,256]{1,0:T(8,128)(2,1)S(1)}, bf16[3584,256]{1,0:T(8,128)(2,1)}, u32[]{:S(2)}) copy-start(bf16[3584,256]{1,0:T(8,128)(2,1)} %param.15) | copy-start | bytes 5505028
  3.3 10.3 %collective-permute-start = (f32[2,256,256]{2,1,0:T(8,128)S(1)}, f32[2,256,256]{2,1,0:T(8,128)}, u32[]{:S(2)}, u32[]{:S(2)}) collective-permute-start(f32[2,256,256]{2,1,0:T(8,128)S(1)} %pad_maximum_fusion), channel_id=1, source_target_pairs={{0,1},{4,7},{1,0},{5,6},{2,3},{6,5},{3,2},{7,4},{8,9},{12,15},{9,8... | collective-permute-start | bytes 1572872 | tf_op jit(solution)/shard_map/ppermute | solution.py:37
  12.1 1.2 copy-start.4
  12.1 15.6 %copy-start.8 = (s32[2,1,2]{2,1,0:T(1,128)S(1)}, s32[2,1,2]{2,1,0:T(1,128)}, u32[]{:S(2)}) copy-start(s32[2,1,2]{2,1,0:T(1,128)} %param.13) | copy-start | bytes 52
  13.3 11.5 %collective-permute-start.5 = (f32[2,256,256]{2,1,0:T(8,128)}, f32[2,256,256]{2,1,0:T(8,128)}, u32[]{:S(2)}, u32[]{:S(2)}) collective-permute-start(f32[2,256,256]{2,1,0:T(8,128)} %pad_maximum_fusion.1), channel_id=1, source_target_pairs={{0,1},{4,7},{1,0},{5,6},{2,3},{6,5},{3,2},{7,4},{8,9},{12,15},{9,8... | collective-permute-start | bytes 1572872 | tf_op jit(solution)/shard_map/ppermute | solution.py:37
  14.6 27.6 %copy-start.6 = (f32[2,1,2,256]{3,2,1,0:T(2,128)S(1)}, f32[2,1,2,256]{3,2,1,0:T(2,128)}, u32[]{:S(2)}) copy-start(f32[2,1,2,256]{3,2,1,0:T(2,128)} %param.11) | copy-start | bytes 12292
  14.6 27.6 %copy-start.7 = (s32[2,1,2,256]{3,2,1,0:T(2,128)S(1)}, s32[2,1,2,256]{3,2,1,0:T(2,128)}, u32[]{:S(2)}) copy-start(s32[2,1,2,256]{3,2,1,0:T(2,128)} %param.12) | copy-start | bytes 12292
  14.6 13.9 %collective-permute-start.1 = (f32[256,256]{1,0:T(8,128)S(1)}, f32[256,256]{1,0:T(8,128)}, u32[]{:S(2)}, u32[]{:S(2)}) collective-permute-start(f32[256,256]{1,0:T(8,128)S(1)} %fusion.9), channel_id=1, source_target_pairs={{0,3},{4,5},{1,2},{5,4},{2,1},{6,7},{3,0},{7,6},{8,11},{12,13},{9,... | collective-permute-start | bytes 786440 | tf_op jit(solution)/shard_map/ppermute | solution.py:37
  26.5 5.7 %collective-permute-start.6 = (f32[256,256]{1,0:T(8,128)}, f32[256,256]{1,0:T(8,128)S(1)}, u32[]{:S(2)}, u32[]{:S(2)}) collective-permute-start(f32[256,256]{1,0:T(8,128)} %fusion.6), channel_id=1, source_target_pairs={{0,3},{4,5},{1,2},{5,4},{2,1},{6,7},{3,0},{7,6},{8,11},{12,13},{9,... | collective-permute-start | bytes 786440 | tf_op jit(solution)/shard_map/ppermute | solution.py:37
  29.6 15.3 %collective-permute-start.3 = (f32[256,256]{1,0:T(8,128)S(1)}, f32[256,256]{1,0:T(8,128)S(1)}, u32[]{:S(2)}, u32[]{:S(2)}) collective-permute-start(f32[256,256]{1,0:T(8,128)S(1)} %fusion.11.r0), channel_id=1, source_target_pairs={{0,1},{4,7},{1,0},{5,6},{2,3},{6,5},{3,2},{7,4},{8,9},{12,15},{9,8... | collective-permute-start | bytes 786440 | tf_op jit(solution)/shard_map/ppermute | solution.py:37
  29.7 5.9 %collective-permute-start.2 = (f32[256,256]{1,0:T(8,128)S(1)}, f32[256,256]{1,0:T(8,128)S(1)}, u32[]{:S(2)}, u32[]{:S(2)}) collective-permute-start(f32[256,256]{1,0:T(8,128)S(1)} %fusion.11.r0), channel_id=1, source_target_pairs={{0,3},{4,5},{1,2},{5,4},{2,1},{6,7},{3,0},{7,6},{8,11},{12,13},{9,... | collective-permute-start | bytes 786440 | tf_op jit(solution)/shard_map/ppermute | solution.py:37
  35.5 9.3 %collective-permute-start.4 = (f32[256,256]{1,0:T(8,128)S(1)}, f32[256,256]{1,0:T(8,128)S(1)}, u32[]{:S(2)}, u32[]{:S(2)}) collective-permute-start(f32[256,256]{1,0:T(8,128)S(1)} %collective-permute-done.2.r1), channel_id=1, source_target_pairs={{0,1},{4,7},{1,0},{5,6},{2,3},{6,5},{3,2},{7,4},{8,9},{12,15},{9,8... | collective-permute-start | bytes 786440 | tf_op jit(solution)/shard_map/ppermute | solution.py:37
  39.4 3.9 %collective-permute-start.9 = (f32[1,256]{1,0:T(1,128)S(1)}, f32[1,256]{1,0:T(1,128)S(1)}, u32[]{:S(2)}, u32[]{:S(2)}) collective-permute-start(f32[1,256]{1,0:T(1,128)S(1)} %bitcast.117), channel_id=1, source_target_pairs={{0,2},{1,3},{2,0},{3,1},{4,6},{5,7},{6,4},{7,5},{8,10},{9,11},{10,... | collective-permute-start | bytes 3080 | tf_op jit(solution)/shard_map/ppermute | solution.py:300
  40.0 3.6 %collective-permute-start.8 = (f32[1,256]{1,0:T(1,128)S(1)}, f32[1,256]{1,0:T(1,128)S(1)}, u32[]{:S(2)}, u32[]{:S(2)}) collective-permute-start(f32[1,256]{1,0:T(1,128)S(1)} %bitcast.118), channel_id=1, source_target_pairs={{0,1},{4,7},{1,0},{5,6},{2,3},{6,5},{3,2},{7,4},{8,9},{12,15},{9,8... | collective-permute-start | bytes 3080 | tf_op jit(solution)/shard_map/ppermute | solution.py:37
  42.1 2.7 %collective-permute-start.7 = (f32[1,256]{1,0:T(1,128)S(1)}, f32[1,256]{1,0:T(1,128)S(1)}, u32[]{:S(2)}, u32[]{:S(2)}) collective-permute-start(f32[1,256]{1,0:T(1,128)S(1)} %bitcast.119), channel_id=1, source_target_pairs={{0,3},{4,5},{1,2},{5,4},{2,1},{6,7},{3,0},{7,6},{8,11},{12,13},{9,... | collective-permute-start | bytes 3080 | tf_op jit(solution)/shard_map/ppermute | solution.py:37
  51.2 31.1 %copy-start.2 = (f32[2,2,2,4,56,256]{5,4,3,2,1,0:T(8,128)}, f32[2,2,2,4,56,256]{5,4,3,2,1,0:T(8,128)S(1)}, u32[]{:S(2)}) copy-start(f32[2,2,2,4,56,256]{5,4,3,2,1,0:T(8,128)S(1)} %get-tuple-element.20) | copy-start | bytes 5505028
  51.2 16.9 %copy-start.1 = (bf16[2,1,2,256,1024]{4,3,2,1,0:T(8,128)(2,1)S(1)}, bf16[2,1,2,256,1024]{4,3,2,1,0:T(8,128)(2,1)}, u32[]{:S(2)}) copy-start(bf16[2,1,2,256,1024]{4,3,2,1,0:T(8,128)(2,1)} %param.10) | copy-start | bytes 6291460
  51.2 10.6 %collective-permute-start.10 = (f32[2,2,2,4,56,256]{5,4,3,2,1,0:T(8,128)S(1)}, f32[2,2,2,4,56,256]{5,4,3,2,1,0:T(8,128)S(1)}, u32[]{:S(2)}, u32[]{:S(2)}) collective-permute-start(f32[2,2,2,4,56,256]{5,4,3,2,1,0:T(8,128)S(1)} %get-tuple-element.21), channel_id=1, source_target_pairs={{0,4},{4,0},{1,5},{5,1},{2,6},{6,2},{3,7},{7,3},{8,12},{12,8},{9,1... | collective-permute-start | bytes 5505032 | tf_op jit(solution)/shard_map/ppermute | solution.py:334
  55.2 6.5 %collective-permute-start.13 = (f32[256,256]{1,0:T(8,128)S(1)}, f32[256,256]{1,0:T(8,128)S(1)}, u32[]{:S(2)}, u32[]{:S(2)}) collective-permute-start(f32[256,256]{1,0:T(8,128)S(1)} %fusion.8.l0), channel_id=1, source_target_pairs={{0,3},{4,5},{1,2},{5,4},{2,1},{6,7},{3,0},{7,6},{8,11},{12,13},{9,... | collective-permute-start | bytes 786440 | tf_op jit(solution)/shard_map/ppermute | solution.py:37
  55.7 9.5 %collective-permute-start.14 = (f32[256,256]{1,0:T(8,128)S(1)}, f32[256,256]{1,0:T(8,128)S(1)}, u32[]{:S(2)}, u32[]{:S(2)}) collective-permute-start(f32[256,256]{1,0:T(8,128)S(1)} %fusion.8.l0), channel_id=1, source_target_pairs={{0,1},{4,7},{1,0},{5,6},{2,3},{6,5},{3,2},{7,4},{8,9},{12,15},{9,8... | collective-permute-start | bytes 786440 | tf_op jit(solution)/shard_map/ppermute | solution.py:37
  61.7 6.4 %collective-permute-start.15 = (f32[256,256]{1,0:T(8,128)S(1)}, f32[256,256]{1,0:T(8,128)S(1)}, u32[]{:S(2)}, u32[]{:S(2)}) collective-permute-start(f32[256,256]{1,0:T(8,128)S(1)} %collective-permute-done.13.l1), channel_id=1, source_target_pairs={{0,1},{4,7},{1,0},{5,6},{2,3},{6,5},{3,2},{7,4},{8,9},{12,15},{9,8... | collective-permute-start | bytes 786440 | tf_op jit(solution)/shard_map/ppermute | solution.py:37
  61.9 20.5 %copy-start.3 = (f32[2,2,2,4,56,256]{5,4,3,2,1,0:T(8,128)}, f32[2,2,2,4,56,256]{5,4,3,2,1,0:T(8,128)S(1)}, u32[]{:S(2)}) copy-start(f32[2,2,2,4,56,256]{5,4,3,2,1,0:T(8,128)S(1)} %collective-permute-done.10) | copy-start | bytes 5505028
  62.0 20.3 %collective-permute-start.11 = (f32[2,2,4,56,256]{4,3,2,1,0:T(8,128)S(1)}, f32[2,2,4,56,256]{4,3,2,1,0:T(8,128)S(1)}, u32[]{:S(2)}, u32[]{:S(2)}) collective-permute-start(f32[2,2,4,56,256]{4,3,2,1,0:T(8,128)S(1)} %fusion), channel_id=1, source_target_pairs={{0,64},{4,196},{64,0},{68,132},{128,192},{132,68},{192,128},{196,4... | collective-permute-start | bytes 2752520 | tf_op jit(solution)/shard_map/ppermute | solution.py:37
  71.1 17.5 %copy-start.9 = (s32[2,64]{1,0:T(2,128)S(1)}, s32[2,64]{1,0:T(2,128)}, u32[]{:S(2)}) copy-start(s32[2,64]{1,0:T(2,128)} %param.14) | copy-start | bytes 1540
  71.1 5.5 %collective-permute-start.16 = (f32[2,2,2,4,16,256]{5,4,3,2,1,0:T(8,128)S(1)}, f32[2,2,2,4,16,256]{5,4,3,2,1,0:T(8,128)S(1)}, u32[]{:S(2)}, u32[]{:S(2)}) collective-permute-start(f32[2,2,2,4,16,256]{5,4,3,2,1,0:T(8,128)S(1)} %get-tuple-element.24), channel_id=1, source_target_pairs={{0,4},{4,0},{1,5},{5,1},{2,6},{6,2},{3,7},{7,3},{8,12},{12,8},{9,1... | collective-permute-start | bytes 1572872 | tf_op jit(solution)/shard_map/ppermute | solution.py:334
  76.6 9.4 %collective-permute-start.17 = (f32[2,2,4,16,256]{4,3,2,1,0:T(8,128)S(1)}, f32[2,2,4,16,256]{4,3,2,1,0:T(8,128)S(1)}, u32[]{:S(2)}, u32[]{:S(2)}) collective-permute-start(f32[2,2,4,16,256]{4,3,2,1,0:T(8,128)S(1)} %fusion.5), channel_id=1, source_target_pairs={{0,8},{4,60},{8,0},{12,20},{16,24},{20,12},{24,16},{28,36},{32,40}... | collective-permute-start | bytes 786440 | tf_op jit(solution)/shard_map/ppermute | solution.py:37
  82.3 1.1 copy-start.5
  83.4 8.9 %collective-permute-start.12 = (f32[2,4,56,256]{3,2,1,0:T(8,128)}, f32[2,4,56,256]{3,2,1,0:T(8,128)}, u32[]{:S(2)}, u32[]{:S(2)}) collective-permute-start(f32[2,4,56,256]{3,2,1,0:T(8,128)} %fusion.3), channel_id=1, source_target_pairs={{0,8},{4,60},{8,0},{12,20},{16,24},{20,12},{24,16},{28,36},{32,40}... | collective-permute-start | bytes 1376264 | tf_op jit(solution)/shard_map/ppermute | solution.py:37
  86.1 5.1 %collective-permute-start.18 = (f32[2,4,16,256]{3,2,1,0:T(8,128)S(1)}, f32[2,4,16,256]{3,2,1,0:T(8,128)S(1)}, u32[]{:S(2)}, u32[]{:S(2)}) collective-permute-start(f32[2,4,16,256]{3,2,1,0:T(8,128)S(1)} %fusion.18), channel_id=1, source_target_pairs={{0,64},{4,196},{64,0},{68,132},{128,192},{132,68},{192,128},{196,4... | collective-permute-start | bytes 393224 | tf_op jit(solution)/shard_map/ppermute | solution.py:37
  93.9 5.7 %collective-permute-start.19 = (f32[4,72,256]{2,1,0:T(8,128)S(1)}, f32[4,72,256]{2,1,0:T(8,128)S(1)}, u32[]{:S(2)}, u32[]{:S(2)}) collective-permute-start(f32[4,72,256]{2,1,0:T(8,128)S(1)} %pad_maximum_fusion.2), channel_id=1, source_target_pairs={{0,192},{4,68},{64,128},{68,4},{128,64},{132,196},{192,0},{196,132... | collective-permute-start | bytes 884744 | tf_op jit(solution)/shard_map/ppermute | solution.py:37
  99.7 4.1 %collective-permute-start.20 = (f32[2,72,256]{2,1,0:T(8,128)S(1)}, f32[2,72,256]{2,1,0:T(8,128)S(1)}, u32[]{:S(2)}, u32[]{:S(2)}) collective-permute-start(f32[2,72,256]{2,1,0:T(8,128)S(1)} %slice.213), channel_id=1, source_target_pairs={{0,56},{4,12},{8,16},{12,4},{16,8},{20,28},{24,32},{28,20},{32,24}... | collective-permute-start | bytes 442376 | tf_op jit(solution)/shard_map/ppermute | solution.py:37
  103.8 6.4 %collective-permute-start.21 = (f32[72,256]{1,0:T(8,128)S(1)}, f32[72,256]{1,0:T(8,128)S(1)}, u32[]{:S(2)}, u32[]{:S(2)}) collective-permute-start(f32[72,256]{1,0:T(8,128)S(1)} %get-tuple-element.54), channel_id=1, source_target_pairs={{0,24},{4,44},{8,48},{12,36},{16,40},{20,60},{24,0},{28,52},{32,56... | collective-permute-start | bytes 221192 | tf_op jit(solution)/shard_map/ppermute | solution.py:37
